TPU v7x, 32 devices: a whole 2x2x4 slice. The times are simulated.
32 devices in a mesh: dp: 8 (over z, x), tensor: 4 (over y, core).
Axes of the slice: x: 2, y: 2, z: 4, core: 2. Of those that a mesh axis runs over, the one named last changes fastest.
Arguments:
- patches: bfloat16 [16, 4, 512, 1024], P(None, 'tensor', 'dp'), may hold values from -6 to 6
- lengths: int32 [16], replicated, may hold values from 1024 to 2048, as said below
- deal: int32 [16], replicated, may hold values from 0 to 15, as said below
- attn_gain: float32 [1024], replicated, may hold values from 0.25 to 1.75
- w_query: bfloat16 [1024, 1024], P(None, 'tensor'), may hold values from -0.1875 to 0.1875
- w_key: bfloat16 [1024, 1024], P(None, 'tensor'), may hold values from -0.1875 to 0.1875
- w_value: bfloat16 [1024, 1024], P(None, 'tensor'), may hold values from -0.1875 to 0.1875
- w_out: bfloat16 [1024, 1024], P('tensor'), may hold values from -1.5 to 1.5
- ffn_gain: float32 [1024], replicated, may hold values from 0.25 to 1.75
- w_gate: bfloat16 [1024, 2816], P(None, 'tensor'), may hold values from -0.1875 to 0.1875
- w_up: bfloat16 [1024, 2816], P(None, 'tensor'), may hold values from -0.1875 to 0.1875
- w_down: bfloat16 [2816, 1024], P('tensor'), may hold values from -0.109375 to 0.109375
- cotangent: bfloat16 [16, 4, 512, 1024], P('dp', 'tensor'), may hold values from -6 to 6
Outputs:
- output: bfloat16 [16, 4, 512, 1024], P('dp', 'tensor')
- grad_patches: bfloat16 [16, 4, 512, 1024], P(None, 'tensor', 'dp')
- grad_attn_gain: float32 [1024], replicated
- grad_w_query: float32 [1024, 1024], P('dp', 'tensor')
- grad_w_key: float32 [1024, 1024], P('dp', 'tensor')
- grad_w_value: float32 [1024, 1024], P('dp', 'tensor')
- grad_w_out: float32 [1024, 1024], P('tensor', 'dp')
- grad_ffn_gain: float32 [1024], replicated
- grad_w_gate: float32 [1024, 2816], P('dp', 'tensor')
- grad_w_up: float32 [1024, 2816], P('dp', 'tensor')
- grad_w_down: float32 [2816, 1024], P('tensor', 'dp')
Inputs may be any that keep to these rules, and one draw needn't show every extreme that they name: `lengths`: length of sequence s; positions from it on are padding, and one sequence has length 2048, one 1024. A permutation: sequence s goes to slot deal[s], which lies in data group deal[s] // 2.
All inputs are finite; a program needn't handle non-finite values.
Results may differ from a plain program's by a relative error of at most 0.02.
Values may be sent and summed in bfloat16 or wider, within the bound.
A program may use at most 256 MiB of HBM per device.

v0:
```python
import jax
import jax.numpy as jnp
from jax import lax
from jax.sharding import PartitionSpec as P

HEAD_DIM = 64
QBLK = 512


EPSILON = 1e-05
NEGATIVE = -1e30


def project(value_tensor, weight_matrix):
    return jnp.einsum(
        "nai,iy->nay", value_tensor, weight_matrix, preferred_element_type=jnp.float32
    )


def project_back(value_tensor, weight_matrix):
    return jnp.einsum(
        "nqc,yc->nqy", value_tensor, weight_matrix, preferred_element_type=jnp.float32
    )


def outer_sum(left_operand, right_operand):
    return jnp.einsum(
        "fhm,fho->mo", left_operand, right_operand, preferred_element_type=jnp.float32
    )


def norm_rows(value_tensor, gain_vector):
    factor = lax.rsqrt(jnp.mean(value_tensor * value_tensor, -1, keepdims=True) + EPSILON)
    return (value_tensor * factor * gain_vector, factor)


def norm_back(value_tensor, factor, gain_vector, upstream):
    scaled = upstream * gain_vector
    inward = factor * scaled - value_tensor * factor**3 * jnp.mean(
        value_tensor * scaled, -1, keepdims=True
    )
    return (inward, jnp.sum(upstream * value_tensor * factor, (0, 1)))


def block_scores(query_block, key_rows, query_start, key_start, block_rows, scale_factor):
    key_block = lax.dynamic_slice_in_dim(key_rows, key_start, block_rows, 0)
    raw_scores = (
        jnp.einsum("qhd,khd->hqk", query_block, key_block, preferred_element_type=jnp.float32)
        * scale_factor
    )
    query_pos = query_start + jnp.arange(block_rows)
    key_pos = key_start + jnp.arange(block_rows)
    return jnp.where(query_pos[:, None] >= key_pos[None, :], raw_scores, NEGATIVE)


def attend_one(members):
    queries, key_rows, value_rows, length = members
    total_rows, head_count, head_size = queries.shape
    block_rows = QBLK
    scale_factor = head_size ** (-0.5)
    live_blocks = (length + block_rows - 1) // block_rows

    def attend_query_step(block_number, loop_state):
        out_all, total_all = loop_state
        query_start = block_number * block_rows
        query_block = lax.dynamic_slice_in_dim(queries, query_start, block_rows, 0)

        def find_total(key_index, running):
            highest, summed = running
            scores = block_scores(
                query_block, key_rows, query_start, key_index * block_rows, block_rows, scale_factor
            )
            new_high = jnp.maximum(highest, jnp.max(scores, -1))
            summed = summed * jnp.exp(highest - new_high) + jnp.sum(
                jnp.exp(scores - new_high[..., None]), -1
            )
            return (new_high, summed)

        start_state = (
            jnp.full((head_count, block_rows), NEGATIVE, jnp.float32),
            jnp.zeros((head_count, block_rows), jnp.float32),
        )
        highest, summed = lax.fori_loop(0, block_number + 1, find_total, start_state)
        log_total = highest + jnp.log(summed)

        def add_values(key_index, accumulated):
            key_start = key_index * block_rows
            scores = block_scores(
                query_block, key_rows, query_start, key_start, block_rows, scale_factor
            )
            probabilities = jnp.exp(scores - log_total[..., None]).astype(jnp.bfloat16)
            value_block = lax.dynamic_slice_in_dim(value_rows, key_start, block_rows, 0)
            return accumulated + jnp.einsum(
                "hqk,khd->qhd", probabilities, value_block, preferred_element_type=jnp.float32
            )

        accumulated = lax.fori_loop(
            0,
            block_number + 1,
            add_values,
            jnp.zeros((block_rows, head_count, head_size), jnp.float32),
        )
        out_all = lax.dynamic_update_slice_in_dim(
            out_all, accumulated.astype(jnp.bfloat16), query_start, 0
        )
        total_all = lax.dynamic_update_slice_in_dim(total_all, log_total, query_start, 1)
        return (out_all, total_all)

    start_all = (
        jnp.zeros((total_rows, head_count, head_size), jnp.bfloat16),
        jnp.zeros((head_count, total_rows), jnp.float32),
    )
    return lax.fori_loop(0, live_blocks, attend_query_step, start_all)


def attention_backward(members):
    queries, key_rows, value_rows, grad_out, log_total, length = members
    total_rows, head_count, head_size = queries.shape
    block_rows = QBLK
    scale_factor = head_size ** (-0.5)
    live_blocks = (length + block_rows - 1) // block_rows

    def attention_query_step(block_number, loop_state):
        grad_queries, grad_keys, grad_values = loop_state
        query_start = block_number * block_rows
        query_block = lax.dynamic_slice_in_dim(queries, query_start, block_rows, 0)
        grad_block = lax.dynamic_slice_in_dim(grad_out, query_start, block_rows, 0)
        total_block = lax.dynamic_slice_in_dim(log_total, query_start, block_rows, 1)

        def probs_at(key_start):
            scores = block_scores(
                query_block, key_rows, query_start, key_start, block_rows, scale_factor
            )
            probabilities = jnp.exp(scores - total_block[..., None])
            value_block = lax.dynamic_slice_in_dim(value_rows, key_start, block_rows, 0)
            grad_probs = jnp.einsum(
                "qhd,khd->hqk", grad_block, value_block, preferred_element_type=jnp.float32
            )
            return (probabilities, grad_probs)

        def row_step(key_index, row_dot):
            probabilities, grad_probs = probs_at(key_index * block_rows)
            return row_dot + jnp.sum(probabilities * grad_probs, -1)

        row_dot = lax.fori_loop(
            0, block_number + 1, row_step, jnp.zeros((head_count, block_rows), jnp.float32)
        )

        def grad_step(key_index, inner_state):
            query_acc, keys_acc, values_acc = inner_state
            key_start = key_index * block_rows
            probabilities, grad_probs = probs_at(key_start)
            grad_scores = (probabilities * (grad_probs - row_dot[..., None])).astype(jnp.bfloat16)
            key_block = lax.dynamic_slice_in_dim(key_rows, key_start, block_rows, 0)
            query_acc = query_acc + jnp.einsum(
                "hqk,khd->qhd", grad_scores, key_block, preferred_element_type=jnp.float32
            )
            key_part = jnp.einsum(
                "hqk,qhd->khd", grad_scores, query_block, preferred_element_type=jnp.float32
            )
            value_part = jnp.einsum(
                "hqk,qhd->khd",
                probabilities.astype(jnp.bfloat16),
                grad_block,
                preferred_element_type=jnp.float32,
            )
            keys_acc = lax.dynamic_update_slice_in_dim(
                keys_acc,
                lax.dynamic_slice_in_dim(keys_acc, key_start, block_rows, 0) + key_part,
                key_start,
                0,
            )
            values_acc = lax.dynamic_update_slice_in_dim(
                values_acc,
                lax.dynamic_slice_in_dim(values_acc, key_start, block_rows, 0) + value_part,
                key_start,
                0,
            )
            return (query_acc, keys_acc, values_acc)

        start_inner = (
            jnp.zeros((block_rows, head_count, head_size), jnp.float32),
            grad_keys,
            grad_values,
        )
        query_acc, grad_keys, grad_values = lax.fori_loop(
            0, block_number + 1, grad_step, start_inner
        )
        grad_queries = lax.dynamic_update_slice_in_dim(
            grad_queries, query_acc * scale_factor, query_start, 0
        )
        return (grad_queries, grad_keys, grad_values)

    zero_rows = jnp.zeros((total_rows, head_count, head_size), jnp.float32)
    grad_queries, grad_keys, grad_values = lax.fori_loop(
        0, live_blocks, attention_query_step, (zero_rows, zero_rows, zero_rows)
    )
    return (grad_queries, grad_keys * scale_factor, grad_values)


def local(
    patches,
    lengths,
    deal,
    attn_gain,
    w_query,
    w_key,
    w_value,
    w_out,
    ffn_gain,
    w_gate,
    w_up,
    w_down,
    cotangent,
):
    seq_count = cotangent.shape[0]
    quarter_rows = cotangent.shape[2]
    group_index = lax.axis_index("dp")
    row_portion = lax.axis_index("tensor")
    slot_owner = jnp.argsort(deal)
    outgoing = patches[slot_owner]
    arrived = lax.all_to_all(outgoing, "dp", split_axis=0, concat_axis=2, tiled=True)
    own_lengths = lax.dynamic_slice_in_dim(
        lengths[slot_owner], group_index * seq_count, seq_count, 0
    )
    inputs = arrived[:, 0].astype(jnp.float32)
    positions = row_portion * quarter_rows + jnp.arange(quarter_rows)
    live_rows = (positions[None, :] < own_lengths[:, None]).astype(jnp.float32)[..., None]
    normed_attn, factor_attn = norm_rows(inputs, attn_gain)
    gathered_attn = lax.all_gather(normed_attn.astype(jnp.bfloat16), "tensor", axis=1, tiled=True)
    total_rows = gathered_attn.shape[1]
    head_count = w_query.shape[1] // HEAD_DIM

    def split_heads(value_tensor):
        return value_tensor.reshape(seq_count, total_rows, head_count, HEAD_DIM)

    def merge_heads(value_tensor):
        return value_tensor.reshape(seq_count, total_rows, head_count * HEAD_DIM).astype(
            jnp.bfloat16
        )

    queries = split_heads(project(gathered_attn, w_query).astype(jnp.bfloat16))
    key_rows = split_heads(project(gathered_attn, w_key).astype(jnp.bfloat16))
    value_rows = split_heads(project(gathered_attn, w_value).astype(jnp.bfloat16))
    mixed_heads, log_total = lax.map(attend_one, (queries, key_rows, value_rows, own_lengths))
    mixed_rows = merge_heads(mixed_heads)
    attention = lax.psum_scatter(
        project(mixed_rows, w_out).astype(jnp.bfloat16), "tensor", scatter_dimension=1, tiled=True
    ).astype(jnp.float32)
    hidden = inputs + attention
    normed_ffn, factor_ffn = norm_rows(hidden, ffn_gain)
    gathered_ffn = lax.all_gather(normed_ffn.astype(jnp.bfloat16), "tensor", axis=1, tiled=True)
    gate_pre = project(gathered_ffn, w_gate)
    up_proj = project(gathered_ffn, w_up)
    sigmoid = 1.0 / (1.0 + jnp.exp(-gate_pre))
    swish_gate = gate_pre / (1.0 + jnp.exp(-gate_pre))
    product = (swish_gate * up_proj).astype(jnp.bfloat16)
    feedforward = lax.psum_scatter(
        project(product, w_down).astype(jnp.bfloat16), "tensor", scatter_dimension=1, tiled=True
    ).astype(jnp.float32)
    output = (live_rows * (hidden + feedforward)).astype(jnp.bfloat16)[:, None]
    grad_result = cotangent[:, 0].astype(jnp.float32) * live_rows
    grad_ffn = lax.all_gather(grad_result.astype(jnp.bfloat16), "tensor", axis=1, tiled=True)
    grad_product = project_back(grad_ffn, w_down)
    grad_w_down = outer_sum(product, grad_ffn)
    grad_gate = (grad_product * up_proj * sigmoid * (1.0 + gate_pre * (1.0 - sigmoid))).astype(
        jnp.bfloat16
    )
    grad_up = (grad_product * swish_gate).astype(jnp.bfloat16)
    grad_w_gate = outer_sum(gathered_ffn, grad_gate)
    grad_w_up = outer_sum(gathered_ffn, grad_up)
    grad_normed_ffn = lax.psum_scatter(
        (project_back(grad_gate, w_gate) + project_back(grad_up, w_up)).astype(jnp.bfloat16),
        "tensor",
        scatter_dimension=1,
        tiled=True,
    ).astype(jnp.float32)
    grad_hidden, gain_ffn_part = norm_back(hidden, factor_ffn, ffn_gain, grad_normed_ffn)
    grad_hidden = grad_hidden + grad_result
    grad_attn = lax.all_gather(grad_hidden.astype(jnp.bfloat16), "tensor", axis=1, tiled=True)
    grad_mixed = project_back(grad_attn, w_out).astype(jnp.bfloat16)
    grad_w_out = outer_sum(mixed_rows, grad_attn)
    grad_queries, grad_keys, grad_values = lax.map(
        attention_backward,
        (queries, key_rows, value_rows, split_heads(grad_mixed), log_total, own_lengths),
    )
    grad_queries = merge_heads(grad_queries)
    grad_keys = merge_heads(grad_keys)
    grad_values = merge_heads(grad_values)
    grad_w_query = outer_sum(gathered_attn, grad_queries)
    grad_w_key = outer_sum(gathered_attn, grad_keys)
    grad_w_value = outer_sum(gathered_attn, grad_values)
    grad_terms = (
        project_back(grad_queries, w_query)
        + project_back(grad_keys, w_key)
        + project_back(grad_values, w_value)
    )
    grad_normed_attn = lax.psum_scatter(
        grad_terms.astype(jnp.bfloat16), "tensor", scatter_dimension=1, tiled=True
    ).astype(jnp.float32)
    grad_inputs, gain_attn_part = norm_back(inputs, factor_attn, attn_gain, grad_normed_attn)
    grad_inputs = grad_inputs + grad_hidden
    returned_value = lax.all_to_all(
        grad_inputs.astype(jnp.bfloat16)[:, None], "dp", split_axis=2, concat_axis=0, tiled=True
    )
    grad_patches = returned_value[deal]
    shards = (
        lax.psum_scatter(grad_w_query, "dp", scatter_dimension=0, tiled=True),
        lax.psum_scatter(grad_w_key, "dp", scatter_dimension=0, tiled=True),
        lax.psum_scatter(grad_w_value, "dp", scatter_dimension=0, tiled=True),
        lax.psum_scatter(grad_w_out, "dp", scatter_dimension=1, tiled=True),
        lax.psum_scatter(grad_w_gate, "dp", scatter_dimension=0, tiled=True),
        lax.psum_scatter(grad_w_up, "dp", scatter_dimension=0, tiled=True),
        lax.psum_scatter(grad_w_down, "dp", scatter_dimension=1, tiled=True),
    )
    gain_grads = lax.psum((gain_attn_part, gain_ffn_part), ("dp", "tensor"))
    return (
        output,
        grad_patches,
        gain_grads[0],
        shards[0],
        shards[1],
        shards[2],
        shards[3],
        gain_grads[1],
        shards[4],
        shards[5],
        shards[6],
    )


def solution(mesh):
    in_specs = (
        P(None, "tensor", "dp", None),
        P(),
        P(),
        P(),
        P(None, "tensor"),
        P(None, "tensor"),
        P(None, "tensor"),
        P("tensor", None),
        P(),
        P(None, "tensor"),
        P(None, "tensor"),
        P("tensor", None),
        P("dp", "tensor", None, None),
    )
    out_specs = (
        P("dp", "tensor", None, None),
        P(None, "tensor", "dp", None),
        P(),
        P("dp", "tensor"),
        P("dp", "tensor"),
        P("dp", "tensor"),
        P("tensor", "dp"),
        P(),
        P("dp", "tensor"),
        P("dp", "tensor"),
        P("tensor", "dp"),
    )
    return jax.shard_map(local, mesh=mesh, in_specs=in_specs, out_specs=out_specs, check_vma=False)
```

profile of v0, /device:TPU:0, one launch (start us, length us, event | category | flops | bytes accessed | tf_op | source)
XLA Modules:
  0.0 1623.8 jit_solution(9510223708256496808)
XLA Ops:
  11.3 55.5 %all_to_all.27 = bf16[16,1,64,1024]{3,2,1,0:T(8,128)(2,1)S(1)} all-to-all(bf16[16,1,64,1024]{3,2,1,0:T(8,128)(2,1)} %bitcast.318), channel_id=1, replica_groups=mesh['dp'=8,'tensor'=4] {'dp'}, dimensions={0} | all-to-all | bytes 4194304 | tf_op jit(solution)/shard_map/all_to_all | solution.py:222
  72.6 56.6 %all-gather.5.cloned.1.call-done = bf16[2,2048,1024]{2,1,0:T(8,128)(2,1)} async-done(((bf16[2,512,1024]{2,1,0:T(8,128)(2,1)}), bf16[2,2048,1024]{2,1,0:T(8,128)(2,1)}) %all-gather.5.cloned.1.call-update) | async-done | bytes 8388624 | tf_op jit(solution)/shard_map/all_gather | solution.py:230
  129.2 7.2 convolution_convert_fusion.3
  144.4 104.9 %while.176 = (s32[]{:T(128)}, bf16[2,2048,4,64]{1,3,2,0:T(8,128)(2,1)}, f32[2,4,2048]{2,1,0:T(4,128)S(1)}, s32[2]{0:T(128)S(1)}, bf16[2,2048,4,64]{1,3,2,0:T(8,1...) while((s32[]{:T(128)}, ...), condition=%wide.region_11.12_spmd, body=%wide.region_2.11_spmd.sunk | while | flops 414982176 | bytes 23611796 | solution.py:245
  151.3 54.0 %while.179 = (s32[]{:T(128)}, bf16[2048,4,64]{0,2,1:T(8,128)(2,1)}, f32[4,2048]{1,0:T(4,128)S(1)}, s32[]{:T(128)}, bf16[2048,4,64]{0,2,1:T(8,128)(2,1)S(1)}, /*i...) while((s32[]{:T(128)}, bf16[2048,4,64]{0,2,1:T(8,128)(2,1)}, ...), condition=%wide.region_10.10_spmd, body=%wide.region_3.9_spmd.sunk | while | flops 414982144 | bytes 14075677 | solution.py:113
  161.6 5.8 while.184
  168.2 6.4 while.183
  174.7 8.8 while.184
  184.3 8.5 while.183
  192.9 11.7 while.184
  214.0 32.9 %while.179 = (s32[]{:T(128)}, bf16[2048,4,64]{0,2,1:T(8,128)(2,1)}, f32[4,2048]{1,0:T(4,128)S(1)}, s32[]{:T(128)}, bf16[2048,4,64]{0,2,1:T(8,128)(2,1)S(1)}, /*i...) while((s32[]{:T(128)}, bf16[2048,4,64]{0,2,1:T(8,128)(2,1)}, ...), condition=%wide.region_10.10_spmd, body=%wide.region_3.9_spmd.sunk | while | flops 414982144 | bytes 14075677 | solution.py:113
  224.4 5.8 while.184
  231.0 6.4 while.183
  237.5 8.8 while.184
  249.3 7.4 convolution_convert_fusion.1
  256.7 71.5 %reduce-scatter.12.cloned.1.call-done = bf16[2,512,1024]{2,1,0:T(8,128)(2,1)} async-done(((bf16[2,2048,1024]{2,1,0:T(8,128)(2,1)}), bf16[2,512,1024]{2,1,0:T(8,128)(2,1)}) %reduce-scatter.12.cloned.1.call-update) | async-done | bytes 2097168 | tf_op jit(solution)/shard_map/reduce_scatter | solution.py:247
  338.6 54.9 %all-gather.7.cloned.1.call-done = bf16[2,2048,1024]{2,1,0:T(8,128)(2,1)} async-done(((bf16[2,512,1024]{2,1,0:T(8,128)(2,1)}), bf16[2,2048,1024]{2,1,0:T(8,128)(2,1)}) %all-gather.7.cloned.1.call-update) | async-done | bytes 8388624 | tf_op jit(solution)/shard_map/all_gather | solution.py:252
  393.5 13.3 fusion.76
  406.8 8.9 fusion.80
  415.7 38.0 %all-gather.9.cloned.1.call-done = bf16[2,2048,1024]{2,1,0:T(8,128)(2,1)} async-done(((bf16[2,512,1024]{2,1,0:T(8,128)(2,1)}), bf16[2,2048,1024]{2,1,0:T(8,128)(2,1)}) %all-gather.9.cloned.1.call-update) | async-done | bytes 8388624 | tf_op jit(solution)/shard_map/all_gather | solution.py:263
  453.7 19.7 %multiply_convert_fusion = (bf16[2,2048,704]{1,2,0:T(8,128)(2,1)}, bf16[2,2048,704]{1,2,0:T(8,128)(2,1)}, bf16[2,2048,704]{1,2,0:T(8,128)(2,1)}) fusion(f32[2,2048,704]{1,2,0:T(8,128)} %fusion.80, f32[2,2048,704]{1,2,0:T(8,128)} %fusion.76, bf16[2,2048,1024]{2,1,0:T(8,128)(2,1)} %all-gather.9.cloned.1.call-done, bf16[704,1024]{1,0:T(8,128)(2,1)} %param.40), kind=kOutput, calls=%fused_computation.92 | convolution fusion | flops 5948833792 | bytes 50200576 | tf_op jit(solution)/shard_map/nqc,yc->nqy/dot_general | solution.py:21
  473.5 13.6 fusion.78
  487.0 12.4 add_convert_fusion.1
  499.5 71.5 %reduce-scatter.16.cloned.1.call-done = bf16[2,512,1024]{2,1,0:T(8,128)(2,1)} async-done(((bf16[2,2048,1024]{2,1,0:T(8,128)(2,1)}), bf16[2,512,1024]{2,1,0:T(8,128)(2,1)}) %reduce-scatter.16.cloned.1.call-update) | async-done | bytes 2097168 | tf_op jit(solution)/shard_map/reduce_scatter | solution.py:272
  571.0 5.4 fusion.66
  579.4 58.3 %all-gather.11.cloned.1.call-done = bf16[2,2048,1024]{2,1,0:T(8,128)(2,1)} async-done(((bf16[2,512,1024]{2,1,0:T(8,128)(2,1)}), bf16[2,2048,1024]{2,1,0:T(8,128)(2,1)}) %all-gather.11.cloned.1.call-update) | async-done | bytes 8388624 | tf_op jit(solution)/shard_map/all_gather | solution.py:280
  637.7 7.1 convolution_convert_fusion.2
  644.8 258.4 %while.178 = (s32[]{:T(128)}, bf16[2,2048,4,64]{1,3,2,0:T(8,128)(2,1)}, bf16[2,2048,4,64]{1,3,2,0:T(8,128)(2,1)}, bf16[2,2048,4,64]{1,3,2,0:T(8,128)(2,1)}, s32[...) while((s32[]{:T(128)}, ...), condition=%wide.region_25.26_spmd, body=%wide.region_17.25_spmd.sunk | while | flops 957351936 | bytes 99788672 | solution.py:283
  655.8 140.4 %while.180 = (s32[]{:T(128)}, bf16[2048,4,64]{0,2,1:T(8,128)(2,1)}, f32[2048,4,64]{0,2,1:T(8,128)}, f32[2048,4,64]{0,2,1:T(8,128)}, s32[]{:T(128)}, /*index=5*/b...) while((s32[]{:T(128)}, bf16[2048,4,64]{0,2,1:T(8,128)(2,1)}, ...), condition=%wide.region_24.24_spmd, body=%wide.region_18.23_spmd.sunk | while | flops 956303360 | bytes 37331872 | solution.py:195
  660.4 9.8 while.182
  672.0 7.0 while.181
  679.0 19.6 %while.182 = (s32[]{:T(128)}, f32[512,4,64]{0,2,1:T(8,128)S(1)}, f32[2048,4,64]{0,2,1:T(8,128)}, f32[2048,4,64]{0,2,1:T(8,128)}, s32[]{:T(128)}, /*index=5*/bf16...) while((s32[]{:T(128)}, f32[512,4,64]{0,2,1:T(8,128)S(1)}, ...), condition=%wide.region_23.22_spmd, body=%wide.region_22.21_spmd.sunk | while | flops 682230784 | bytes 24674528 | solution.py:186
  700.4 10.5 while.181
  711.0 29.4 %while.182 = (s32[]{:T(128)}, f32[512,4,64]{0,2,1:T(8,128)S(1)}, f32[2048,4,64]{0,2,1:T(8,128)}, f32[2048,4,64]{0,2,1:T(8,128)}, s32[]{:T(128)}, /*index=5*/bf16...) while((s32[]{:T(128)}, f32[512,4,64]{0,2,1:T(8,128)S(1)}, ...), condition=%wide.region_23.22_spmd, body=%wide.region_22.21_spmd.sunk | while | flops 682230784 | bytes 24674528 | solution.py:186
  742.1 14.0 while.181
  756.2 39.2 %while.182 = (s32[]{:T(128)}, f32[512,4,64]{0,2,1:T(8,128)S(1)}, f32[2048,4,64]{0,2,1:T(8,128)}, f32[2048,4,64]{0,2,1:T(8,128)}, s32[]{:T(128)}, /*index=5*/bf16...) while((s32[]{:T(128)}, f32[512,4,64]{0,2,1:T(8,128)S(1)}, ...), condition=%wide.region_23.22_spmd, body=%wide.region_22.21_spmd.sunk | while | flops 682230784 | bytes 24674528 | solution.py:186
  812.3 85.3 %while.180 = (s32[]{:T(128)}, bf16[2048,4,64]{0,2,1:T(8,128)(2,1)}, f32[2048,4,64]{0,2,1:T(8,128)}, f32[2048,4,64]{0,2,1:T(8,128)}, s32[]{:T(128)}, /*index=5*/b...) while((s32[]{:T(128)}, bf16[2048,4,64]{0,2,1:T(8,128)(2,1)}, ...), condition=%wide.region_24.24_spmd, body=%wide.region_18.23_spmd.sunk | while | flops 956303360 | bytes 37331872 | solution.py:195
  816.8 9.8 while.182
  828.4 7.0 while.181
  835.5 19.6 %while.182 = (s32[]{:T(128)}, f32[512,4,64]{0,2,1:T(8,128)S(1)}, f32[2048,4,64]{0,2,1:T(8,128)}, f32[2048,4,64]{0,2,1:T(8,128)}, s32[]{:T(128)}, /*index=5*/bf16...) while((s32[]{:T(128)}, f32[512,4,64]{0,2,1:T(8,128)S(1)}, ...), condition=%wide.region_23.22_spmd, body=%wide.region_22.21_spmd.sunk | while | flops 682230784 | bytes 24674528 | solution.py:186
  856.9 10.5 while.181
  867.4 29.4 %while.182 = (s32[]{:T(128)}, f32[512,4,64]{0,2,1:T(8,128)S(1)}, f32[2048,4,64]{0,2,1:T(8,128)}, f32[2048,4,64]{0,2,1:T(8,128)}, s32[]{:T(128)}, /*index=5*/bf16...) while((s32[]{:T(128)}, f32[512,4,64]{0,2,1:T(8,128)S(1)}, ...), condition=%wide.region_23.22_spmd, body=%wide.region_22.21_spmd.sunk | while | flops 682230784 | bytes 24674528 | solution.py:186
  903.3 10.0 fusion.86
  913.3 8.2 fusion.89
  921.5 15.6 add_convert_fusion
  938.4 12.3 convolution_convert_fusion
  950.8 11.7 convolution_bitcast_fusion.4
  962.6 11.6 convolution_bitcast_fusion.3
  974.2 11.8 convolution_bitcast_fusion.2
  986.1 6.8 convolution_bitcast_fusion.5
  993.0 7.5 convolution_bitcast_fusion.8
  1000.8 6.9 convolution_bitcast_fusion.7
  1008.6 4.4 fusion.68
  1013.0 69.6 %reduce-scatter.14.cloned.1.call-done = bf16[2,512,1024]{2,1,0:T(8,128)(2,1)} async-done(((bf16[2,2048,1024]{2,1,0:T(8,128)(2,1)}), bf16[2,512,1024]{2,1,0:T(8,128)(2,1)}) %reduce-scatter.14.cloned.1.call-update) | async-done | bytes 2097168 | tf_op jit(solution)/shard_map/reduce_scatter | solution.py:258
  1082.6 7.5 fusion.71
  1093.6 5.5 all-to-all-start.1
  1099.2 7.4 convolution_bitcast_fusion.6
  1106.7 79.3 %all-reduce = (f32[1024]{0:T(1024)}, f32[1024]{0:T(1024)}) all-reduce(f32[1024]{0:T(1024)S(1)} %get-tuple-element.786, f32[1024]{0:T(1024)S(1)} %copy-done.41), channel_id=1, replica_groups=mesh['dp'=8,'tensor'=4] {'dp','tensor'}, use_global_device_ids=true, to_apply=%region_29.30 | all-reduce | flops 2048 | bytes 16384 | tf_op jit(solution)/shard_map/psum | solution.py:316
  1195.6 76.0 %reduce-scatter.28.cloned.1.call-done = f32[128,704]{0,1:T(8,128)} async-done(((f32[1024,704]{0,1:T(8,128)}), f32[128,704]{0,1:T(8,128)}) %reduce-scatter.28.cloned.1.call-update) | async-done | bytes 360464 | tf_op jit(solution)/shard_map/reduce_scatter | solution.py:312
  1271.6 76.2 %reduce-scatter.30.cloned.1.call-done = f32[128,704]{0,1:T(8,128)} async-done(((f32[1024,704]{0,1:T(8,128)}), f32[128,704]{0,1:T(8,128)}) %reduce-scatter.30.cloned.1.call-update) | async-done | bytes 360464 | tf_op jit(solution)/shard_map/reduce_scatter | solution.py:313
  1347.8 67.8 %reduce-scatter.26.cloned.1.call-done = f32[256,128]{1,0:T(8,128)} async-done(((f32[256,1024]{1,0:T(8,128)}), f32[256,128]{1,0:T(8,128)}) %reduce-scatter.26.cloned.1.call-update) | async-done | bytes 131088 | tf_op jit(solution)/shard_map/reduce_scatter | solution.py:311
  1415.6 67.2 %reduce-scatter.20.cloned.1.call-done = f32[128,256]{1,0:T(8,128)} async-done(((f32[1024,256]{1,0:T(8,128)}), f32[128,256]{1,0:T(8,128)}) %reduce-scatter.20.cloned.1.call-update) | async-done | bytes 131088 | tf_op jit(solution)/shard_map/reduce_scatter | solution.py:308
  1482.8 67.0 %reduce-scatter.22.cloned.1.call-done = f32[128,256]{1,0:T(8,128)} async-done(((f32[1024,256]{1,0:T(8,128)}), f32[128,256]{1,0:T(8,128)}) %reduce-scatter.22.cloned.1.call-update) | async-done | bytes 131088 | tf_op jit(solution)/shard_map/reduce_scatter | solution.py:309
  1549.8 67.0 %reduce-scatter.24.cloned.1.call-done = f32[128,256]{1,0:T(8,128)} async-done(((f32[1024,256]{1,0:T(8,128)}), f32[128,256]{1,0:T(8,128)}) %reduce-scatter.24.cloned.1.call-update) | async-done | bytes 131088 | tf_op jit(solution)/shard_map/reduce_scatter | solution.py:310
  (662 shorter events, 428.5 us)
Async XLA Ops:
  7.2 122.0 %all-gather.5.cloned.1.call-start = ((), (), s32[]{:S(2)}) async-start(), calls=%async_computation.13 | async-start | bytes 10485760 | tf_op jit(solution)/shard_map/all_gather | solution.py:230
  67.4 4.3 copy-start.29
  70.0 59.2 %copy-start.19 = (bf16[1024,256]{1,0:T(8,128)(2,1)S(1)}, bf16[1024,256]{1,0:T(8,128)(2,1)}, u32[]{:S(2)}) copy-start(bf16[1024,256]{1,0:T(8,128)(2,1)} %param.35) | copy-start | bytes 1572868
  71.8 256.5 %reduce-scatter.12.cloned.1.call-start = ((), (), s32[]{:S(2)}) async-start(), calls=%async_computation.14 | async-start | bytes 10485760 | tf_op jit(solution)/shard_map/reduce_scatter | solution.py:247
  72.6 63.9 %copy-start.21 = (bf16[1024,256]{1,0:T(8,128)(2,1)S(1)}, bf16[1024,256]{1,0:T(8,128)(2,1)}, u32[]{:S(2)}) copy-start(bf16[1024,256]{1,0:T(8,128)(2,1)} %param.34) | copy-start | bytes 1572868
  129.2 7.2 copy-start.44
  136.5 4.0 copy-start.22
  256.7 75.2 %copy-start.31 = (f32[1024]{0:T(1024)S(1)}, f32[1024]{0:T(1024)}, u32[]{:S(2)}) copy-start(f32[1024]{0:T(1024)} %param.37) | copy-start | bytes 12292
  256.7 136.8 %all-gather.7.cloned.1.call-start = ((), (), s32[]{:S(2)}) async-start(), calls=%async_computation.15 | async-start | bytes 10485760 | tf_op jit(solution)/shard_map/all_gather | solution.py:252
  328.2 4.1 copy-start.4
  328.2 4.7 copy-start.8
  331.9 244.5 %copy-start.27 = (f32[2,512]{1,0:T(2,128)}, f32[2,512]{1,0:T(2,128)S(1)}, u32[]{:S(2)}) copy-start(f32[2,512]{1,0:T(2,128)S(1)} %get-tuple-element.954) | copy-start | bytes 12292
  331.9 244.5 %copy-start.37 = (f32[2,512]{1,0:T(2,128)}, f32[2,512]{1,0:T(2,128)S(1)}, u32[]{:S(2)}) copy-start(f32[2,512]{1,0:T(2,128)S(1)} %get-tuple-element.953) | copy-start | bytes 12292
  335.0 118.7 %all-gather.9.cloned.1.call-start = ((), (), s32[]{:S(2)}) async-start(), calls=%async_computation.17 | async-start | bytes 10485760 | tf_op jit(solution)/shard_map/all_gather | solution.py:263
  335.2 241.2 %copy-start.33 = (f32[2,512]{1,0:T(2,128)}, f32[2,512]{1,0:T(2,128)S(1)}, u32[]{:S(2)}) copy-start(f32[2,512]{1,0:T(2,128)S(1)} %compare_convert_fusion) | copy-start | bytes 12292
  338.5 232.5 %reduce-scatter.16.cloned.1.call-start = ((), (), s32[]{:S(2)}) async-start(), calls=%async_computation.18 | async-start | bytes 10485760 | tf_op jit(solution)/shard_map/reduce_scatter | solution.py:272
  393.5 13.3 copy-start.45
  393.5 13.3 copy-start.46
  473.5 13.6 copy-start.47
  473.5 13.6 copy-start.50
  499.5 138.3 %all-gather.11.cloned.1.call-start = ((), (), s32[]{:S(2)}) async-start(), calls=%async_computation.19 | async-start | bytes 10485760 | tf_op jit(solution)/shard_map/all_gather | solution.py:280
  571.0 5.4 copy-start.5
  571.0 5.4 copy-start.10
  571.0 5.4 copy-start.11
  576.4 61.3 %copy-start.24 = (bf16[256,1024]{1,0:T(8,128)(2,1)S(1)}, bf16[256,1024]{1,0:T(8,128)(2,1)}, u32[]{:S(2)}) copy-start(bf16[256,1024]{1,0:T(8,128)(2,1)} %param.36) | copy-start | bytes 1572868
  579.3 429.3 %reduce-scatter.18.cloned.1.call-start = ((), (), s32[]{:S(2)}) async-start(), calls=%async_computation.20 | async-start | bytes 10485760 | tf_op jit(solution)/shard_map/reduce_scatter | solution.py:298
  645.2 6.3 copy-start.25
  646.5 4.0 copy-start.7
  796.2 4.1 copy-start.6
  796.2 4.1 copy-start.15
  796.2 5.5 copy-start.26
  796.2 5.5 copy-start.43
  801.7 6.3 copy-start.25
  803.0 4.0 copy-start.7
  897.6 4.1 copy-start.6
  897.6 4.1 copy-start.15
  897.6 5.5 copy-start.26
  897.6 5.5 copy-start.43
  903.2 10.0 copy-start.17
  903.3 10.0 copy-start.23
  913.3 8.2 copy-start.13
  913.3 8.2 copy-start.20
  937.0 145.6 %reduce-scatter.14.cloned.1.call-start = ((), (), s32[]{:S(2)}) async-start(), calls=%async_computation.16 | async-start | bytes 10485760 | tf_op jit(solution)/shard_map/reduce_scatter | solution.py:258
  950.7 244.9 %reduce-scatter.32.cloned.1.call-start = ((), (), s32[]{:S(2)}) async-start(), calls=%async_computation.27 | async-start | bytes 3244032 | tf_op jit(solution)/shard_map/reduce_scatter | solution.py:314
  962.5 309.1 %reduce-scatter.28.cloned.1.call-start = ((), (), s32[]{:S(2)}) async-start(), calls=%async_computation.25 | async-start | bytes 3244032 | tf_op jit(solution)/shard_map/reduce_scatter | solution.py:312
  974.1 11.9 copy-start.18
  974.2 373.6 %reduce-scatter.30.cloned.1.call-start = ((), (), s32[]{:S(2)}) async-start(), calls=%async_computation.26 | async-start | bytes 3244032 | tf_op jit(solution)/shard_map/reduce_scatter | solution.py:313
  986.0 429.6 %reduce-scatter.26.cloned.1.call-start = ((), (), s32[]{:S(2)}) async-start(), calls=%async_computation.24 | async-start | bytes 1179648 | tf_op jit(solution)/shard_map/reduce_scatter | solution.py:311
  992.9 7.9 copy-start.30
  992.9 7.9 copy-start.14
  992.9 489.9 %reduce-scatter.20.cloned.1.call-start = ((), (), s32[]{:S(2)}) async-start(), calls=%async_computation.21 | async-start | bytes 1179648 | tf_op jit(solution)/shard_map/reduce_scatter | solution.py:308
  1000.5 549.3 %reduce-scatter.22.cloned.1.call-start = ((), (), s32[]{:S(2)}) async-start(), calls=%async_computation.22 | async-start | bytes 1179648 | tf_op jit(solution)/shard_map/reduce_scatter | solution.py:309
  1000.8 7.8 copy-start.36
  1007.7 74.9 %copy-start.9 = (bf16[2,512,1024]{2,1,0:T(8,128)(2,1)S(1)}, bf16[2,512,1024]{2,1,0:T(8,128)(2,1)}, u32[]{:S(2)}) copy-start(bf16[2,512,1024]{2,1,0:T(8,128)(2,1)} %reduce-scatter.12.cloned.1.call-done) | copy-start | bytes 6291460
  1007.7 74.9 %copy-start.28 = (f32[2,512]{1,0:T(2,128)S(1)}, f32[2,512]{1,0:T(2,128)}, u32[]{:S(2)}) copy-start(f32[2,512]{1,0:T(2,128)} %copy-done.27) | copy-start | bytes 12292
  1007.7 74.9 %copy-start.32 = (f32[1024]{0:T(1024)S(1)}, f32[1024]{0:T(1024)}, u32[]{:S(2)}) copy-start(f32[1024]{0:T(1024)} %param.37) | copy-start | bytes 12292
  1007.7 74.9 %copy-start.34 = (f32[2,512]{1,0:T(2,128)S(1)}, f32[2,512]{1,0:T(2,128)}, u32[]{:S(2)}) copy-start(f32[2,512]{1,0:T(2,128)} %copy-done.33) | copy-start | bytes 12292
  1007.7 74.9 %copy-start.38 = (f32[2,512]{1,0:T(2,128)S(1)}, f32[2,512]{1,0:T(2,128)}, u32[]{:S(2)}) copy-start(f32[2,512]{1,0:T(2,128)} %copy-done.37) | copy-start | bytes 12292
  1007.7 74.9 %copy-start.40 = (f32[2,512]{1,0:T(2,128)S(1)}, f32[2,512]{1,0:T(2,128)}, u32[]{:S(2)}) copy-start(f32[2,512]{1,0:T(2,128)} %copy-done.39) | copy-start | bytes 12292
  1093.6 92.3 %all-to-all-start.1 = ((bf16[2,1,512,1024]{3,0,1,2:T(2,128)(2,1)}), bf16[2,1,512,1024]{3,0,1,2:T(2,128)(2,1)S(1)}, u32[]{:S(2)}, u32[]{:S(2)}) async-start(bf16[2,1,512,1024]{3,0,1,2:T(2,128)(2,1)} %copy.132), calls=%async_computation.5 | async-start | bytes 4194304 | tf_op jit(solution)/shard_map/all_to_all | solution.py:303
  1099.1 7.5 copy-start.49
  1099.1 7.5 copy-start.41
  1099.1 517.7 %reduce-scatter.24.cloned.1.call-start = ((), (), s32[]{:S(2)}) async-start(), calls=%async_computation.23 | async-start | bytes 1179648 | tf_op jit(solution)/shard_map/reduce_scatter | solution.py:310
  1186.5 430.3 %copy-start.1 = (bf16[16,1,64,1024]{3,2,1,0:T(8,128)(2,1)S(1)}, bf16[16,1,64,1024]{3,2,1,0:T(8,128)(2,1)}, u32[]{:S(2)}) copy-start(bf16[16,1,64,1024]{3,2,1,0:T(8,128)(2,1)} %param.29) | copy-start | bytes 6291460
  (12 other events, 26.5 us)
Sparse Core Ops, SparseCore 0:
  71.9 57.2 all-gather.4
  256.8 71.3 reduce-scatter.11
  335.1 58.2 all-gather.6
  395.4 58.2 all-gather.8
  499.6 71.3 reduce-scatter.15
  579.4 58.2 all-gather.10
  937.2 71.3 reduce-scatter.17
  1011.2 71.3 reduce-scatter.13
  1086.7 108.8 reduce-scatter.31
  1199.6 71.9 reduce-scatter.27
  1275.7 72.0 reduce-scatter.29
  1351.6 63.9 reduce-scatter.25
  1419.6 63.1 reduce-scatter.19
  1486.6 63.1 reduce-scatter.21
  1553.6 63.1 reduce-scatter.23
where the time goes:
time: 1630 us; the launch traced here: 1620 us
  waiting for transfers between devices  847 us (52%)
  matrix products  468 us (29%)
  blocking collectives  135 us (8%)
  other arithmetic  83.5 us (5%)
  local copies, waits for them, and re-layouts  61.6 us (4%)
    dot_general x7, matrix products, project_back(): jnp.einsum('nqc,yc->nqy', value_tensor, weight_matrix, preferred_element_...  86.5 us
    dot_general x32, matrix products, probs_at(): jnp.einsum('qhd,khd->hqk', grad_block, value_block, preferred_element_typ...  79.5 us
    psum x1, blocking collectives, local(): gain_grads = lax.psum((gain_attn_part, gain_ffn_part), ('dp', 'tensor'))  79.3 us
    reduce_scatter x1, waiting for transfers between devices, local(): lax.psum_scatter(grad_w_up, 'dp', scatter_dimension=0, tiled=True)  76.2 us
    reduce_scatter x1, waiting for transfers between devices, local(): lax.psum_scatter(grad_w_gate, 'dp', scatter_dimension=0, tiled=True)  76 us
    reduce_scatter x1, waiting for transfers between devices, local(): lax.psum_scatter((project_back(grad_gate, w_gate) + project_back(grad_up,...  71.5 us
    reduce_scatter x1, waiting for transfers between devices, local(): lax.psum_scatter(project(mixed_rows, w_out).astype(jnp.bfloat16), 'tensor...  71.5 us
    reduce_scatter x1, waiting for transfers between devices, local(): lax.psum_scatter(project(product, w_down).astype(jnp.bfloat16), 'tensor',...  69.6 us
  transfers between devices with their start and end apart: 16, of which 15 were waited for; matrix products, arithmetic and copies ran while one was open for 8% of the time, Pallas kernels for 0%

commit v1 on v0

v1 whole, which is shorter than its diff:
```python
import functools

import jax
import jax.numpy as jnp
from jax import lax
from jax.experimental import pallas as pl
from jax.experimental.pallas import tpu as pltpu
from jax.sharding import PartitionSpec as P

HEAD_DIM = 64
PAIR = 2 * HEAD_DIM
EPSILON = 1e-05
NEGATIVE = -1e30
LOW = jnp.bfloat16
F32 = jnp.float32


def dot(left, right, left_dim, right_dim, dtype=F32):
    return lax.dot_general(
        left, right, (((left_dim,), (right_dim,)), ((), ())), preferred_element_type=dtype
    )


def norm_rows(rows, gain_vector):
    factor = lax.rsqrt(jnp.mean(rows * rows, -1, keepdims=True) + EPSILON)
    return ((rows * factor * gain_vector).astype(LOW), factor)


def norm_back(rows, factor, gain_vector, upstream):
    scaled = upstream * gain_vector
    inward = factor * scaled - rows * factor**3 * jnp.mean(rows * scaled, -1, keepdims=True)
    return (inward, jnp.sum(upstream * rows * factor, 0))


def head_masks(rows):
    lane = lax.broadcasted_iota(jnp.int32, (rows, PAIR), 1)
    return (lane < HEAD_DIM, lane >= HEAD_DIM)


def attend_kernel(info, q_ref, k_ref, v_ref, o_ref, total_ref):
    block = q_ref.shape[0]
    number = pl.program_id(1)
    masks = head_masks(block)

    @pl.when(number < info[0])
    def _():
        query = q_ref[...] * jnp.asarray(HEAD_DIM**-0.5, LOW)
        queries = [jnp.where(m, query, jnp.zeros_like(query)) for m in masks]
        above = lax.broadcasted_iota(jnp.int32, (block, block), 0) >= lax.broadcasted_iota(
            jnp.int32, (block, block), 1
        )

        def step(key_number, state, diagonal):
            start = pl.multiple_of(info[1 + key_number] * block, block)
            keys = k_ref[pl.ds(start, block), :]
            values = v_ref[pl.ds(start, block), :]
            result = []
            for head in range(2):
                high, acc = state[head]
                scores = dot(queries[head], keys, 1, 1)
                if diagonal:
                    scores = jnp.where(above, scores, NEGATIVE)
                new_high = jnp.maximum(high, jnp.max(scores, -1, keepdims=True))
                probs = jnp.exp(scores - new_high).astype(LOW)
                extended = jnp.where(masks[head], values, jnp.ones_like(values))
                acc = acc * jnp.exp(high - new_high) + dot(probs, extended, 1, 0)
                result.append((new_high, acc))
            return tuple(result)

        start_state = tuple(
            (jnp.full((block, 1), NEGATIVE, F32), jnp.zeros((block, PAIR), F32)) for _ in range(2)
        )
        state = step(number, start_state, True)
        state = lax.fori_loop(0, number, lambda n, s: step(n, s, False), state)
        (high0, acc0), (high1, acc1) = state
        sum0 = acc0[:, HEAD_DIM : HEAD_DIM + 1]
        sum1 = acc1[:, 0:1]
        o_ref[...] = jnp.where(masks[0], acc0 / sum0, acc1 / sum1).astype(LOW)
        total_ref[...] = jnp.where(masks[0], high0 + jnp.log(sum0), high1 + jnp.log(sum1))

    @pl.when(number >= info[0])
    def _():
        o_ref[...] = jnp.zeros_like(o_ref)
        total_ref[...] = jnp.zeros_like(total_ref)


def attend(info, qkv, block):
    rows, width = qkv.shape
    pairs = width // (3 * PAIR)
    here = pl.BlockSpec((block, PAIR), lambda h, i, info: (info[1 + i], h))
    return pl.pallas_call(
        attend_kernel,
        grid_spec=pltpu.PrefetchScalarGridSpec(
            num_scalar_prefetch=1,
            grid=(pairs, rows // block),
            in_specs=[
                here,
                pl.BlockSpec((rows, PAIR), lambda h, i, info: (0, pairs + h)),
                pl.BlockSpec((rows, PAIR), lambda h, i, info: (0, 2 * pairs + h)),
            ],
            out_specs=[here, here],
        ),
        out_shape=[
            jax.ShapeDtypeStruct((rows, pairs * PAIR), LOW),
            jax.ShapeDtypeStruct((rows, pairs * PAIR), F32),
        ],
        name="attend",
    )(info, qkv, qkv, qkv)


def attend_back_kernel(
    block, info, q_ref, k_ref, v_ref, do_ref, o_ref, total_ref, dq_ref, dk_ref, dv_ref, dq_acc, dk_acc, dv_acc
):
    masks = head_masks(block)
    dk_acc[...] = jnp.zeros_like(dk_acc)
    dv_acc[...] = jnp.zeros_like(dv_acc)
    dq_ref[...] = jnp.zeros_like(dq_ref)
    below = lax.broadcasted_iota(jnp.int32, (block, block), 0) <= lax.broadcasted_iota(
        jnp.int32, (block, block), 1
    )

    def split(value):
        return [jnp.where(m, value, jnp.zeros_like(value)) for m in masks]

    def query_step(number, carry):
        start = pl.multiple_of(info[1 + number] * block, block)
        here = pl.ds(start, block)
        queries = split(q_ref[here, :] * jnp.asarray(HEAD_DIM**-0.5, LOW))
        grad = do_ref[here, :]
        grads = split(grad)
        product = (grad.astype(F32) * o_ref[here, :].astype(F32)).T
        row_dots = [
            jnp.sum(product[h * HEAD_DIM : (h + 1) * HEAD_DIM], 0, keepdims=True) for h in range(2)
        ]
        turned = total_ref[here, :].T
        totals = [turned[h * HEAD_DIM : h * HEAD_DIM + 1] for h in range(2)]
        dq_acc[...] = jnp.zeros_like(dq_acc)

        def key_step(key_number, diagonal):
            there = pl.ds(pl.multiple_of(info[1 + key_number] * block, block), block)
            keys = k_ref[there, :]
            values = v_ref[there, :]
            split_keys = split(keys)
            dq = dq_acc[...]
            dk = dk_acc[there, :]
            dv = dv_acc[there, :]
            for head in range(2):
                scores = dot(keys, queries[head], 1, 1)
                if diagonal:
                    scores = jnp.where(below, scores, NEGATIVE)
                probs = jnp.exp(scores - totals[head])
                grad_probs = dot(values, grads[head], 1, 1)
                grad_scores = (probs * (grad_probs - row_dots[head])).astype(LOW)
                dv = dv + dot(probs.astype(LOW), grads[head], 1, 0)
                dk = dk + dot(grad_scores, queries[head], 1, 0)
                dq = dq + dot(grad_scores, split_keys[head], 0, 0)
            dq_acc[...] = dq
            dk_acc[there, :] = dk
            dv_acc[there, :] = dv

        key_step(number, True)

        def loop_step(key_number, inner):
            key_step(key_number, False)
            return inner

        lax.fori_loop(0, number, loop_step, 0)
        dq_ref[here, :] = (dq_acc[...] * HEAD_DIM**-0.5).astype(LOW)
        return carry

    lax.fori_loop(0, info[0], query_step, 0)
    dk_ref[...] = dk_acc[...].astype(LOW)
    dv_ref[...] = dv_acc[...].astype(LOW)


def attend_back(info, qkv, grad_out, mixed, totals, block):
    rows, width = qkv.shape
    pairs = width // (3 * PAIR)

    def column(offset):
        return pl.BlockSpec((rows, PAIR), lambda h, info: (0, offset + h))

    shape = jax.ShapeDtypeStruct((rows, pairs * PAIR), LOW)
    return pl.pallas_call(
        functools.partial(attend_back_kernel, block),
        grid_spec=pltpu.PrefetchScalarGridSpec(
            num_scalar_prefetch=1,
            grid=(pairs,),
            in_specs=[column(0), column(pairs), column(2 * pairs), column(0), column(0), column(0)],
            out_specs=[column(0)] * 3,
            scratch_shapes=[
                pltpu.VMEM((block, PAIR), F32),
                pltpu.VMEM((rows, PAIR), F32),
                pltpu.VMEM((rows, PAIR), F32),
            ],
        ),
        out_shape=[shape] * 3,
        name="attend_back",
    )(info, qkv, qkv, qkv, grad_out, mixed, totals)


def after(value, *others):
    return lax.optimization_barrier((value,) + others)[0]


def local(
    patches,
    lengths,
    deal,
    attn_gain,
    w_query,
    w_key,
    w_value,
    w_out,
    ffn_gain,
    w_gate,
    w_up,
    w_down,
    cotangent,
):
    groups = lax.axis_size("dp")
    seq_total = patches.shape[0]
    band = patches.shape[2]
    quarter = cotangent.shape[2]
    width = patches.shape[3]
    group = lax.axis_index("dp")
    place = lax.axis_index("tensor")
    chip = place // 2
    core = place % 2

    def swap_core(value):
        return lax.ppermute(value, "tensor", [(0, 1), (1, 0), (2, 3), (3, 2)])

    def swap_chip(value):
        return lax.ppermute(value, "tensor", [(0, 2), (2, 0), (1, 3), (3, 1)])

    slot_owner = jnp.argsort(deal)
    owners = slot_owner.reshape(groups, 2)
    mine = jnp.take(owners, chip, axis=1)
    theirs = jnp.take(owners, 1 - chip, axis=1)
    length = lengths[mine[group]]
    given = swap_chip(patches[theirs, 0])
    sent = jnp.stack((patches[mine, 0], given), 1)
    arrived = lax.all_to_all(sent, "dp", split_axis=0, concat_axis=0, tiled=True)
    inputs = arrived.transpose(1, 0, 2, 3).reshape(2 * quarter, width).astype(F32)

    w_qkv = jnp.concatenate((w_query, w_key, w_value), 1)
    w_qkv_far, w_out_far = swap_chip((after(w_qkv, given), after(w_out, given)))
    w_gate_far, w_up_far, w_down_far = swap_chip(
        tuple(after(w, w_qkv_far) for w in (w_gate, w_up, w_down))
    )
    cot_near = jnp.take(cotangent[:, 0], chip, axis=0)
    cot_far = swap_chip(after(jnp.take(cotangent[:, 0], 1 - chip, axis=0), w_qkv_far))

    numbers = jnp.arange(4)
    slots = 2 * (numbers % 2 != core) + (numbers // 2 != chip)
    live_blocks = (length + quarter - 1) // quarter
    info = jnp.concatenate((live_blocks[None], slots)).astype(jnp.int32)
    offsets = jnp.arange(quarter)
    positions = jnp.concatenate(
        ((2 * chip + core) * quarter + offsets, (2 * (1 - chip) + core) * quarter + offsets)
    )
    live_rows = (positions < length).astype(F32)[:, None]
    own_rows = 2 * quarter

    def gather(value):
        return jnp.concatenate((value, swap_core(value)), 0)

    def scatter(make):
        far = swap_core(make(slice(own_rows, None)).astype(LOW))
        return make(slice(0, own_rows)) + far.astype(F32)

    normed_attn, factor_attn = norm_rows(inputs, attn_gain)
    rows_attn = gather(normed_attn)
    qkv = [dot(rows_attn, w, 1, 0, LOW) for w in (w_qkv, w_qkv_far)]
    mixed_near, total_near = attend(info, qkv[0], quarter)
    mixed_far, total_far = attend(info, qkv[1], quarter)
    attention = scatter(
        lambda part: dot(mixed_near[part], w_out, 1, 0) + dot(mixed_far[part], w_out_far, 1, 0)
    )
    hidden = inputs + attention
    normed_ffn, factor_ffn = norm_rows(hidden, ffn_gain)
    rows_ffn = gather(normed_ffn)
    gates = jnp.concatenate((w_gate, w_gate_far), 1)
    ups = jnp.concatenate((w_up, w_up_far), 1)
    downs = jnp.concatenate((w_down, w_down_far), 0)
    gate_pre = dot(rows_ffn, gates, 1, 0)
    up_proj = dot(rows_ffn, ups, 1, 0)
    sigmoid = 1.0 / (1.0 + jnp.exp(-gate_pre))
    swish_gate = gate_pre * sigmoid
    product = (swish_gate * up_proj).astype(LOW)
    feedforward = scatter(lambda part: dot(product[part], downs, 1, 0))
    result = (live_rows * (hidden + feedforward)).astype(LOW)
    result_far = swap_chip(result[quarter:])
    output = jnp.where(
        chip == 0,
        jnp.stack((result[:quarter], result_far)),
        jnp.stack((result_far, result[:quarter])),
    )[:, None]

    grad_result = jnp.concatenate((cot_near, cot_far), 0).astype(F32) * live_rows
    grad_ffn = gather(grad_result.astype(LOW))
    grad_product = dot(grad_ffn, downs, 1, 1)
    grad_gate = (grad_product * up_proj * sigmoid * (1.0 + gate_pre * (1.0 - sigmoid))).astype(LOW)
    grad_up = (grad_product * swish_gate).astype(LOW)

    half = w_gate.shape[1]

    def over_chips(parts, ahead=()):
        far = swap_chip(jnp.concatenate([far.astype(LOW) for _, far in parts], 0))
        summed = jnp.concatenate([near for near, _ in parts], 0) + far.astype(F32)
        spread = summed.astype(LOW).reshape(-1, groups, width // groups).transpose(1, 0, 2)
        moved = lax.all_to_all(spread, "dp", split_axis=0, concat_axis=0, tiled=True)
        return jnp.sum(moved.astype(F32), 0)

    def halves(value):
        return (value[:half], value[half:])

    ffn_shards = over_chips(
        [
            halves(dot(product, grad_ffn, 0, 0)),
            halves(dot(grad_gate, rows_ffn, 0, 0)),
            halves(dot(grad_up, rows_ffn, 0, 0)),
        ]
    )
    grad_normed_ffn = scatter(
        lambda part: dot(grad_gate[part], gates, 1, 1) + dot(grad_up[part], ups, 1, 1)
    )
    grad_hidden, gain_ffn_part = norm_back(hidden, factor_ffn, ffn_gain, grad_normed_ffn)
    grad_hidden = grad_hidden + grad_result
    grad_attn = gather(grad_hidden.astype(LOW))
    out_shard = over_chips([(dot(mixed_near, grad_attn, 0, 0), dot(mixed_far, grad_attn, 0, 0))])
    grad_far = attend_back(
        info, qkv[1], dot(grad_attn, w_out_far, 1, 1, LOW), mixed_far, total_far, quarter
    )
    grad_near = attend_back(
        info, qkv[0], dot(grad_attn, w_out, 1, 1, LOW), mixed_near, total_near, quarter
    )
    grad_far = jnp.concatenate(grad_far, 1)
    grad_near = jnp.concatenate(grad_near, 1)
    grad_normed_attn = scatter(
        lambda part: dot(grad_near[part], w_qkv, 1, 1) + dot(grad_far[part], w_qkv_far, 1, 1)
    )
    qkv_shards = over_chips([(dot(grad_near, rows_attn, 0, 0), dot(grad_far, rows_attn, 0, 0))])
    grad_inputs, gain_attn_part = norm_back(inputs, factor_attn, attn_gain, grad_normed_attn)
    grad_inputs = (grad_inputs + grad_hidden).astype(LOW)
    returned = lax.all_to_all(
        grad_inputs.reshape(2, groups, band, width).transpose(1, 0, 2, 3),
        "dp",
        split_axis=0,
        concat_axis=0,
        tiled=True,
    )
    back_near = returned[:, 0]
    back_far = swap_chip(returned[:, 1])
    by_slot = jnp.where(
        chip == 0, jnp.stack((back_near, back_far), 1), jnp.stack((back_far, back_near), 1)
    ).reshape(seq_total, band, width)
    grad_patches = by_slot[deal][:, None]

    def total_of(value):
        value = value + swap_core(value)
        value = value + swap_chip(value)
        step = 1
        while step < groups:
            value = value + lax.ppermute(value, "dp", [(i, i ^ step) for i in range(groups)])
            step *= 2
        return value

    gain_grads = total_of(jnp.stack((gain_attn_part, gain_ffn_part)))
    part = w_query.shape[1]
    return (
        output,
        grad_patches,
        gain_grads[0],
        qkv_shards[:part].T,
        qkv_shards[part : 2 * part].T,
        qkv_shards[2 * part :].T,
        out_shard,
        gain_grads[1],
        ffn_shards[half : 2 * half].T,
        ffn_shards[2 * half :].T,
        ffn_shards[:half],
    )


def solution(mesh):
    in_specs = (
        P(None, "tensor", "dp", None),
        P(),
        P(),
        P(),
        P(None, "tensor"),
        P(None, "tensor"),
        P(None, "tensor"),
        P("tensor", None),
        P(),
        P(None, "tensor"),
        P(None, "tensor"),
        P("tensor", None),
        P("dp", "tensor", None, None),
    )
    out_specs = (
        P("dp", "tensor", None, None),
        P(None, "tensor", "dp", None),
        P(),
        P("dp", "tensor"),
        P("dp", "tensor"),
        P("dp", "tensor"),
        P("tensor", "dp"),
        P(),
        P("dp", "tensor"),
        P("dp", "tensor"),
        P("tensor", "dp"),
    )
    return jax.shard_map(local, mesh=mesh, in_specs=in_specs, out_specs=out_specs, check_vma=False)
```

time: 1630 us -> 736 us (0.45)
  waiting for transfers between devices: 847 us -> 230 us
  matrix products: 468 us -> 172 us
  Pallas kernels: 0 us -> 129 us
  blocking collectives: 135 us -> 53.3 us
  starting transfers between devices: 6.39 us -> 43.2 us
  other arithmetic: 83.5 us -> 50.3 us
  local copies, waits for them, and re-layouts: 61.6 us -> 43.9 us
    reduce_scatter x11 -> x0, waiting for transfers between devices: 639 us -> none  [the longest x1 76.2 us: local(): lax.psum_scatter(grad_w_up, 'dp', scatter_dimension=0, tiled=True)]
    dot_general x165 -> x28, matrix products: 468 us -> 172 us  [dot(): lax.dot_general(left, right, (((left_dim,), (right_dim,)), ((), ())), pre...]
    ppermute x0 -> x25, waiting for transfers between devices: none -> 211 us  [the longest x13 169 us: swap_chip(): return lax.ppermute(value, 'tensor', [(0, 2), (2, 0), (1, 3), (3, 1)])]
    all_gather x4 -> x0, waiting for transfers between devices: 208 us -> none  [the longest x1 58.3 us: local(): lax.all_gather(grad_hidden.astype(jnp.bfloat16), 'tensor', axis=1, tiled=...]
    pallas_call x0 -> x4, Pallas kernels: none -> 129 us  [the longest x2 72.2 us: attend_back(): pl.pallas_call(functools.partial(attend_back_kernel, block), grid_spec=pl...]
    psum x1 -> x0, blocking collectives: 79.3 us -> none  [local(): gain_grads = lax.psum((gain_attn_part, gain_ffn_part), ('dp', 'tensor'))]
    ppermute x0 -> x25, starting transfers between devices: none -> 23.4 us  [the longest x13 15.7 us: swap_chip(): return lax.ppermute(value, 'tensor', [(0, 2), (2, 0), (1, 3), (3, 1)])]
    all_to_all x1 -> x4, waiting for transfers between devices: 0.01 us -> 18.9 us  [the longest x3 18.9 us: over_chips(): lax.all_to_all(spread, 'dp', split_axis=0, concat_axis=0, tiled=True)]
  transfers between devices with their start and end apart: 16 -> 29, of which waited for: 15 -> 12; matrix products, arithmetic and copies ran while one was open for 8% -> 26% of each run, Pallas kernels for 0% -> 18%
where the time goes in v1:
time: 736 us; the launch traced here: 726 us
  waiting for transfers between devices  230 us (31%)
  matrix products  172 us (23%)
  Pallas kernels  129 us (18%)
  blocking collectives  53.3 us (7%)
  other arithmetic  50.3 us (7%)
  local copies, waits for them, and re-layouts  43.9 us (6%)
  starting transfers between devices  43.2 us (6%)
    dot_general x28, matrix products, dot(): lax.dot_general(left, right, (((left_dim,), (right_dim,)), ((), ())), pre...  172 us
    ppermute x13, waiting for transfers between devices, swap_chip(): return lax.ppermute(value, 'tensor', [(0, 2), (2, 0), (1, 3), (3, 1)])  169 us
    pallas_call x2, Pallas kernels, attend_back(): pl.pallas_call(functools.partial(attend_back_kernel, block), grid_spec=pl...  72.2 us
    pallas_call x2, Pallas kernels, attend(): pl.pallas_call(attend_kernel, grid_spec=pltpu.PrefetchScalarGridSpec(num_...  56.6 us
    all_to_all x1, blocking collectives, local(): lax.all_to_all(sent, 'dp', split_axis=0, concat_axis=0, tiled=True)  53.3 us
    ppermute x3, waiting for transfers between devices, total_of(): lax.ppermute(value, 'dp', [(i, i ^ step) for i in range(groups)])  37.8 us
    all_to_all x3, waiting for transfers between devices, over_chips(): lax.all_to_all(spread, 'dp', split_axis=0, concat_axis=0, tiled=True)  18.9 us
    all_to_all x3, starting transfers between devices, over_chips(): lax.all_to_all(spread, 'dp', split_axis=0, concat_axis=0, tiled=True)  16.2 us
  transfers between devices with their start and end apart: 29, of which 12 were waited for; matrix products, arithmetic and copies ran while one was open for 26% of the time, Pallas kernels for 18%

profile of v1, /device:TPU:0, one launch (start us, length us, event | category | flops | bytes accessed | tf_op | source)
XLA Modules:
  0.0 726.1 jit_solution(15402953227587261338)
XLA Ops:
  0.7 2.0 sort.17
  4.6 3.0 collective-permute-start
  8.3 22.8 %collective-permute-done = bf16[8,64,1024]{2,1,0:T(8,128)(2,1)} collective-permute-done((bf16[8,64,1024]{2,1,0:T(8,128)(2,1)}, bf16[8,64,1024]{2,1,0:T(8,128)(2,1)}, u32[]{:S(2)}, u32[]{:S(2)}) %collective-permute-start) | collective-permute-done | bytes 1048608 | tf_op jit(solution)/shard_map/ppermute | solution.py:235
  32.5 53.3 %all_to_all.25 = bf16[8,2,64,1024]{3,2,1,0:T(8,128)(2,1)S(1)} all-to-all(bf16[8,2,64,1024]{3,2,1,0:T(8,128)(2,1)S(1)} %pad_maximum_fusion.7), channel_id=1, replica_groups=mesh['dp'=8,'tensor'=4] {'dp'}, dimensions={0} | all-to-all | bytes 4194304 | tf_op jit(solution)/shard_map/all_to_all | solution.py:244
  86.3 2.2 copy.37
  89.2 4.0 fusion.5
  101.9 2.7 select_bitcast_fusion.1
  105.1 28.4 %collective-permute-done.2 = bf16[1024,768]{1,0:T(8,128)(2,1)} collective-permute-done((bf16[1024,768]{1,0:T(8,128)(2,1)}, bf16[1024,768]{1,0:T(8,128)(2,1)}, u32[]{:S(2)}, u32[]{:S(2)}) %collective-permute-start.2) | collective-permute-done | bytes 1572896 | tf_op jit(solution)/shard_map/ppermute | solution.py:235
  137.6 7.7 %fusion.67.q_ref.k_ref.v_ref = bf16[2048,768]{1,0:T(8,128)(2,1)} fusion(bf16[1024,768]{1,0:T(8,128)(2,1)} %collective-permute-done.2, bf16[1024,1024]{1,0:T(8,128)(2,1)} %collective-permute-done.1, bf16[1024,1024]{1,0:T(8,128)(2,1)} %fusion.5), kind=kOutput, calls=%fused_computation.158 | convolution fusion | flops 3229614080 | bytes 8912896 | tf_op jit(solution)/shard_map/dot_general | solution.py:19
  145.3 7.7 %fusion.68.q_ref.k_ref.v_ref = bf16[2048,768]{1,0:T(8,128)(2,1)} fusion(bf16[1024,768]{1,0:T(8,128)(2,1)} %constant_dynamic-update-slice_fusion, bf16[1024,1024]{1,0:T(8,128)(2,1)} %collective-permute-done.1, bf16[1024,1024]{1,0:T(8,128)(2,1)} %fusion.5), kind=kOutput, calls=%fused_computation.159 | convolution fusion | flops 3229614080 | bytes 8912896 | tf_op jit(solution)/shard_map/dot_general | solution.py:19
  153.1 28.5 %attend.2 = (bf16[2048,256]{1,0:T(8,128)(2,1)}, f32[2048,256]{1,0:T(8,128)}) custom-call(s32[5]{0:T(128)} %pad_add_fusion.info, bf16[2048,768]{1,0:T(8,128)(2,1)} %fusion.68.q_ref.k_ref.v_ref, bf16[2048,768]{1,0:T(8,128)(2,1)} %fusion.68.q_ref.k_ref.v_ref, bf16[2048,768]{1,0:T(8,128)(2,1)} %fusion.68.q_ref.k_ref.v_ref), custom_call_target="tpu_custom_call" | custom-call | tf_op jit(solution)/shard_map/attend/pallas_call | solution.py:91
  181.5 3.8 fusion.46
  185.3 28.1 %attend.3 = (bf16[2048,256]{1,0:T(8,128)(2,1)}, f32[2048,256]{1,0:T(8,128)}) custom-call(s32[5]{0:T(128)} %pad_add_fusion.info, bf16[2048,768]{1,0:T(8,128)(2,1)} %fusion.67.q_ref.k_ref.v_ref, bf16[2048,768]{1,0:T(8,128)(2,1)} %fusion.67.q_ref.k_ref.v_ref, bf16[2048,768]{1,0:T(8,128)(2,1)} %fusion.67.q_ref.k_ref.v_ref), custom_call_target="tpu_custom_call" | custom-call | tf_op jit(solution)/shard_map/attend/pallas_call | solution.py:91
  213.4 3.3 add_convert_fusion.2
  222.0 7.1 collective-permute-done.8
  230.5 29.0 %collective-permute-done.6 = bf16[1024,704]{0,1:T(8,128)(2,1)} collective-permute-done((bf16[1024,704]{0,1:T(8,128)(2,1)}, bf16[1024,704]{0,1:T(8,128)(2,1)}, u32[]{:S(2)}, u32[]{:S(2)}) %collective-permute-start.6) | collective-permute-done | bytes 1441824 | tf_op jit(solution)/shard_map/ppermute | solution.py:235
  261.0 2.8 fusion.50
  264.0 2.8 fusion.48
  267.5 4.5 multiply_reduce_fusion.2
  273.2 2.8 copy-done.37
  276.0 11.2 %fusion.27 = f32[2048,1408]{1,0:T(8,128)} fusion(bf16[1408,1024]{1,0:T(8,128)(2,1)S(1)} %copy-done.37, bf16[1024,1024]{1,0:T(8,128)(2,1)} %collective-permute-done.12, bf16[1024,1024]{1,0:T(8,128)(2,1)} %fusion.13), kind=kOutput, calls=%fused_computation.66 | convolution fusion | flops 5913968640 | bytes 18612224 | tf_op jit(solution)/shard_map/dot_general | solution.py:19
  288.5 11.1 %fusion.65 = f32[2048,1408]{1,0:T(8,128)} fusion(bf16[1024,1408]{0,1:T(8,128)(2,1)S(1)} %copy-done.40, bf16[1024,1024]{1,0:T(8,128)(2,1)S(1)} %collective-permute-done.5, bf16[1024,1024]{1,0:T(8,128)(2,1)S(1)} %multiply_convert_fusion.4), kind=kOutput, calls=%fused_computation.156 | convolution fusion | flops 5913968640 | bytes 18612224 | tf_op jit(solution)/shard_map/dot_general | solution.py:19
  299.6 22.6 %multiply_convert_fusion.1 = (bf16[2048,1408]{1,0:T(8,128)(2,1)}, bf16[2048,1408]{1,0:T(8,128)(2,1)}, bf16[2048,1408]{1,0:T(8,128)(2,1)}) fusion(f32[2048,1408]{1,0:T(8,128)} %fusion.27, f32[2048,1408]{1,0:T(8,128)} %fusion.65, bf16[1024,1408]{0,1:T(8,128)(2,1)} %copy-done.34, bf16[1024,1024]{1,0:T(8,128)(2,1)} %copy-done.59, bf16[1024,1024]{1,0:T(8,128)(2,1)} %copy-done.24), kind=kOutput, calls=%fused_computation.4 | convolution fusion | flops 5957222400 | bytes 47448064 | tf_op jit(solution)/shard_map/dot_general | solution.py:19
  322.2 6.2 fusion.14
  328.5 3.4 fusion.18
  332.0 4.8 add_convert_fusion.1
  336.8 3.4 fusion.20
  340.2 9.0 %fusion.64 = f32[1408,1024]{1,0:T(8,128)S(1)} fusion(bf16[2048,1408]{1,0:T(8,128)(2,1)} %get-tuple-element.114, bf16[1024,1024]{1,0:T(8,128)(2,1)S(1)} %copy-done.60, bf16[1024,1024]{1,0:T(8,128)(2,1)S(1)} %copy-done.25), kind=kOutput, calls=%fused_computation.155 | convolution fusion | flops 5913968640 | bytes 15728640 | tf_op jit(solution)/shard_map/dot_general | solution.py:19
  349.3 2.0 multiply_reduce_fusion
  351.3 4.2 fusion.69
  356.1 9.6 %fusion.63 = f32[1408,1024]{1,0:T(8,128)S(1)} fusion(bf16[2048,1408]{1,0:T(8,128)(2,1)} %get-tuple-element.115, bf16[1024,1024]{1,0:T(8,128)(2,1)S(1)} %copy-done.61, bf16[1024,1024]{1,0:T(8,128)(2,1)S(1)} %copy-done.25), kind=kOutput, calls=%fused_computation.154 | convolution fusion | flops 5913968640 | bytes 15728640 | tf_op jit(solution)/shard_map/dot_general | solution.py:19
  367.3 1.8 slice.226
  369.1 8.8 %fusion.26 = f32[1408,1024]{1,0:T(8,128)S(1)} fusion(bf16[2048,1408]{1,0:T(8,128)(2,1)S(1)} %bitcast.138, bf16[1024,1024]{1,0:T(8,128)(2,1)} %collective-permute-done.12, bf16[1024,1024]{1,0:T(8,128)(2,1)} %fusion.13), kind=kOutput, calls=%fused_computation.65 | convolution fusion | flops 5913968640 | bytes 15728640 | tf_op jit(solution)/shard_map/dot_general | solution.py:19
  379.4 2.2 convolution_convert_fusion.1
  383.2 2.3 fusion.61.do_ref
  385.5 36.2 %attend_back.3 = (bf16[2048,256]{1,0:T(8,128)(2,1)}, bf16[2048,256]{1,0:T(8,128)(2,1)}, bf16[2048,256]{1,0:T(8,128)(2,1)}) custom-call(s32[5]{0:T(128)} %pad_add_fusion.info, bf16[2048,768]{1,0:T(8,128)(2,1)} %fusion.67.q_ref.k_ref.v_ref, bf16[2048,768]{1,0:T(8,128)(2,1)} %fusion.67.q_ref.k_ref.v_ref, bf16[2048,768]{1,0:T(8,128)(2,1)} %fusion.67.q_ref.k_ref.v_ref, ...), custom_call_target="tpu_custom_call" | custom-call | tf_op jit(solution)/shard_map/attend_back/pallas_call | solution.py:184
  424.5 8.0 %convolution_convert_fusion = bf16[768,1024]{1,0:T(8,128)(2,1)} fusion(bf16[2048,768]{1,0:T(8,128)(2,1)S(1)} %constant_dynamic-update-slice_fusion.12, bf16[1024,1024]{1,0:T(8,128)(2,1)} %collective-permute-done.1, bf16[1024,1024]{1,0:T(8,128)(2,1)} %fusion.5), kind=kOutput, calls=%fused_computation.73 | convolution fusion | flops 3230400512 | bytes 8912896 | tf_op jit(solution)/shard_map/dot_general | solution.py:19
  432.5 2.4 fusion.62.do_ref
  434.9 36.0 %attend_back.2 = (bf16[2048,256]{1,0:T(8,128)(2,1)}, bf16[2048,256]{1,0:T(8,128)(2,1)}, bf16[2048,256]{1,0:T(8,128)(2,1)}) custom-call(s32[5]{0:T(128)} %pad_add_fusion.info, bf16[2048,768]{1,0:T(8,128)(2,1)} %fusion.68.q_ref.k_ref.v_ref, bf16[2048,768]{1,0:T(8,128)(2,1)} %fusion.68.q_ref.k_ref.v_ref, bf16[2048,768]{1,0:T(8,128)(2,1)} %fusion.68.q_ref.k_ref.v_ref, ...), custom_call_target="tpu_custom_call" | custom-call | tf_op jit(solution)/shard_map/attend_back/pallas_call | solution.py:184
  473.7 6.4 fusion.36
  482.3 4.2 all-to-all-start.3
  486.6 6.4 add_convert_fusion
  493.0 6.2 fusion.42
  500.8 5.9 all-to-all-start.2
  506.8 3.6 pad_maximum_fusion
  511.9 3.2 fusion.40
  515.2 3.4 fusion.38
  518.6 3.9 fusion.12
  525.7 18.8 %all-to-all-done.2 = bf16[8,768,128]{2,1,0:T(8,128)(2,1)} async-done(((bf16[8,768,128]{2,1,0:T(8,128)(2,1)}), bf16[8,768,128]{2,1,0:T(8,128)(2,1)}, u32[]{:S(2)}, u32[]{:S(2)}) %all-to-all-start.2) | async-done | bytes 1572896 | tf_op jit(solution)/shard_map/all_to_all | solution.py:313
  544.5 3.6 all-to-all-start.1
  548.2 58.0 %collective-permute-done.24 = bf16[2112,1024]{1,0:T(8,128)(2,1)} collective-permute-done((bf16[2112,1024]{1,0:T(8,128)(2,1)}, bf16[2112,1024]{1,0:T(8,128)(2,1)}, u32[]{:S(2)}, u32[]{:S(2)}) %collective-permute-start.24) | collective-permute-done | bytes 4325408 | tf_op jit(solution)/shard_map/ppermute | solution.py:235
  606.2 4.1 bitcast_bitcast_fusion
  610.3 6.0 all-to-all-start.4
  616.4 6.2 fusion.28
  622.7 4.1 collective-permute-done.9
  626.8 5.6 multiply_convert_fusion.3
  636.3 23.7 %collective-permute-done.18 = f32[2,1024]{1,0:T(2,128)S(1)} collective-permute-done((f32[2,1024]{1,0:T(2,128)S(1)}, f32[2,1024]{1,0:T(2,128)S(1)}, u32[]{:S(2)}, u32[]{:S(2)}) %collective-permute-start.18) | collective-permute-done | bytes 8224 | tf_op jit(solution)/shard_map/ppermute | solution.py:235
  660.0 2.1 collective-permute-start.19
  666.4 3.9 maximum_select_fusion
  670.3 15.8 %collective-permute-done.20 = f32[2,1024]{1,0:T(2,128)S(1)} collective-permute-done((f32[2,1024]{1,0:T(2,128)S(1)}, f32[2,1024]{1,0:T(2,128)S(1)}, u32[]{:S(2)}, u32[]{:S(2)}) %collective-permute-start.20) | collective-permute-done | bytes 8224 | tf_op jit(solution)/shard_map/ppermute | solution.py:366
  686.1 3.9 collective-permute-start.21
  690.8 21.1 %collective-permute-done.21 = f32[2,1024]{1,0:T(2,128)S(1)} collective-permute-done((f32[2,1024]{1,0:T(2,128)S(1)}, f32[2,1024]{1,0:T(2,128)S(1)}, u32[]{:S(2)}, u32[]{:S(2)}) %collective-permute-start.21) | collective-permute-done | bytes 8224 | tf_op jit(solution)/shard_map/ppermute | solution.py:366
  718.0 3.7 gather_fusion.2
  721.7 2.9 convert_reduce_fusion
  (252 shorter events, 62.3 us)
Async XLA Ops:
  4.6 26.5 %collective-permute-start = (bf16[8,64,1024]{2,1,0:T(8,128)(2,1)}, bf16[8,64,1024]{2,1,0:T(8,128)(2,1)}, u32[]{:S(2)}, u32[]{:S(2)}) collective-permute-start(bf16[8,64,1024]{2,1,0:T(8,128)(2,1)} %gather_fusion.1), channel_id=1, source_target_pairs={{0,2},{2,0},{1,3},{3,1},{4,6},{6,4},{5,7},{7,5},{8,10},{10,8},{9,1... | collective-permute-start | bytes 3145736 | tf_op jit(solution)/shard_map/ppermute | solution.py:235
  89.1 183.4 %copy-start.50 = (f32[1024]{0:T(1024)}, f32[1024]{0:T(1024)S(1)}, u32[]{:S(2)}) copy-start(f32[1024]{0:T(1024)S(1)} %rsqrt.26) | copy-start | bytes 12292
  93.2 6.8 copy-start.62
  93.2 43.9 %collective-permute-start.1 = (bf16[1024,1024]{1,0:T(8,128)(2,1)}, bf16[1024,1024]{1,0:T(8,128)(2,1)}, u32[]{:S(2)}, u32[]{:S(2)}) collective-permute-start(bf16[1024,1024]{1,0:T(8,128)(2,1)} %fusion.5), channel_id=1, source_target_pairs={{0,1},{1,0},{2,3},{3,2},{4,5},{5,4},{6,7},{7,6},{8,9},{9,8},{10,11... | collective-permute-start | bytes 6291464 | tf_op jit(solution)/shard_map/ppermute | solution.py:232
  94.1 10.5 %copy-start.19 = (bf16[256,1024]{1,0:T(8,128)(2,1)S(1)}, bf16[256,1024]{1,0:T(8,128)(2,1)}, u32[]{:S(2)}) copy-start(bf16[256,1024]{1,0:T(8,128)(2,1)} %param.24) | copy-start | bytes 1572868
  96.0 37.6 %collective-permute-start.2 = (bf16[1024,768]{1,0:T(8,128)(2,1)}, bf16[1024,768]{1,0:T(8,128)(2,1)}, u32[]{:S(2)}, u32[]{:S(2)}) collective-permute-start(bf16[1024,768]{1,0:T(8,128)(2,1)} %constant_dynamic-update-slice_fusion), channel_id=1, source_target_pairs={{0,2},{2,0},{1,3},{3,1},{4,6},{6,4},{5,7},{7,5},{8,10},{10,8},{9,1... | collective-permute-start | bytes 4718600 | tf_op jit(solution)/shard_map/ppermute | solution.py:235
  104.6 108.8 %collective-permute-start.3 = (bf16[256,1024]{1,0:T(8,128)(2,1)S(1)}, bf16[256,1024]{1,0:T(8,128)(2,1)S(1)}, u32[]{:S(2)}, u32[]{:S(2)}) collective-permute-start(bf16[256,1024]{1,0:T(8,128)(2,1)S(1)} %copy-done.19), channel_id=1, source_target_pairs={{0,2},{2,0},{1,3},{3,1},{4,6},{6,4},{5,7},{7,5},{8,10},{10,8},{9,1... | collective-permute-start | bytes 1572872 | tf_op jit(solution)/shard_map/ppermute | solution.py:235
  133.5 86.9 %collective-permute-start.7 = (bf16[1024,704]{0,1:T(8,128)(2,1)}, bf16[1024,704]{0,1:T(8,128)(2,1)}, u32[]{:S(2)}, u32[]{:S(2)}) collective-permute-start(bf16[1024,704]{0,1:T(8,128)(2,1)} %param.27), channel_id=1, source_target_pairs={{0,2},{2,0},{1,3},{3,1},{4,6},{6,4},{5,7},{7,5},{8,10},{10,8},{9,1... | collective-permute-start | bytes 4325384 | tf_op jit(solution)/shard_map/ppermute | solution.py:235
  135.1 83.6 %collective-permute-start.11 = (bf16[512,1024]{1,0:T(8,128)(2,1)}, bf16[512,1024]{1,0:T(8,128)(2,1)S(1)}, u32[]{:S(2)}, u32[]{:S(2)}) collective-permute-start(bf16[512,1024]{1,0:T(8,128)(2,1)} %get-tuple-element.38), channel_id=1, source_target_pairs={{0,2},{2,0},{1,3},{3,1},{4,6},{6,4},{5,7},{7,5},{8,10},{10,8},{9,1... | collective-permute-start | bytes 3145736 | tf_op jit(solution)/shard_map/ppermute | solution.py:235
  135.6 93.5 %collective-permute-start.8 = (bf16[704,1024]{1,0:T(8,128)(2,1)}, bf16[704,1024]{1,0:T(8,128)(2,1)}, u32[]{:S(2)}, u32[]{:S(2)}) collective-permute-start(bf16[704,1024]{1,0:T(8,128)(2,1)} %param.28), channel_id=1, source_target_pairs={{0,2},{2,0},{1,3},{3,1},{4,6},{6,4},{5,7},{7,5},{8,10},{10,8},{9,1... | collective-permute-start | bytes 4325384 | tf_op jit(solution)/shard_map/ppermute | solution.py:235
  137.1 122.4 %collective-permute-start.6 = (bf16[1024,704]{0,1:T(8,128)(2,1)}, bf16[1024,704]{0,1:T(8,128)(2,1)}, u32[]{:S(2)}, u32[]{:S(2)}) collective-permute-start(bf16[1024,704]{0,1:T(8,128)(2,1)} %param.26), channel_id=1, source_target_pairs={{0,2},{2,0},{1,3},{3,1},{4,6},{6,4},{5,7},{7,5},{8,10},{10,8},{9,1... | collective-permute-start | bytes 4325384 | tf_op jit(solution)/shard_map/ppermute | solution.py:235
  216.8 50.0 %collective-permute-start.4 = (bf16[1024,1024]{1,0:T(8,128)(2,1)S(1)}, bf16[1024,1024]{1,0:T(8,128)(2,1)S(1)}, u32[]{:S(2)}, u32[]{:S(2)}) collective-permute-start(bf16[1024,1024]{1,0:T(8,128)(2,1)S(1)} %add_convert_fusion.2), channel_id=1, source_target_pairs={{0,1},{1,0},{2,3},{3,2},{4,5},{5,4},{6,7},{7,6},{8,9},{9,8},{10,11... | collective-permute-start | bytes 6291464 | tf_op jit(solution)/shard_map/ppermute | solution.py:232
  220.5 52.7 %collective-permute-start.12 = (bf16[1024,1024]{1,0:T(8,128)(2,1)}, bf16[1024,1024]{1,0:T(8,128)(2,1)}, u32[]{:S(2)}, u32[]{:S(2)}) collective-permute-start(bf16[1024,1024]{1,0:T(8,128)(2,1)} %fusion.13), channel_id=1, source_target_pairs={{0,1},{1,0},{2,3},{3,2},{4,5},{5,4},{6,7},{7,6},{8,9},{9,8},{10,11... | collective-permute-start | bytes 6291464 | tf_op jit(solution)/shard_map/ppermute | solution.py:232
  221.9 41.8 %copy-start.39 = (bf16[1024,1408]{0,1:T(8,128)(2,1)}, bf16[1024,1408]{0,1:T(8,128)(2,1)S(1)}, u32[]{:S(2)}) copy-start(bf16[1024,1408]{0,1:T(8,128)(2,1)S(1)} %constant_dynamic-update-slice_fusion.5) | copy-start | bytes 8650756
  221.9 39.0 %copy-start.10 = (bf16[2048,256]{1,0:T(8,128)(2,1)S(1)}, bf16[2048,256]{1,0:T(8,128)(2,1)}, u32[]{:S(2)}) copy-start(bf16[2048,256]{1,0:T(8,128)(2,1)} %get-tuple-element.31.o_ref) | copy-start | bytes 3145732
  222.0 39.0 %copy-start.20 = (bf16[256,1024]{1,0:T(8,128)(2,1)S(1)}, bf16[256,1024]{1,0:T(8,128)(2,1)}, u32[]{:S(2)}) copy-start(bf16[256,1024]{1,0:T(8,128)(2,1)} %param.24) | copy-start | bytes 1572868
  230.5 33.2 %copy-start.36 = (bf16[1408,1024]{1,0:T(8,128)(2,1)}, bf16[1408,1024]{1,0:T(8,128)(2,1)S(1)}, u32[]{:S(2)}) copy-start(bf16[1408,1024]{1,0:T(8,128)(2,1)S(1)} %constant_dynamic-update-slice_fusion.7) | copy-start | bytes 8650756
  272.0 79.3 %copy-start.4 = (f32[1024,1024]{1,0:T(8,128)}, f32[1024,1024]{1,0:T(8,128)S(1)}, u32[]{:S(2)}) copy-start(f32[1024,1024]{1,0:T(8,128)S(1)} %get-tuple-element.113) | copy-start | bytes 12582916
  272.5 14.7 %copy-start.24 = (bf16[1024,1024]{1,0:T(8,128)(2,1)}, bf16[1024,1024]{1,0:T(8,128)(2,1)S(1)}, u32[]{:S(2)}) copy-start(bf16[1024,1024]{1,0:T(8,128)(2,1)S(1)} %multiply_convert_fusion.4) | copy-start | bytes 6291460
  272.5 14.7 %collective-permute-start.5 = (bf16[1024,1024]{1,0:T(8,128)(2,1)S(1)}, bf16[1024,1024]{1,0:T(8,128)(2,1)S(1)}, u32[]{:S(2)}, u32[]{:S(2)}) collective-permute-start(bf16[1024,1024]{1,0:T(8,128)(2,1)S(1)} %multiply_convert_fusion.4), channel_id=1, source_target_pairs={{0,1},{1,0},{2,3},{3,2},{4,5},{5,4},{6,7},{7,6},{8,9},{9,8},{10,11... | collective-permute-start | bytes 6291464 | tf_op jit(solution)/shard_map/ppermute | solution.py:232
  273.2 15.3 %copy-start.40 = (bf16[1024,1408]{0,1:T(8,128)(2,1)S(1)}, bf16[1024,1408]{0,1:T(8,128)(2,1)}, u32[]{:S(2)}) copy-start(bf16[1024,1408]{0,1:T(8,128)(2,1)} %copy-done.39) | copy-start | bytes 8650756
  322.2 9.7 %slice-start.3 = ((s8[5767168]{0:T(1024)(128)(4,1)}), s8[4194304]{0:T(1024)(128)(4,1)S(1)}, s32[]{:S(2)}) async-start(s8[5767168]{0:T(1024)(128)(4,1)} %bitcast.135), calls=%async_computation.8 | async-start | bytes 8388608
  336.8 12.5 %collective-permute-start.13 = (bf16[1024,1024]{1,0:T(8,128)(2,1)}, bf16[1024,1024]{1,0:T(8,128)(2,1)S(1)}, u32[]{:S(2)}, u32[]{:S(2)}) collective-permute-start(bf16[1024,1024]{1,0:T(8,128)(2,1)} %add_convert_fusion.1), channel_id=1, source_target_pairs={{0,1},{1,0},{2,3},{3,2},{4,5},{5,4},{6,7},{7,6},{8,9},{9,8},{10,11... | collective-permute-start | bytes 6291464 | tf_op jit(solution)/shard_map/ppermute | solution.py:232
  349.2 16.5 %copy-start.7 = (f32[1408,1024]{1,0:T(8,128)}, f32[1408,1024]{1,0:T(8,128)S(1)}, u32[]{:S(2)}) copy-start(f32[1408,1024]{1,0:T(8,128)S(1)} %fusion.64) | copy-start | bytes 17301508
  351.3 17.8 %slice-start.5 = ((s8[5767168]{0:T(1024)(128)(4,1)}), s8[4194304]{0:T(1024)(128)(4,1)S(1)}, s32[]{:S(2)}) async-start(s8[5767168]{0:T(1024)(128)(4,1)} %bitcast.137), calls=%async_computation.10 | async-start | bytes 8388608
  355.5 27.6 %copy-start.26 = (bf16[1024,1024]{1,0:T(8,128)(2,1)}, bf16[1024,1024]{1,0:T(8,128)(2,1)S(1)}, u32[]{:S(2)}) copy-start(bf16[1024,1024]{1,0:T(8,128)(2,1)S(1)} %get-tuple-element.109) | copy-start | bytes 6291460
  355.5 13.6 %slice-start.6 = ((s8[5767168]{0:T(1024)(128)(4,1)}), s8[1572864]{0:T(1024)(128)(4,1)S(1)}, s32[]{:S(2)}) async-start(s8[5767168]{0:T(1024)(128)(4,1)} %bitcast.137), calls=%async_computation.11 | async-start | bytes 3145728
  355.5 23.9 %collective-permute-start.14 = (bf16[1024,1024]{1,0:T(8,128)(2,1)S(1)}, bf16[1024,1024]{1,0:T(8,128)(2,1)S(1)}, u32[]{:S(2)}, u32[]{:S(2)}) collective-permute-start(bf16[1024,1024]{1,0:T(8,128)(2,1)S(1)} %get-tuple-element.109), channel_id=1, source_target_pairs={{0,1},{1,0},{2,3},{3,2},{4,5},{5,4},{6,7},{7,6},{8,9},{9,8},{10,11... | collective-permute-start | bytes 6291464 | tf_op jit(solution)/shard_map/ppermute | solution.py:232
  365.8 12.2 %copy-start.8 = (f32[1408,1024]{1,0:T(8,128)}, f32[1408,1024]{1,0:T(8,128)S(1)}, u32[]{:S(2)}) copy-start(f32[1408,1024]{1,0:T(8,128)S(1)} %fusion.63) | copy-start | bytes 17301508
  381.6 98.5 %collective-permute-start.23 = (bf16[256,1024]{1,0:T(8,128)(2,1)}, bf16[256,1024]{1,0:T(8,128)(2,1)S(1)}, u32[]{:S(2)}, u32[]{:S(2)}) collective-permute-start(bf16[256,1024]{1,0:T(8,128)(2,1)} %convolution_convert_fusion.1), channel_id=1, source_target_pairs={{0,2},{2,0},{1,3},{3,1},{4,6},{6,4},{5,7},{7,5},{8,10},{10,8},{9,1... | collective-permute-start | bytes 1572872 | tf_op jit(solution)/shard_map/ppermute | solution.py:235
  424.4 8.0 %copy-start.45 = (bf16[2048,768]{1,0:T(8,128)(2,1)}, bf16[2048,768]{1,0:T(8,128)(2,1)S(1)}, u32[]{:S(2)}) copy-start(bf16[2048,768]{1,0:T(8,128)(2,1)S(1)} %constant_dynamic-update-slice_fusion.12) | copy-start | bytes 9437188
  424.4 8.0 %copy-start.21 = (bf16[256,1024]{1,0:T(8,128)(2,1)S(1)}, bf16[256,1024]{1,0:T(8,128)(2,1)}, u32[]{:S(2)}) copy-start(bf16[256,1024]{1,0:T(8,128)(2,1)} %param.24) | copy-start | bytes 1572868
  424.5 8.0 %copy-start.27 = (bf16[1024,1024]{1,0:T(8,128)(2,1)S(1)}, bf16[1024,1024]{1,0:T(8,128)(2,1)}, u32[]{:S(2)}) copy-start(bf16[1024,1024]{1,0:T(8,128)(2,1)} %copy-done.26) | copy-start | bytes 6291460
  424.5 8.0 %copy-start.57 = (bf16[1024,1024]{1,0:T(8,128)(2,1)S(1)}, bf16[1024,1024]{1,0:T(8,128)(2,1)}, u32[]{:S(2)}) copy-start(bf16[1024,1024]{1,0:T(8,128)(2,1)} %copy-done.56) | copy-start | bytes 6291460
  432.5 60.6 %collective-permute-start.22 = (bf16[768,1024]{1,0:T(8,128)(2,1)}, bf16[768,1024]{1,0:T(8,128)(2,1)}, u32[]{:S(2)}, u32[]{:S(2)}) collective-permute-start(bf16[768,1024]{1,0:T(8,128)(2,1)} %convolution_convert_fusion), channel_id=1, source_target_pairs={{0,2},{2,0},{1,3},{3,1},{4,6},{6,4},{5,7},{7,5},{8,10},{10,8},{9,1... | collective-permute-start | bytes 4718600 | tf_op jit(solution)/shard_map/ppermute | solution.py:235
  473.7 6.4 copy-start.47
  473.7 6.4 copy-start.11
  473.7 6.4 copy-start.28
  473.7 6.4 copy-start.58
  482.3 18.5 %all-to-all-start.3 = ((bf16[8,256,128]{2,1,0:T(8,128)(2,1)}), bf16[8,256,128]{2,1,0:T(8,128)(2,1)S(1)}, u32[]{:S(2)}, u32[]{:S(2)}) async-start(bf16[8,256,128]{2,1,0:T(8,128)(2,1)} %bitcast.119), calls=%async_computation.3 | async-start | bytes 1048576 | tf_op jit(solution)/shard_map/all_to_all | solution.py:313
  486.6 6.4 copy-start.48
  493.0 25.6 %collective-permute-start.15 = (bf16[1024,1024]{1,0:T(8,128)(2,1)}, bf16[1024,1024]{1,0:T(8,128)(2,1)}, u32[]{:S(2)}, u32[]{:S(2)}) collective-permute-start(bf16[1024,1024]{1,0:T(8,128)(2,1)} %add_convert_fusion), channel_id=1, source_target_pairs={{0,1},{1,0},{2,3},{3,2},{4,5},{5,4},{6,7},{7,6},{8,9},{9,8},{10,11... | collective-permute-start | bytes 6291464 | tf_op jit(solution)/shard_map/ppermute | solution.py:232
  499.3 7.5 %copy-start.13 = (bf16[704,1024]{1,0:T(8,128)(2,1)S(1)}, bf16[704,1024]{1,0:T(8,128)(2,1)}, u32[]{:S(2)}) copy-start(bf16[704,1024]{1,0:T(8,128)(2,1)} %slice.227) | copy-start | bytes 4325380
  499.3 7.5 %copy-start.14 = (bf16[704,1024]{1,0:T(8,128)(2,1)S(1)}, bf16[704,1024]{1,0:T(8,128)(2,1)}, u32[]{:S(2)}) copy-start(bf16[704,1024]{1,0:T(8,128)(2,1)} %slice.226) | copy-start | bytes 4325380
  500.8 9.6 %copy-start.22 = (bf16[8,256,128]{2,1,0:T(8,128)(2,1)}, bf16[8,256,128]{2,1,0:T(8,128)(2,1)S(1)}, u32[]{:S(2)}) copy-start(bf16[8,256,128]{2,1,0:T(8,128)(2,1)S(1)} %all-to-all-done.3) | copy-start | bytes 1572868
  500.8 43.7 %all-to-all-start.2 = ((bf16[8,768,128]{2,1,0:T(8,128)(2,1)}), bf16[8,768,128]{2,1,0:T(8,128)(2,1)}, u32[]{:S(2)}, u32[]{:S(2)}) async-start(bf16[8,768,128]{2,1,0:T(8,128)(2,1)} %bitcast.117), calls=%async_computation.2 | async-start | bytes 3145728 | tf_op jit(solution)/shard_map/all_to_all | solution.py:313
  510.4 95.8 %collective-permute-start.24 = (bf16[2112,1024]{1,0:T(8,128)(2,1)}, bf16[2112,1024]{1,0:T(8,128)(2,1)}, u32[]{:S(2)}, u32[]{:S(2)}) collective-permute-start(bf16[2112,1024]{1,0:T(8,128)(2,1)} %pad_maximum_fusion), channel_id=1, source_target_pairs={{0,2},{2,0},{1,3},{3,1},{4,6},{6,4},{5,7},{7,5},{8,10},{10,8},{9,1... | collective-permute-start | bytes 12976136 | tf_op jit(solution)/shard_map/ppermute | solution.py:235
  544.5 65.8 %all-to-all-start.1 = ((bf16[8,2,64,1024]{3,2,1,0:T(8,128)(2,1)}), bf16[8,2,64,1024]{3,2,1,0:T(8,128)(2,1)S(1)}, u32[]{:S(2)}, u32[]{:S(2)}) async-start(bf16[8,2,64,1024]{3,2,1,0:T(8,128)(2,1)} %bitcast.120), calls=%async_computation.1 | async-start | bytes 4194304 | tf_op jit(solution)/shard_map/all_to_all | solution.py:347
  548.2 58.1 %slice-start.2 = ((f32[1408,1024]{1,0:T(8,128)}), f32[704,1024]{1,0:T(8,128)S(1)}, s32[]{:S(2)}) async-start(f32[1408,1024]{1,0:T(8,128)} %copy-done.9), calls=%async_computation.7 | async-start | bytes 5767168 | tf_op jit(solution)/shard_map/slice | solution.py:317
  548.2 58.1 %slice-start = ((f32[1408,1024]{1,0:T(8,128)}), f32[704,1024]{1,0:T(8,128)S(1)}, s32[]{:S(2)}) async-start(f32[1408,1024]{1,0:T(8,128)} %copy-done.7), calls=%async_computation.5 | async-start | bytes 5767168 | tf_op jit(solution)/shard_map/slice | solution.py:317
  548.2 58.1 %slice-start.1 = ((f32[1408,1024]{1,0:T(8,128)}), f32[704,1024]{1,0:T(8,128)S(1)}, s32[]{:S(2)}) async-start(f32[1408,1024]{1,0:T(8,128)} %copy-done.8), calls=%async_computation.6 | async-start | bytes 5767168 | tf_op jit(solution)/shard_map/slice | solution.py:317
  610.3 111.4 %all-to-all-start.4 = ((bf16[8,2112,128]{2,1,0:T(8,128)(2,1)}), bf16[8,2112,128]{2,1,0:T(8,128)(2,1)}, u32[]{:S(2)}, u32[]{:S(2)}) async-start(bf16[8,2112,128]{2,1,0:T(8,128)(2,1)} %bitcast_bitcast_fusion), calls=%async_computation.4 | async-start | bytes 8650752 | tf_op jit(solution)/shard_map/all_to_all | solution.py:313
  616.3 10.5 %copy-start.5 = (f32[1024,1024]{1,0:T(8,128)S(1)}, f32[1024,1024]{1,0:T(8,128)}, u32[]{:S(2)}) copy-start(f32[1024,1024]{1,0:T(8,128)} %copy-done.4) | copy-start | bytes 12582916
  616.4 10.5 %copy-start.38 = (bf16[1408,1024]{1,0:T(8,128)(2,1)S(1)}, bf16[1408,1024]{1,0:T(8,128)(2,1)}, u32[]{:S(2)}) copy-start(bf16[1408,1024]{1,0:T(8,128)(2,1)} %copy-done.36) | copy-start | bytes 8650756
  622.6 4.2 collective-permute-start.9
  632.4 3.2 collective-permute-start.17
  634.1 32.3 %collective-permute-start.10 = (bf16[512,1024]{1,0:T(8,128)(2,1)}, bf16[512,1024]{1,0:T(8,128)(2,1)}, u32[]{:S(2)}, u32[]{:S(2)}) collective-permute-start(bf16[512,1024]{1,0:T(8,128)(2,1)} %get-tuple-element.122), channel_id=1, source_target_pairs={{0,2},{2,0},{1,3},{3,1},{4,6},{6,4},{5,7},{7,5},{8,10},{10,8},{9,1... | collective-permute-start | bytes 3145736 | tf_op jit(solution)/shard_map/ppermute | solution.py:235
  635.7 24.3 %collective-permute-start.18 = (f32[2,1024]{1,0:T(2,128)S(1)}, f32[2,1024]{1,0:T(2,128)S(1)}, u32[]{:S(2)}, u32[]{:S(2)}) collective-permute-start(f32[2,1024]{1,0:T(2,128)S(1)} %fusion.60), channel_id=1, source_target_pairs={{0,2},{2,0},{1,3},{3,1},{4,6},{6,4},{5,7},{7,5},{8,10},{10,8},{9,1... | collective-permute-start | bytes 24584 | tf_op jit(solution)/shard_map/ppermute | solution.py:235
  660.0 5.7 collective-permute-start.19
  663.3 26.8 %copy-start.23 = (bf16[8,256,128]{2,1,0:T(8,128)(2,1)S(1)}, bf16[8,256,128]{2,1,0:T(8,128)(2,1)}, u32[]{:S(2)}) copy-start(bf16[8,256,128]{2,1,0:T(8,128)(2,1)} %copy-done.22) | copy-start | bytes 1572868
  663.3 53.1 %collective-permute-start.16 = (bf16[8,64,1024]{2,1,0:T(8,128)(2,1)}, bf16[8,64,1024]{2,1,0:T(8,128)(2,1)S(1)}, u32[]{:S(2)}, u32[]{:S(2)}) collective-permute-start(bf16[8,64,1024]{2,1,0:T(8,128)(2,1)} %get-tuple-element.118), channel_id=1, source_target_pairs={{0,2},{2,0},{1,3},{3,1},{4,6},{6,4},{5,7},{7,5},{8,10},{10,8},{9,1... | collective-permute-start | bytes 3145736 | tf_op jit(solution)/shard_map/ppermute | solution.py:235
  665.7 20.4 %collective-permute-start.20 = (f32[2,1024]{1,0:T(2,128)S(1)}, f32[2,1024]{1,0:T(2,128)S(1)}, u32[]{:S(2)}, u32[]{:S(2)}) collective-permute-start(f32[2,1024]{1,0:T(2,128)S(1)} %add.196), channel_id=1, source_target_pairs={{0,8},{4,12},{8,0},{12,4},{16,24},{20,28},{24,16},{28,20},{1,9},{5... | collective-permute-start | bytes 24584 | tf_op jit(solution)/shard_map/ppermute | solution.py:366
  686.1 25.7 %collective-permute-start.21 = (f32[2,1024]{1,0:T(2,128)S(1)}, f32[2,1024]{1,0:T(2,128)S(1)}, u32[]{:S(2)}, u32[]{:S(2)}) collective-permute-start(f32[2,1024]{1,0:T(2,128)S(1)} %add.197), channel_id=1, source_target_pairs={{0,16},{4,20},{8,24},{12,28},{16,0},{20,4},{24,8},{28,12},{1,17},{... | collective-permute-start | bytes 24584 | tf_op jit(solution)/shard_map/ppermute | solution.py:366
  718.0 7.7 %copy-start.1 = (bf16[16,1,64,1024]{3,2,1,0:T(8,128)(2,1)S(1)}, bf16[16,1,64,1024]{3,2,1,0:T(8,128)(2,1)}, u32[]{:S(2)}) copy-start(bf16[16,1,64,1024]{3,2,1,0:T(8,128)(2,1)} %param.17) | copy-start | bytes 6291460
  (37 other events, 133.8 us)

commit v2 on v1

--- a/solution.py
+++ b/solution.py
@@ -6,6 +6,7 @@
 from jax.experimental import pallas as pl
 from jax.experimental.pallas import tpu as pltpu
 from jax.sharding import PartitionSpec as P
+
 
 HEAD_DIM = 64
 PAIR = 2 * HEAD_DIM
@@ -203,7 +204,7 @@
     return lax.optimization_barrier((value,) + others)[0]
 
 
-def local(
+def layer(
     patches,
     lengths,
     deal,
@@ -234,23 +235,27 @@
     def swap_chip(value):
         return lax.ppermute(value, "tensor", [(0, 2), (2, 0), (1, 3), (3, 1)])
 
+    def exchange(value):
+        return lax.all_to_all(value, "dp", split_axis=0, concat_axis=0, tiled=True)
+
     slot_owner = jnp.argsort(deal)
     owners = slot_owner.reshape(groups, 2)
     mine = jnp.take(owners, chip, axis=1)
     theirs = jnp.take(owners, 1 - chip, axis=1)
     length = lengths[mine[group]]
     given = swap_chip(patches[theirs, 0])
-    sent = jnp.stack((patches[mine, 0], given), 1)
-    arrived = lax.all_to_all(sent, "dp", split_axis=0, concat_axis=0, tiled=True)
-    inputs = arrived.transpose(1, 0, 2, 3).reshape(2 * quarter, width).astype(F32)
+    arrived_near = exchange(patches[mine, 0])
+    arrived_far = exchange(given)
+    inputs = jnp.stack((arrived_near, arrived_far)).reshape(2 * quarter, width).astype(F32)
 
     w_qkv = jnp.concatenate((w_query, w_key, w_value), 1)
-    w_qkv_far, w_out_far = swap_chip((after(w_qkv, given), after(w_out, given)))
-    w_gate_far, w_up_far, w_down_far = swap_chip(
-        tuple(after(w, w_qkv_far) for w in (w_gate, w_up, w_down))
-    )
+    w_qkv_far = swap_chip(after(w_qkv, given))
+    w_out_far = swap_chip(after(w_out, given))
+    w_gate_far = swap_chip(after(w_gate, arrived_far))
+    w_up_far = swap_chip(after(w_up, arrived_far))
+    w_down_far = swap_chip(after(w_down, arrived_far))
     cot_near = jnp.take(cotangent[:, 0], chip, axis=0)
-    cot_far = swap_chip(after(jnp.take(cotangent[:, 0], 1 - chip, axis=0), w_qkv_far))
+    cot_far = swap_chip(after(jnp.take(cotangent[:, 0], 1 - chip, axis=0), arrived_far))
 
     numbers = jnp.arange(4)
     slots = 2 * (numbers % 2 != core) + (numbers // 2 != chip)
@@ -306,55 +311,43 @@
 
     half = w_gate.shape[1]
 
-    def over_chips(parts, ahead=()):
+    def over_chips(parts):
         far = swap_chip(jnp.concatenate([far.astype(LOW) for _, far in parts], 0))
         summed = jnp.concatenate([near for near, _ in parts], 0) + far.astype(F32)
         spread = summed.astype(LOW).reshape(-1, groups, width // groups).transpose(1, 0, 2)
-        moved = lax.all_to_all(spread, "dp", split_axis=0, concat_axis=0, tiled=True)
-        return jnp.sum(moved.astype(F32), 0)
+        return jnp.sum(exchange(spread).astype(F32), 0)
 
     def halves(value):
         return (value[:half], value[half:])
 
-    ffn_shards = over_chips(
-        [
-            halves(dot(product, grad_ffn, 0, 0)),
-            halves(dot(grad_gate, rows_ffn, 0, 0)),
-            halves(dot(grad_up, rows_ffn, 0, 0)),
-        ]
-    )
+    down_shard = over_chips([halves(dot(product, grad_ffn, 0, 0))])
+    up_halves = halves(dot(grad_up, rows_ffn, 0, 0))
+    gate_up_shards = over_chips([halves(dot(grad_gate, rows_ffn, 0, 0)), up_halves])
     grad_normed_ffn = scatter(
         lambda part: dot(grad_gate[part], gates, 1, 1) + dot(grad_up[part], ups, 1, 1)
     )
     grad_hidden, gain_ffn_part = norm_back(hidden, factor_ffn, ffn_gain, grad_normed_ffn)
     grad_hidden = grad_hidden + grad_result
     grad_attn = gather(grad_hidden.astype(LOW))
-    out_shard = over_chips([(dot(mixed_near, grad_attn, 0, 0), dot(mixed_far, grad_attn, 0, 0))])
-    grad_far = attend_back(
-        info, qkv[1], dot(grad_attn, w_out_far, 1, 1, LOW), mixed_far, total_far, quarter
-    )
-    grad_near = attend_back(
-        info, qkv[0], dot(grad_attn, w_out, 1, 1, LOW), mixed_near, total_near, quarter
-    )
+    out_halves = (dot(mixed_near, grad_attn, 0, 0), dot(mixed_far, grad_attn, 0, 0))
+    back_far = dot(grad_attn, w_out_far, 1, 1, LOW)
+    grad_far = attend_back(info, qkv[1], back_far, mixed_far, total_far, quarter)
     grad_far = jnp.concatenate(grad_far, 1)
+    weight_far = dot(grad_far, rows_attn, 0, 0, LOW)
+    back_near = after(dot(grad_attn, w_out, 1, 1, LOW), weight_far)
+    grad_near = attend_back(info, qkv[0], back_near, mixed_near, total_near, quarter)
     grad_near = jnp.concatenate(grad_near, 1)
     grad_normed_attn = scatter(
         lambda part: dot(grad_near[part], w_qkv, 1, 1) + dot(grad_far[part], w_qkv_far, 1, 1)
     )
-    qkv_shards = over_chips([(dot(grad_near, rows_attn, 0, 0), dot(grad_far, rows_attn, 0, 0))])
+    qkv_shards = over_chips([out_halves, (dot(grad_near, rows_attn, 0, 0), weight_far)])
     grad_inputs, gain_attn_part = norm_back(inputs, factor_attn, attn_gain, grad_normed_attn)
     grad_inputs = (grad_inputs + grad_hidden).astype(LOW)
-    returned = lax.all_to_all(
-        grad_inputs.reshape(2, groups, band, width).transpose(1, 0, 2, 3),
-        "dp",
-        split_axis=0,
-        concat_axis=0,
-        tiled=True,
-    )
-    back_near = returned[:, 0]
-    back_far = swap_chip(returned[:, 1])
+    returned = exchange(grad_inputs[quarter:].reshape(groups, band, width))
+    by_far = swap_chip(returned)
+    by_near = exchange(grad_inputs[:quarter].reshape(groups, band, width))
     by_slot = jnp.where(
-        chip == 0, jnp.stack((back_near, back_far), 1), jnp.stack((back_far, back_near), 1)
+        chip == 0, jnp.stack((by_near, by_far), 1), jnp.stack((by_far, by_near), 1)
     ).reshape(seq_total, band, width)
     grad_patches = by_slot[deal][:, None]
 
@@ -373,14 +366,14 @@
         output,
         grad_patches,
         gain_grads[0],
-        qkv_shards[:part].T,
         qkv_shards[part : 2 * part].T,
-        qkv_shards[2 * part :].T,
-        out_shard,
+        qkv_shards[2 * part : 3 * part].T,
+        qkv_shards[3 * part :].T,
+        qkv_shards[:part],
         gain_grads[1],
-        ffn_shards[half : 2 * half].T,
-        ffn_shards[2 * half :].T,
-        ffn_shards[:half],
+        gate_up_shards[:half].T,
+        gate_up_shards[half:].T,
+        down_shard,
     )
 
 
@@ -413,4 +406,4 @@
         P("dp", "tensor"),
         P("tensor", "dp"),
     )
-    return jax.shard_map(local, mesh=mesh, in_specs=in_specs, out_specs=out_specs, check_vma=False)
+    return jax.shard_map(layer, mesh=mesh, in_specs=in_specs, out_specs=out_specs, check_vma=False)

time: 736 us -> 715 us (0.971)
  blocking collectives: 53.3 us -> 29.9 us
  waiting for transfers between devices: 230 us -> 219 us
  matrix products: 172 us -> 182 us
    all_to_all x4 -> x6, waiting for transfers between devices: 18.9 us -> 57.7 us  [exchange(): return lax.all_to_all(value, 'dp', split_axis=0, concat_axis=0, tiled=True)]
    ppermute x3, waiting for transfers between devices: 37.8 us -> 3.37 us  [total_of(): lax.ppermute(value, 'dp', [(i, i ^ step) for i in range(groups)])]
    all_to_all x1, blocking collectives: 53.3 us -> 29.9 us  [exchange(): return lax.all_to_all(value, 'dp', split_axis=0, concat_axis=0, tiled=True)]
    ppermute x13, waiting for transfers between devices: 169 us -> 157 us  [swap_chip(): return lax.ppermute(value, 'tensor', [(0, 2), (2, 0), (1, 3), (3, 1)])]
    dot_general x28, matrix products: 172 us -> 182 us  [dot(): lax.dot_general(left, right, (((left_dim,), (right_dim,)), ((), ())), pre...]
    all_to_all x4 -> x6, starting transfers between devices: 19.8 us -> 28.4 us  [exchange(): return lax.all_to_all(value, 'dp', split_axis=0, concat_axis=0, tiled=True)]
    transpose x1 -> x3, other arithmetic: 4.09 us -> 11.8 us  [over_chips(): summed.astype(LOW).reshape(-1, groups, width // groups).transpose(1, 0, 2)]
    unnamed x150 -> x116, local copies, waits for them, and re-layouts: 15.9 us -> 19.2 us
  transfers between devices with their start and end apart: 29 -> 31, of which waited for: 12 -> 14; matrix products, arithmetic and copies ran while one was open for 26% -> 31% of each run, Pallas kernels for 18% -> 18%
where the time goes in v2:
time: 715 us; the launch traced here: 705 us
  waiting for transfers between devices  219 us (31%)
  matrix products  182 us (25%)
  Pallas kernels  128 us (18%)
  other arithmetic  49.8 us (7%)
  starting transfers between devices  47.7 us (7%)
  local copies, waits for them, and re-layouts  43.7 us (6%)
  blocking collectives  29.9 us (4%)
    dot_general x28, matrix products, dot(): lax.dot_general(left, right, (((left_dim,), (right_dim,)), ((), ())), pre...  182 us
    ppermute x13, waiting for transfers between devices, swap_chip(): return lax.ppermute(value, 'tensor', [(0, 2), (2, 0), (1, 3), (3, 1)])  157 us
    pallas_call x2, Pallas kernels, attend_back(): pl.pallas_call(functools.partial(attend_back_kernel, block), grid_spec=pl...  72 us
    all_to_all x6, waiting for transfers between devices, exchange(): return lax.all_to_all(value, 'dp', split_axis=0, concat_axis=0, tiled=True)  57.7 us
    pallas_call x2, Pallas kernels, attend(): pl.pallas_call(attend_kernel, grid_spec=pltpu.PrefetchScalarGridSpec(num_...  56.3 us
    all_to_all x1, blocking collectives, exchange(): return lax.all_to_all(value, 'dp', split_axis=0, concat_axis=0, tiled=True)  29.9 us
    all_to_all x6, starting transfers between devices, exchange(): return lax.all_to_all(value, 'dp', split_axis=0, concat_axis=0, tiled=True)  28.4 us
    unnamed x116, local copies, waits for them, and re-layouts  19.2 us
  transfers between devices with their start and end apart: 31, of which 14 were waited for; matrix products, arithmetic and copies ran while one was open for 31% of the time, Pallas kernels for 18%

profile of v2, /device:TPU:0, one launch (start us, length us, event | category | flops | bytes accessed | tf_op | source)
XLA Modules:
  0.0 705.4 jit_solution(7763178498510496537)
XLA Ops:
  0.7 2.0 sort.17
  4.6 7.3 %all-to-all-start = ((bf16[8,64,1024]{2,1,0:T(8,128)(2,1)}), bf16[8,64,1024]{2,1,0:T(8,128)(2,1)S(1)}, u32[]{:S(2)}, u32[]{:S(2)}) async-start(bf16[8,64,1024]{2,1,0:T(8,128)(2,1)} %gather_fusion), calls=%async_computation | async-start | bytes 2097152 | tf_op jit(solution)/shard_map/all_to_all | solution.py:239
  15.1 23.3 %collective-permute-done = bf16[8,64,1024]{2,1,0:T(8,128)(2,1)S(1)} collective-permute-done((bf16[8,64,1024]{2,1,0:T(8,128)(2,1)}, bf16[8,64,1024]{2,1,0:T(8,128)(2,1)S(1)}, u32[]{:S(2)}, u32[]{:S(2)}) %collective-permute-start) | collective-permute-done | bytes 1048608 | tf_op jit(solution)/shard_map/ppermute | solution.py:236
  38.4 29.9 %all_to_all.35 = bf16[8,64,1024]{2,1,0:T(8,128)(2,1)S(1)} all-to-all(bf16[8,64,1024]{2,1,0:T(8,128)(2,1)S(1)} %collective-permute-done), channel_id=1, replica_groups=mesh['dp'=8,'tensor'=4] {'dp'}, dimensions={0} | all-to-all | bytes 2097152 | tf_op jit(solution)/shard_map/all_to_all | solution.py:239
  79.3 2.7 select_bitcast_fusion.1
  86.0 7.8 %fusion.72.q_ref.k_ref.v_ref = bf16[2048,768]{1,0:T(8,128)(2,1)} fusion(bf16[1024,768]{1,0:T(8,128)(2,1)} %constant_dynamic-update-slice_fusion, bf16[1024,1024]{1,0:T(8,128)(2,1)} %collective-permute-done.1, bf16[1024,1024]{1,0:T(8,128)(2,1)} %fusion.5), kind=kOutput, calls=%fused_computation.160 | convolution fusion | flops 3229614080 | bytes 8912896 | tf_op jit(solution)/shard_map/dot_general | solution.py:20
  93.8 17.1 %collective-permute-done.2 = bf16[1024,768]{1,0:T(8,128)(2,1)} collective-permute-done((bf16[1024,768]{1,0:T(8,128)(2,1)}, bf16[1024,768]{1,0:T(8,128)(2,1)}, u32[]{:S(2)}, u32[]{:S(2)}) %collective-permute-start.2) | collective-permute-done | bytes 1572896 | tf_op jit(solution)/shard_map/ppermute | solution.py:236
  110.9 7.7 %fusion.71.q_ref.k_ref.v_ref = bf16[2048,768]{1,0:T(8,128)(2,1)} fusion(bf16[1024,768]{1,0:T(8,128)(2,1)} %collective-permute-done.2, bf16[1024,1024]{1,0:T(8,128)(2,1)} %collective-permute-done.1, bf16[1024,1024]{1,0:T(8,128)(2,1)} %fusion.5), kind=kOutput, calls=%fused_computation.159 | convolution fusion | flops 3229614080 | bytes 8912896 | tf_op jit(solution)/shard_map/dot_general | solution.py:20
  118.6 28.1 %attend.3 = (bf16[2048,256]{1,0:T(8,128)(2,1)}, f32[2048,256]{1,0:T(8,128)}) custom-call(s32[5]{0:T(128)} %pad_add_fusion.info, bf16[2048,768]{1,0:T(8,128)(2,1)} %fusion.71.q_ref.k_ref.v_ref, bf16[2048,768]{1,0:T(8,128)(2,1)} %fusion.71.q_ref.k_ref.v_ref, bf16[2048,768]{1,0:T(8,128)(2,1)} %fusion.71.q_ref.k_ref.v_ref), custom_call_target="tpu_custom_call" | custom-call | tf_op jit(solution)/shard_map/attend/pallas_call | solution.py:92
  146.7 28.3 %attend.2 = (bf16[2048,256]{1,0:T(8,128)(2,1)}, f32[2048,256]{1,0:T(8,128)}) custom-call(s32[5]{0:T(128)} %pad_add_fusion.info, bf16[2048,768]{1,0:T(8,128)(2,1)} %fusion.72.q_ref.k_ref.v_ref, bf16[2048,768]{1,0:T(8,128)(2,1)} %fusion.72.q_ref.k_ref.v_ref, bf16[2048,768]{1,0:T(8,128)(2,1)} %fusion.72.q_ref.k_ref.v_ref), custom_call_target="tpu_custom_call" | custom-call | tf_op jit(solution)/shard_map/attend/pallas_call | solution.py:92
  175.0 2.0 fusion.47
  177.0 3.1 add_convert_fusion.2
  187.5 18.9 %collective-permute-done.8 = bf16[704,1024]{1,0:T(8,128)(2,1)} collective-permute-done((bf16[704,1024]{1,0:T(8,128)(2,1)}, bf16[704,1024]{1,0:T(8,128)(2,1)}, u32[]{:S(2)}, u32[]{:S(2)}) %collective-permute-start.8) | collective-permute-done | bytes 1441824 | tf_op jit(solution)/shard_map/ppermute | solution.py:236
  211.7 2.8 multiply_reduce_fusion.2
  215.1 21.7 %collective-permute-done.6 = bf16[1024,704]{0,1:T(8,128)(2,1)S(1)} collective-permute-done((bf16[1024,704]{0,1:T(8,128)(2,1)S(1)}, bf16[1024,704]{0,1:T(8,128)(2,1)S(1)}, u32[]{:S(2)}, u32[]{:S(2)}) %collective-permute-start.6) | collective-permute-done | bytes 1441824 | tf_op jit(solution)/shard_map/ppermute | solution.py:236
  236.9 11.6 %fusion.29 = f32[2048,1408]{1,0:T(8,128)} fusion(bf16[1408,1024]{1,0:T(8,128)(2,1)S(1)} %copy-done.29, bf16[1024,1024]{1,0:T(8,128)(2,1)} %collective-permute-done.12, bf16[1024,1024]{1,0:T(8,128)(2,1)S(1)} %fusion.13), kind=kOutput, calls=%fused_computation.69 | convolution fusion | flops 5913968640 | bytes 18612224 | tf_op jit(solution)/shard_map/dot_general | solution.py:20
  249.9 11.3 %fusion.67 = f32[2048,1408]{1,0:T(8,128)} fusion(bf16[1024,1408]{0,1:T(8,128)(2,1)S(1)} %copy-done.32, bf16[1024,1024]{1,0:T(8,128)(2,1)S(1)} %collective-permute-done.5, bf16[1024,1024]{1,0:T(8,128)(2,1)S(1)} %multiply_convert_fusion.4), kind=kOutput, calls=%fused_computation.155 | convolution fusion | flops 5913968640 | bytes 18612224 | tf_op jit(solution)/shard_map/dot_general | solution.py:20
  261.2 22.6 %multiply_convert_fusion.1 = (bf16[2048,1408]{1,0:T(8,128)(2,1)}, bf16[2048,1408]{1,0:T(8,128)(2,1)}, bf16[2048,1408]{1,0:T(8,128)(2,1)}) fusion(f32[2048,1408]{1,0:T(8,128)} %fusion.29, f32[2048,1408]{1,0:T(8,128)} %fusion.67, bf16[1024,1408]{0,1:T(8,128)(2,1)} %copy-done.25, bf16[1024,1024]{1,0:T(8,128)(2,1)} %copy-done.46, bf16[1024,1024]{1,0:T(8,128)(2,1)} %copy-done.16), kind=kOutput, calls=%fused_computation.4 | convolution fusion | flops 5957222400 | bytes 47448064 | tf_op jit(solution)/shard_map/dot_general | solution.py:20
  283.8 9.8 %fusion.28 = f32[1408,1024]{1,0:T(8,128)S(1)} fusion(bf16[2048,1408]{1,0:T(8,128)(2,1)} %get-tuple-element.118, bf16[1024,1024]{1,0:T(8,128)(2,1)} %collective-permute-done.12, bf16[1024,1024]{1,0:T(8,128)(2,1)S(1)} %fusion.13), kind=kOutput, calls=%fused_computation.68 | convolution fusion | flops 5913968640 | bytes 15728640 | tf_op jit(solution)/shard_map/dot_general | solution.py:20
  295.5 7.0 fusion.16
  302.5 6.6 add_convert_fusion.1
  309.2 9.0 %fusion.66 = f32[1408,1024]{1,0:T(8,128)S(1)} fusion(bf16[2048,1408]{1,0:T(8,128)(2,1)} %get-tuple-element.116, bf16[1024,1024]{1,0:T(8,128)(2,1)S(1)} %copy-done.47, bf16[1024,1024]{1,0:T(8,128)(2,1)S(1)} %copy-done.17), kind=kOutput, calls=%fused_computation.154 | convolution fusion | flops 5913968640 | bytes 15728640 | tf_op jit(solution)/shard_map/dot_general | solution.py:20
  318.2 11.8 %fusion.65 = f32[1408,1024]{1,0:T(8,128)S(1)} fusion(bf16[2048,1408]{1,0:T(8,128)(2,1)} %get-tuple-element.117, bf16[1024,1024]{1,0:T(8,128)(2,1)} %copy-done.46, bf16[1024,1024]{1,0:T(8,128)(2,1)S(1)} %copy-done.17), kind=kOutput, calls=%fused_computation.153 | convolution fusion | flops 5913968640 | bytes 15728640 | tf_op jit(solution)/shard_map/dot_general | solution.py:20
  333.0 5.7 fusion.20
  338.8 5.2 fusion.22
  344.1 2.0 multiply_reduce_fusion
  346.1 4.1 fusion.73
  350.5 3.7 slice.174
  356.1 2.8 bitcast_bitcast_fusion.2
  358.9 3.8 all-to-all-start.6
  362.7 34.7 %collective-permute-done.23 = bf16[1408,1024]{1,0:T(8,128)(2,1)} collective-permute-done((bf16[1408,1024]{1,0:T(8,128)(2,1)}, bf16[1408,1024]{1,0:T(8,128)(2,1)}, u32[]{:S(2)}, u32[]{:S(2)}) %collective-permute-start.23) | collective-permute-done | bytes 2883616 | tf_op jit(solution)/shard_map/ppermute | solution.py:236
  397.4 5.6 bitcast_bitcast_fusion
  403.1 4.7 fusion.63.do_ref
  407.8 36.0 %attend_back.2 = (bf16[2048,256]{1,0:T(8,128)(2,1)}, bf16[2048,256]{1,0:T(8,128)(2,1)}, bf16[2048,256]{1,0:T(8,128)(2,1)}) custom-call(s32[5]{0:T(128)} %pad_add_fusion.info, bf16[2048,768]{1,0:T(8,128)(2,1)} %fusion.71.q_ref.k_ref.v_ref, bf16[2048,768]{1,0:T(8,128)(2,1)} %fusion.71.q_ref.k_ref.v_ref, bf16[2048,768]{1,0:T(8,128)(2,1)} %fusion.71.q_ref.k_ref.v_ref, ...), custom_call_target="tpu_custom_call" | custom-call | tf_op jit(solution)/shard_map/attend_back/pallas_call | solution.py:185
  446.7 5.1 fusion.64.do_ref
  451.7 6.8 fusion.70
  458.6 36.0 %attend_back.3 = (bf16[2048,256]{1,0:T(8,128)(2,1)}, bf16[2048,256]{1,0:T(8,128)(2,1)}, bf16[2048,256]{1,0:T(8,128)(2,1)}) custom-call(s32[5]{0:T(128)} %pad_add_fusion.info, bf16[2048,768]{1,0:T(8,128)(2,1)} %fusion.72.q_ref.k_ref.v_ref, bf16[2048,768]{1,0:T(8,128)(2,1)} %fusion.72.q_ref.k_ref.v_ref, bf16[2048,768]{1,0:T(8,128)(2,1)} %fusion.72.q_ref.k_ref.v_ref, ...), custom_call_target="tpu_custom_call" | custom-call | tf_op jit(solution)/shard_map/attend_back/pallas_call | solution.py:185
  494.6 2.4 constant_dynamic-update-slice_fusion.14
  497.0 2.3 constant_dynamic-update-slice_fusion.13
  499.4 4.8 all-to-all-start.5
  505.3 3.8 fusion.39
  509.2 3.2 add_convert_fusion
  512.5 3.7 fusion.43
  516.2 3.4 fusion.41
  519.7 2.6 fusion.12
  525.6 43.7 %all-to-all-done.5 = bf16[8,1408,128]{2,1,0:T(8,128)(2,1)} async-done(((bf16[8,1408,128]{2,1,0:T(8,128)(2,1)}), bf16[8,1408,128]{2,1,0:T(8,128)(2,1)}, u32[]{:S(2)}, u32[]{:S(2)}) %all-to-all-start.5) | async-done | bytes 2883616 | tf_op jit(solution)/shard_map/all_to_all | solution.py:239
  569.3 3.6 all-to-all-start.3
  572.9 3.6 convolution_convert_fusion
  579.1 6.4 fusion.31
  585.5 13.3 %all-to-all-done.3 = bf16[8,64,1024]{2,1,0:T(8,128)(2,1)S(1)} async-done(((bf16[8,64,1024]{2,1,0:T(8,128)(2,1)}), bf16[8,64,1024]{2,1,0:T(8,128)(2,1)S(1)}, u32[]{:S(2)}, u32[]{:S(2)}) %all-to-all-start.3) | async-done | bytes 1048608 | tf_op jit(solution)/shard_map/all_to_all | solution.py:239
  599.8 3.9 all-to-all-start.2
  603.8 3.5 fusion.62
  607.3 6.2 fusion.69
  613.5 12.1 %collective-permute-done.22 = bf16[1024,1024]{1,0:T(8,128)(2,1)} collective-permute-done((bf16[1024,1024]{1,0:T(8,128)(2,1)}, bf16[1024,1024]{1,0:T(8,128)(2,1)}, u32[]{:S(2)}, u32[]{:S(2)}) %collective-permute-start.22) | collective-permute-done | bytes 2097184 | tf_op jit(solution)/shard_map/ppermute | solution.py:236
  625.7 3.3 bitcast_bitcast_fusion.1
  629.6 5.0 all-to-all-start.4
  634.7 8.0 %multiply_convert_fusion.3 = bf16[1024,1024]{1,0:T(8,128)(2,1)S(1)} fusion(f32[1024,1024]{1,0:T(8,128)} %copy-done.2, bf16[1024,1024]{1,0:T(8,128)(2,1)} %collective-permute-done.9, f32[1024]{0:T(1024)S(1)} %fusion.53, bf16[1408,1024]{1,0:T(8,128)(2,1)} %copy-done.28, bf16[2048,1408]{1,0:T(8,128)(2,1)} %get-tuple-element.118), kind=kOutput, calls=%fused_computation.43 | convolution fusion | flops 2958032896 | bytes 14159872 | tf_op jit(solution)/shard_map/dot_general | solution.py:20
  647.2 20.4 %collective-permute-done.18 = f32[2,1024]{1,0:T(2,128)S(1)} collective-permute-done((f32[2,1024]{1,0:T(2,128)S(1)}, f32[2,1024]{1,0:T(2,128)S(1)}, u32[]{:S(2)}, u32[]{:S(2)}) %collective-permute-start.18) | collective-permute-done | bytes 8224 | tf_op jit(solution)/shard_map/ppermute | solution.py:236
  671.4 2.5 collective-permute-start.20
  674.5 3.2 maximum_select_fusion
  680.3 2.0 collective-permute-done.21
  682.9 2.3 convert_reduce_fusion
  686.1 8.5 %collective-permute-done.16 = bf16[8,64,1024]{2,1,0:T(8,128)(2,1)S(1)} collective-permute-done((bf16[8,64,1024]{2,1,0:T(8,128)(2,1)}, bf16[8,64,1024]{2,1,0:T(8,128)(2,1)S(1)}, u32[]{:S(2)}, u32[]{:S(2)}) %collective-permute-start.16) | collective-permute-done | bytes 1048608 | tf_op jit(solution)/shard_map/ppermute | solution.py:236
  696.2 3.9 gather_fusion.2
  (213 shorter events, 69.9 us)
Async XLA Ops:
  4.6 33.7 %all-to-all-start = ((bf16[8,64,1024]{2,1,0:T(8,128)(2,1)}), bf16[8,64,1024]{2,1,0:T(8,128)(2,1)S(1)}, u32[]{:S(2)}, u32[]{:S(2)}) async-start(bf16[8,64,1024]{2,1,0:T(8,128)(2,1)} %gather_fusion), calls=%async_computation | async-start | bytes 2097152 | tf_op jit(solution)/shard_map/all_to_all | solution.py:239
  11.9 56.9 %copy-start.41 = (f32[1024]{0:T(1024)S(1)}, f32[1024]{0:T(1024)}, u32[]{:S(2)}) copy-start(f32[1024]{0:T(1024)} %param.20) | copy-start | bytes 12292
  13.5 24.8 %collective-permute-start = (bf16[8,64,1024]{2,1,0:T(8,128)(2,1)}, bf16[8,64,1024]{2,1,0:T(8,128)(2,1)S(1)}, u32[]{:S(2)}, u32[]{:S(2)}) collective-permute-start(bf16[8,64,1024]{2,1,0:T(8,128)(2,1)} %gather_fusion.1), channel_id=1, source_target_pairs={{0,2},{2,0},{1,3},{3,1},{4,6},{6,4},{5,7},{7,5},{8,10},{10,8},{9,1... | collective-permute-start | bytes 3145736 | tf_op jit(solution)/shard_map/ppermute | solution.py:236
  38.4 173.3 %copy-start.3 = (bf16[8,64,1024]{2,1,0:T(8,128)(2,1)}, bf16[8,64,1024]{2,1,0:T(8,128)(2,1)S(1)}, u32[]{:S(2)}) copy-start(bf16[8,64,1024]{2,1,0:T(8,128)(2,1)S(1)} %all-to-all-done) | copy-start | bytes 3145732
  68.2 143.5 %copy-start.5 = (bf16[8,64,1024]{2,1,0:T(8,128)(2,1)}, bf16[8,64,1024]{2,1,0:T(8,128)(2,1)S(1)}, u32[]{:S(2)}) copy-start(bf16[8,64,1024]{2,1,0:T(8,128)(2,1)S(1)} %all_to_all.35) | copy-start | bytes 3145732
  68.8 3.6 copy-start.39
  68.8 3.6 copy-start.36
  68.8 8.6 %copy-start.48 = (s32[16]{0:T(128)S(1)}, s32[16]{0:T(128)}, u32[]{:S(2)}) copy-start(s32[16]{0:T(128)} %param.18) | copy-start | bytes 196
  70.7 13.8 %collective-permute-start.1 = (bf16[1024,1024]{1,0:T(8,128)(2,1)}, bf16[1024,1024]{1,0:T(8,128)(2,1)}, u32[]{:S(2)}, u32[]{:S(2)}) collective-permute-start(bf16[1024,1024]{1,0:T(8,128)(2,1)} %fusion.5), channel_id=1, source_target_pairs={{0,1},{1,0},{2,3},{3,2},{4,5},{5,4},{6,7},{7,6},{8,9},{9,8},{10,11... | collective-permute-start | bytes 6291464 | tf_op jit(solution)/shard_map/ppermute | solution.py:233
  73.3 37.6 %collective-permute-start.2 = (bf16[1024,768]{1,0:T(8,128)(2,1)}, bf16[1024,768]{1,0:T(8,128)(2,1)}, u32[]{:S(2)}, u32[]{:S(2)}) collective-permute-start(bf16[1024,768]{1,0:T(8,128)(2,1)} %constant_dynamic-update-slice_fusion), channel_id=1, source_target_pairs={{0,2},{2,0},{1,3},{3,1},{4,6},{6,4},{5,7},{7,5},{8,10},{10,8},{9,1... | collective-permute-start | bytes 4718600 | tf_op jit(solution)/shard_map/ppermute | solution.py:236
  82.0 95.0 %collective-permute-start.3 = (bf16[256,1024]{1,0:T(8,128)(2,1)}, bf16[256,1024]{1,0:T(8,128)(2,1)}, u32[]{:S(2)}, u32[]{:S(2)}) collective-permute-start(bf16[256,1024]{1,0:T(8,128)(2,1)} %param.24), channel_id=1, source_target_pairs={{0,2},{2,0},{1,3},{3,1},{4,6},{6,4},{5,7},{7,5},{8,10},{10,8},{9,1... | collective-permute-start | bytes 1572872 | tf_op jit(solution)/shard_map/ppermute | solution.py:236
  82.5 103.5 %collective-permute-start.7 = (bf16[1024,704]{0,1:T(8,128)(2,1)}, bf16[1024,704]{0,1:T(8,128)(2,1)}, u32[]{:S(2)}, u32[]{:S(2)}) collective-permute-start(bf16[1024,704]{0,1:T(8,128)(2,1)} %param.27), channel_id=1, source_target_pairs={{0,2},{2,0},{1,3},{3,1},{4,6},{6,4},{5,7},{7,5},{8,10},{10,8},{9,1... | collective-permute-start | bytes 4325384 | tf_op jit(solution)/shard_map/ppermute | solution.py:236
  84.0 99.8 %collective-permute-start.11 = (bf16[512,1024]{1,0:T(8,128)(2,1)}, bf16[512,1024]{1,0:T(8,128)(2,1)}, u32[]{:S(2)}, u32[]{:S(2)}) collective-permute-start(bf16[512,1024]{1,0:T(8,128)(2,1)} %get-tuple-element.39), channel_id=1, source_target_pairs={{0,2},{2,0},{1,3},{3,1},{4,6},{6,4},{5,7},{7,5},{8,10},{10,8},{9,1... | collective-permute-start | bytes 3145736 | tf_op jit(solution)/shard_map/ppermute | solution.py:236
  84.5 121.9 %collective-permute-start.8 = (bf16[704,1024]{1,0:T(8,128)(2,1)}, bf16[704,1024]{1,0:T(8,128)(2,1)}, u32[]{:S(2)}, u32[]{:S(2)}) collective-permute-start(bf16[704,1024]{1,0:T(8,128)(2,1)} %param.28), channel_id=1, source_target_pairs={{0,2},{2,0},{1,3},{3,1},{4,6},{6,4},{5,7},{7,5},{8,10},{10,8},{9,1... | collective-permute-start | bytes 4325384 | tf_op jit(solution)/shard_map/ppermute | solution.py:236
  180.1 31.6 %collective-permute-start.4 = (bf16[1024,1024]{1,0:T(8,128)(2,1)}, bf16[1024,1024]{1,0:T(8,128)(2,1)}, u32[]{:S(2)}, u32[]{:S(2)}) collective-permute-start(bf16[1024,1024]{1,0:T(8,128)(2,1)} %add_convert_fusion.2), channel_id=1, source_target_pairs={{0,1},{1,0},{2,3},{3,2},{4,5},{5,4},{6,7},{7,6},{8,9},{9,8},{10,11... | collective-permute-start | bytes 6291464 | tf_op jit(solution)/shard_map/ppermute | solution.py:233
  183.8 53.0 %collective-permute-start.6 = (bf16[1024,704]{0,1:T(8,128)(2,1)S(1)}, bf16[1024,704]{0,1:T(8,128)(2,1)S(1)}, u32[]{:S(2)}, u32[]{:S(2)}) collective-permute-start(bf16[1024,704]{0,1:T(8,128)(2,1)S(1)} %copy-done.20), channel_id=1, source_target_pairs={{0,2},{2,0},{1,3},{3,1},{4,6},{6,4},{5,7},{7,5},{8,10},{10,8},{9,1... | collective-permute-start | bytes 4325384 | tf_op jit(solution)/shard_map/ppermute | solution.py:236
  185.4 22.5 %copy-start.8 = (bf16[2048,256]{1,0:T(8,128)(2,1)S(1)}, bf16[2048,256]{1,0:T(8,128)(2,1)}, u32[]{:S(2)}) copy-start(bf16[2048,256]{1,0:T(8,128)(2,1)} %get-tuple-element.32.o_ref) | copy-start | bytes 3145732
  185.4 22.5 %copy-start.14 = (bf16[256,1024]{1,0:T(8,128)(2,1)S(1)}, bf16[256,1024]{1,0:T(8,128)(2,1)}, u32[]{:S(2)}) copy-start(bf16[256,1024]{1,0:T(8,128)(2,1)} %param.24) | copy-start | bytes 1572868
  185.5 51.4 %collective-permute-start.12 = (bf16[1024,1024]{1,0:T(8,128)(2,1)S(1)}, bf16[1024,1024]{1,0:T(8,128)(2,1)}, u32[]{:S(2)}, u32[]{:S(2)}) collective-permute-start(bf16[1024,1024]{1,0:T(8,128)(2,1)S(1)} %fusion.13), channel_id=1, source_target_pairs={{0,1},{1,0},{2,3},{3,2},{4,5},{5,4},{6,7},{7,6},{8,9},{9,8},{10,11... | collective-permute-start | bytes 6291464 | tf_op jit(solution)/shard_map/ppermute | solution.py:233
  187.5 21.1 %copy-start.31 = (bf16[1024,1408]{0,1:T(8,128)(2,1)}, bf16[1024,1408]{0,1:T(8,128)(2,1)S(1)}, u32[]{:S(2)}) copy-start(bf16[1024,1408]{0,1:T(8,128)(2,1)S(1)} %constant_dynamic-update-slice_fusion.5) | copy-start | bytes 8650756
  214.5 131.6 %copy-start.2 = (f32[1024,1024]{1,0:T(8,128)}, f32[1024,1024]{1,0:T(8,128)S(1)}, u32[]{:S(2)}) copy-start(f32[1024,1024]{1,0:T(8,128)S(1)} %get-tuple-element.115) | copy-start | bytes 12582916
  214.5 22.2 %copy-start.24 = (bf16[1024,1408]{0,1:T(8,128)(2,1)S(1)}, bf16[1024,1408]{0,1:T(8,128)(2,1)}, u32[]{:S(2)}) copy-start(bf16[1024,1408]{0,1:T(8,128)(2,1)} %constant_dynamic-update-slice_fusion.4) | copy-start | bytes 8650756
  214.5 22.4 %copy-start.29 = (bf16[1408,1024]{1,0:T(8,128)(2,1)S(1)}, bf16[1408,1024]{1,0:T(8,128)(2,1)}, u32[]{:S(2)}) copy-start(bf16[1408,1024]{1,0:T(8,128)(2,1)} %copy-done.28) | copy-start | bytes 8650756
  215.0 33.6 %copy-start.16 = (bf16[1024,1024]{1,0:T(8,128)(2,1)}, bf16[1024,1024]{1,0:T(8,128)(2,1)S(1)}, u32[]{:S(2)}) copy-start(bf16[1024,1024]{1,0:T(8,128)(2,1)S(1)} %multiply_convert_fusion.4) | copy-start | bytes 6291460
  215.0 33.6 %collective-permute-start.5 = (bf16[1024,1024]{1,0:T(8,128)(2,1)S(1)}, bf16[1024,1024]{1,0:T(8,128)(2,1)S(1)}, u32[]{:S(2)}, u32[]{:S(2)}) collective-permute-start(bf16[1024,1024]{1,0:T(8,128)(2,1)S(1)} %multiply_convert_fusion.4), channel_id=1, source_target_pairs={{0,1},{1,0},{2,3},{3,2},{4,5},{5,4},{6,7},{7,6},{8,9},{9,8},{10,11... | collective-permute-start | bytes 6291464 | tf_op jit(solution)/shard_map/ppermute | solution.py:233
  236.9 11.7 %copy-start.25 = (bf16[1024,1408]{0,1:T(8,128)(2,1)}, bf16[1024,1408]{0,1:T(8,128)(2,1)S(1)}, u32[]{:S(2)}) copy-start(bf16[1024,1408]{0,1:T(8,128)(2,1)S(1)} %constant_dynamic-update-slice_fusion.3) | copy-start | bytes 8650756
  236.9 13.0 %copy-start.32 = (bf16[1024,1408]{0,1:T(8,128)(2,1)S(1)}, bf16[1024,1408]{0,1:T(8,128)(2,1)}, u32[]{:S(2)}) copy-start(bf16[1024,1408]{0,1:T(8,128)(2,1)} %copy-done.31) | copy-start | bytes 8650756
  283.8 11.7 %copy-start.33 = (bf16[1024,1408]{0,1:T(8,128)(2,1)S(1)}, bf16[1024,1408]{0,1:T(8,128)(2,1)}, u32[]{:S(2)}) copy-start(bf16[1024,1408]{0,1:T(8,128)(2,1)} %copy-done.31) | copy-start | bytes 8650756
  293.7 8.8 %slice-start = ((s8[5767168]{0:T(1024)(128)(4,1)}), s8[4194304]{0:T(1024)(128)(4,1)S(1)}, s32[]{:S(2)}) async-start(s8[5767168]{0:T(1024)(128)(4,1)} %bitcast.133), calls=%async_computation.7 | async-start | bytes 8388608
  293.9 62.2 %collective-permute-start.24 = (bf16[704,1024]{1,0:T(8,128)(2,1)S(1)}, bf16[704,1024]{1,0:T(8,128)(2,1)}, u32[]{:S(2)}, u32[]{:S(2)}) collective-permute-start(bf16[704,1024]{1,0:T(8,128)(2,1)S(1)} %slice.230), channel_id=1, source_target_pairs={{0,2},{2,0},{1,3},{3,1},{4,6},{6,4},{5,7},{7,5},{8,10},{10,8},{9,1... | collective-permute-start | bytes 4325384 | tf_op jit(solution)/shard_map/ppermute | solution.py:236
  295.5 7.0 copy-start.26
  295.5 7.0 slice-start.1
  302.5 6.7 copy-start.17
  302.5 6.7 copy-start.47
  309.1 34.9 %collective-permute-start.13 = (bf16[1024,1024]{1,0:T(8,128)(2,1)}, bf16[1024,1024]{1,0:T(8,128)(2,1)S(1)}, u32[]{:S(2)}, u32[]{:S(2)}) collective-permute-start(bf16[1024,1024]{1,0:T(8,128)(2,1)} %add_convert_fusion.1), channel_id=1, source_target_pairs={{0,1},{1,0},{2,3},{3,2},{4,5},{5,4},{6,7},{7,6},{8,9},{9,8},{10,11... | collective-permute-start | bytes 6291464 | tf_op jit(solution)/shard_map/ppermute | solution.py:233
  318.2 11.8 %copy-start.13 = (f32[1408,1024]{1,0:T(8,128)}, f32[1408,1024]{1,0:T(8,128)S(1)}, u32[]{:S(2)}) copy-start(f32[1408,1024]{1,0:T(8,128)S(1)} %fusion.66) | copy-start | bytes 17301508
  332.3 6.5 copy-start.27
  332.3 65.2 %collective-permute-start.23 = (bf16[1408,1024]{1,0:T(8,128)(2,1)}, bf16[1408,1024]{1,0:T(8,128)(2,1)}, u32[]{:S(2)}, u32[]{:S(2)}) collective-permute-start(bf16[1408,1024]{1,0:T(8,128)(2,1)} %pad_maximum_fusion.4), channel_id=1, source_target_pairs={{0,2},{2,0},{1,3},{3,1},{4,6},{6,4},{5,7},{7,5},{8,10},{10,8},{9,1... | collective-permute-start | bytes 8650760 | tf_op jit(solution)/shard_map/ppermute | solution.py:236
  350.2 52.9 %collective-permute-start.14 = (bf16[1024,1024]{1,0:T(8,128)(2,1)}, bf16[1024,1024]{1,0:T(8,128)(2,1)S(1)}, u32[]{:S(2)}, u32[]{:S(2)}) collective-permute-start(bf16[1024,1024]{1,0:T(8,128)(2,1)} %get-tuple-element.111), channel_id=1, source_target_pairs={{0,1},{1,0},{2,3},{3,2},{4,5},{5,4},{6,7},{7,6},{8,9},{9,8},{10,11... | collective-permute-start | bytes 6291464 | tf_op jit(solution)/shard_map/ppermute | solution.py:233
  358.9 140.4 %all-to-all-start.6 = ((bf16[8,704,128]{2,1,0:T(8,128)(2,1)}), bf16[8,704,128]{2,1,0:T(8,128)(2,1)S(1)}, u32[]{:S(2)}, u32[]{:S(2)}) async-start(bf16[8,704,128]{2,1,0:T(8,128)(2,1)} %bitcast_bitcast_fusion.2), calls=%async_computation.6 | async-start | bytes 2883584 | tf_op jit(solution)/shard_map/all_to_all | solution.py:239
  403.1 4.7 copy-start.44
  446.7 5.1 copy-start.37
  499.4 4.8 copy-start.22
  499.4 69.9 %all-to-all-start.5 = ((bf16[8,1408,128]{2,1,0:T(8,128)(2,1)}), bf16[8,1408,128]{2,1,0:T(8,128)(2,1)}, u32[]{:S(2)}, u32[]{:S(2)}) async-start(bf16[8,1408,128]{2,1,0:T(8,128)(2,1)} %bitcast_bitcast_fusion), calls=%async_computation.5 | async-start | bytes 5767168 | tf_op jit(solution)/shard_map/all_to_all | solution.py:239
  505.3 3.9 copy-start.38
  512.4 7.2 %collective-permute-start.15 = (bf16[1024,1024]{1,0:T(8,128)(2,1)S(1)}, bf16[1024,1024]{1,0:T(8,128)(2,1)S(1)}, u32[]{:S(2)}, u32[]{:S(2)}) collective-permute-start(bf16[1024,1024]{1,0:T(8,128)(2,1)S(1)} %add_convert_fusion), channel_id=1, source_target_pairs={{0,1},{1,0},{2,3},{3,2},{4,5},{5,4},{6,7},{7,6},{8,9},{9,8},{10,11... | collective-permute-start | bytes 6291464 | tf_op jit(solution)/shard_map/ppermute | solution.py:233
  516.2 3.4 copy-start.4
  524.1 48.8 %copy-start.12 = (bf16[2048,256]{1,0:T(8,128)(2,1)S(1)}, bf16[2048,256]{1,0:T(8,128)(2,1)}, u32[]{:S(2)}) copy-start(bf16[2048,256]{1,0:T(8,128)(2,1)} %get-tuple-element.34.o_ref) | copy-start | bytes 3145732
  569.3 29.6 %all-to-all-start.3 = ((bf16[8,64,1024]{2,1,0:T(8,128)(2,1)}), bf16[8,64,1024]{2,1,0:T(8,128)(2,1)S(1)}, u32[]{:S(2)}, u32[]{:S(2)}) async-start(bf16[8,64,1024]{2,1,0:T(8,128)(2,1)} %bitcast.13), calls=%async_computation.3 | async-start | bytes 2097152 | tf_op jit(solution)/shard_map/all_to_all | solution.py:239
  572.9 3.6 copy-start.18
  578.1 25.7 %copy-start.9 = (bf16[2048,256]{1,0:T(8,128)(2,1)S(1)}, bf16[2048,256]{1,0:T(8,128)(2,1)}, u32[]{:S(2)}) copy-start(bf16[2048,256]{1,0:T(8,128)(2,1)} %get-tuple-element.32.o_ref) | copy-start | bytes 3145732
  578.1 47.6 %collective-permute-start.22 = (bf16[1024,1024]{1,0:T(8,128)(2,1)}, bf16[1024,1024]{1,0:T(8,128)(2,1)}, u32[]{:S(2)}, u32[]{:S(2)}) collective-permute-start(bf16[1024,1024]{1,0:T(8,128)(2,1)} %pad_maximum_fusion.9), channel_id=1, source_target_pairs={{0,2},{2,0},{1,3},{3,1},{4,6},{6,4},{5,7},{7,5},{8,10},{10,8},{9,1... | collective-permute-start | bytes 6291464 | tf_op jit(solution)/shard_map/ppermute | solution.py:236
  585.5 49.2 %collective-permute-start.9 = (bf16[1024,1024]{1,0:T(8,128)(2,1)}, bf16[1024,1024]{1,0:T(8,128)(2,1)}, u32[]{:S(2)}, u32[]{:S(2)}) collective-permute-start(bf16[1024,1024]{1,0:T(8,128)(2,1)} %fusion.31), channel_id=1, source_target_pairs={{0,1},{1,0},{2,3},{3,2},{4,5},{5,4},{6,7},{7,6},{8,9},{9,8},{10,11... | collective-permute-start | bytes 6291464 | tf_op jit(solution)/shard_map/ppermute | solution.py:233
  599.8 29.8 %all-to-all-start.2 = ((bf16[8,64,1024]{2,1,0:T(8,128)(2,1)}), bf16[8,64,1024]{2,1,0:T(8,128)(2,1)S(1)}, u32[]{:S(2)}, u32[]{:S(2)}) async-start(bf16[8,64,1024]{2,1,0:T(8,128)(2,1)} %bitcast.121), calls=%async_computation.2 | async-start | bytes 2097152 | tf_op jit(solution)/shard_map/all_to_all | solution.py:239
  629.6 70.4 %all-to-all-start.4 = ((bf16[8,1024,128]{2,1,0:T(8,128)(2,1)}), bf16[8,1024,128]{2,1,0:T(8,128)(2,1)}, u32[]{:S(2)}, u32[]{:S(2)}) async-start(bf16[8,1024,128]{2,1,0:T(8,128)(2,1)} %bitcast_bitcast_fusion.1), calls=%async_computation.4 | async-start | bytes 4194304 | tf_op jit(solution)/shard_map/all_to_all | solution.py:239
  642.7 4.5 copy-start.49
  643.8 30.6 %collective-permute-start.10 = (bf16[512,1024]{1,0:T(8,128)(2,1)}, bf16[512,1024]{1,0:T(8,128)(2,1)}, u32[]{:S(2)}, u32[]{:S(2)}) collective-permute-start(bf16[512,1024]{1,0:T(8,128)(2,1)} %get-tuple-element.124), channel_id=1, source_target_pairs={{0,2},{2,0},{1,3},{3,1},{4,6},{6,4},{5,7},{7,5},{8,10},{10,8},{9,1... | collective-permute-start | bytes 3145736 | tf_op jit(solution)/shard_map/ppermute | solution.py:236
  644.1 1.2 collective-permute-start.17
  645.4 22.3 %collective-permute-start.18 = (f32[2,1024]{1,0:T(2,128)S(1)}, f32[2,1024]{1,0:T(2,128)S(1)}, u32[]{:S(2)}, u32[]{:S(2)}) collective-permute-start(f32[2,1024]{1,0:T(2,128)S(1)} %fusion.61), channel_id=1, source_target_pairs={{0,2},{2,0},{1,3},{3,1},{4,6},{6,4},{5,7},{7,5},{8,10},{10,8},{9,1... | collective-permute-start | bytes 24584 | tf_op jit(solution)/shard_map/ppermute | solution.py:236
  667.7 3.7 collective-permute-start.19
  671.4 6.3 collective-permute-start.20
  673.9 20.7 %collective-permute-start.16 = (bf16[8,64,1024]{2,1,0:T(8,128)(2,1)}, bf16[8,64,1024]{2,1,0:T(8,128)(2,1)S(1)}, u32[]{:S(2)}, u32[]{:S(2)}) collective-permute-start(bf16[8,64,1024]{2,1,0:T(8,128)(2,1)} %copy-done.21), channel_id=1, source_target_pairs={{0,2},{2,0},{1,3},{3,1},{4,6},{6,4},{5,7},{7,5},{8,10},{10,8},{9,1... | collective-permute-start | bytes 3145736 | tf_op jit(solution)/shard_map/ppermute | solution.py:236
  677.7 4.6 collective-permute-start.21
  696.2 8.8 %copy-start.1 = (bf16[16,1,64,1024]{3,2,1,0:T(8,128)(2,1)S(1)}, bf16[16,1,64,1024]{3,2,1,0:T(8,128)(2,1)}, u32[]{:S(2)}) copy-start(bf16[16,1,64,1024]{3,2,1,0:T(8,128)(2,1)} %param.17) | copy-start | bytes 6291460
  (19 other events, 47.2 us)

commit v3 on v2

--- a/solution.py
+++ b/solution.py
@@ -289,8 +289,8 @@
     gates = jnp.concatenate((w_gate, w_gate_far), 1)
     ups = jnp.concatenate((w_up, w_up_far), 1)
     downs = jnp.concatenate((w_down, w_down_far), 0)
-    gate_pre = dot(rows_ffn, gates, 1, 0)
-    up_proj = dot(rows_ffn, ups, 1, 0)
+    gate_pre = dot(rows_ffn, gates, 1, 0, LOW).astype(F32)
+    up_proj = dot(rows_ffn, ups, 1, 0, LOW).astype(F32)
     sigmoid = 1.0 / (1.0 + jnp.exp(-gate_pre))
     swish_gate = gate_pre * sigmoid
     product = (swish_gate * up_proj).astype(LOW)
@@ -303,7 +303,7 @@
         jnp.stack((result_far, result[:quarter])),
     )[:, None]
 
-    grad_result = jnp.concatenate((cot_near, cot_far), 0).astype(F32) * live_rows
+    grad_result = jnp.concatenate((cot_near, after(cot_far, rows_ffn)), 0).astype(F32) * live_rows
     grad_ffn = gather(grad_result.astype(LOW))
     grad_product = dot(grad_ffn, downs, 1, 1)
     grad_gate = (grad_product * up_proj * sigmoid * (1.0 + gate_pre * (1.0 - sigmoid))).astype(LOW)
@@ -314,8 +314,20 @@
     def over_chips(parts):
         far = swap_chip(jnp.concatenate([far.astype(LOW) for _, far in parts], 0))
         summed = jnp.concatenate([near for near, _ in parts], 0) + far.astype(F32)
-        spread = summed.astype(LOW).reshape(-1, groups, width // groups).transpose(1, 0, 2)
-        return jnp.sum(exchange(spread).astype(F32), 0)
+        rows = summed.shape[0]
+        held = summed.reshape(rows, groups, width // groups).transpose(1, 0, 2)
+        step = 1
+        while step < groups:
+            side = (group // step) % 2
+            pairs = held.reshape(-1, 2, rows, width // groups)
+            moved = lax.ppermute(
+                lax.dynamic_index_in_dim(pairs, 1 - side, 1, False).astype(LOW),
+                "dp",
+                [(i, i ^ step) for i in range(groups)],
+            )
+            held = lax.dynamic_index_in_dim(pairs, side, 1, False) + moved.astype(F32)
+            step *= 2
+        return held[0]
 
     def halves(value):
         return (value[:half], value[half:])

time: 715 us -> 744 us (1.041)
  waiting for transfers between devices: 219 us -> 272 us
  matrix products: 182 us -> 168 us
    ppermute x13, waiting for transfers between devices: 157 us -> 220 us  [swap_chip(): return lax.ppermute(value, 'tensor', [(0, 2), (2, 0), (1, 3), (3, 1)])]
    all_to_all x6 -> x3, waiting for transfers between devices: 57.7 us -> 0.01 us  [exchange(): return lax.all_to_all(value, 'dp', split_axis=0, concat_axis=0, tiled=True)]
    ppermute x0 -> x9, waiting for transfers between devices: none -> 36.3 us  [over_chips(): lax.ppermute(lax.dynamic_index_in_dim(pairs, 1 - side, 1, False).astype(L...]
    dot_general x28, matrix products: 182 us -> 168 us  [dot(): lax.dot_general(left, right, (((left_dim,), (right_dim,)), ((), ())), pre...]
    all_to_all x6 -> x3, starting transfers between devices: 28.4 us -> 15.9 us  [exchange(): return lax.all_to_all(value, 'dp', split_axis=0, concat_axis=0, tiled=True)]
    ppermute x3, waiting for transfers between devices: 3.37 us -> 15.4 us  [total_of(): lax.ppermute(value, 'dp', [(i, i ^ step) for i in range(groups)])]
    transpose x3 -> x0, other arithmetic: 11.8 us -> none  [over_chips(): summed.astype(LOW).reshape(-1, groups, width // groups).transpose(1, 0, 2)]
    ppermute x0 -> x9, starting transfers between devices: none -> 9.93 us  [over_chips(): lax.ppermute(lax.dynamic_index_in_dim(pairs, 1 - side, 1, False).astype(L...]
  transfers between devices with their start and end apart: 31 -> 37, of which waited for: 14 -> 17; matrix products, arithmetic and copies ran while one was open for 31% -> 23% of each run, Pallas kernels for 18% -> 18%
where the time goes in v3:
time: 744 us; the launch traced here: 734 us
  waiting for transfers between devices  272 us (37%)
  matrix products  168 us (23%)
  Pallas kernels  129 us (17%)
  local copies, waits for them, and re-layouts  45.8 us (6%)
  other arithmetic  42.7 us (6%)
  starting transfers between devices  42.3 us (6%)
  blocking collectives  29.9 us (4%)
    ppermute x13, waiting for transfers between devices, swap_chip(): return lax.ppermute(value, 'tensor', [(0, 2), (2, 0), (1, 3), (3, 1)])  220 us
    dot_general x28, matrix products, dot(): lax.dot_general(left, right, (((left_dim,), (right_dim,)), ((), ())), pre...  168 us
    pallas_call x2, Pallas kernels, attend_back(): pl.pallas_call(functools.partial(attend_back_kernel, block), grid_spec=pl...  72.3 us
    pallas_call x2, Pallas kernels, attend(): pl.pallas_call(attend_kernel, grid_spec=pltpu.PrefetchScalarGridSpec(num_...  56.4 us
    ppermute x9, waiting for transfers between devices, over_chips(): lax.ppermute(lax.dynamic_index_in_dim(pairs, 1 - side, 1, False).astype(L...  36.3 us
    all_to_all x1, blocking collectives, exchange(): return lax.all_to_all(value, 'dp', split_axis=0, concat_axis=0, tiled=True)  29.9 us
    unnamed x140, local copies, waits for them, and re-layouts  21.5 us
    all_to_all x3, starting transfers between devices, exchange(): return lax.all_to_all(value, 'dp', split_axis=0, concat_axis=0, tiled=True)  15.9 us
  transfers between devices with their start and end apart: 37, of which 17 were waited for; matrix products, arithmetic and copies ran while one was open for 23% of the time, Pallas kernels for 18%

profile of v3, /device:TPU:0, one launch (start us, length us, event | category | flops | bytes accessed | tf_op | source)
XLA Modules:
  0.0 734.0 jit_solution(13051199614321619573)
XLA Ops:
  0.7 2.0 sort.17
  4.6 7.3 all-to-all-start
  15.1 23.3 %collective-permute-done = bf16[8,64,1024]{2,1,0:T(8,128)(2,1)S(1)} collective-permute-done((bf16[8,64,1024]{2,1,0:T(8,128)(2,1)}, bf16[8,64,1024]{2,1,0:T(8,128)(2,1)S(1)}, u32[]{:S(2)}, u32[]{:S(2)}) %collective-permute-start) | collective-permute-done | bytes 1048608 | tf_op jit(solution)/shard_map/ppermute | solution.py:236
  38.4 29.9 %all_to_all.20 = bf16[8,64,1024]{2,1,0:T(8,128)(2,1)S(1)} all-to-all(bf16[8,64,1024]{2,1,0:T(8,128)(2,1)S(1)} %collective-permute-done), channel_id=1, replica_groups=mesh['dp'=8,'tensor'=4] {'dp'}, dimensions={0} | all-to-all | bytes 2097152 | tf_op jit(solution)/shard_map/all_to_all | solution.py:239
  68.8 1.9 fusion.12
  79.8 7.7 %fusion.82.q_ref.k_ref.v_ref = bf16[2048,768]{1,0:T(8,128)(2,1)} fusion(bf16[1024,768]{1,0:T(8,128)(2,1)} %constant_dynamic-update-slice_fusion, bf16[1024,1024]{1,0:T(8,128)(2,1)} %collective-permute-done.1, bf16[1024,1024]{1,0:T(8,128)(2,1)} %fusion.12), kind=kOutput, calls=%fused_computation.188 | convolution fusion | flops 3229614080 | bytes 8912896 | tf_op jit(solution)/shard_map/dot_general | solution.py:20
  87.5 23.4 %collective-permute-done.2 = bf16[1024,768]{1,0:T(8,128)(2,1)} collective-permute-done((bf16[1024,768]{1,0:T(8,128)(2,1)}, bf16[1024,768]{1,0:T(8,128)(2,1)}, u32[]{:S(2)}, u32[]{:S(2)}) %collective-permute-start.2) | collective-permute-done | bytes 1572896 | tf_op jit(solution)/shard_map/ppermute | solution.py:236
  110.9 7.8 %fusion.81.q_ref.k_ref.v_ref = bf16[2048,768]{1,0:T(8,128)(2,1)} fusion(bf16[1024,768]{1,0:T(8,128)(2,1)} %collective-permute-done.2, bf16[1024,1024]{1,0:T(8,128)(2,1)} %collective-permute-done.1, bf16[1024,1024]{1,0:T(8,128)(2,1)} %fusion.12), kind=kOutput, calls=%fused_computation.187 | convolution fusion | flops 3229614080 | bytes 8912896 | tf_op jit(solution)/shard_map/dot_general | solution.py:20
  118.7 28.0 %attend.2 = (bf16[2048,256]{1,0:T(8,128)(2,1)}, f32[2048,256]{1,0:T(8,128)}) custom-call(s32[5]{0:T(128)} %pad_add_fusion.info, bf16[2048,768]{1,0:T(8,128)(2,1)} %fusion.82.q_ref.k_ref.v_ref, bf16[2048,768]{1,0:T(8,128)(2,1)} %fusion.82.q_ref.k_ref.v_ref, bf16[2048,768]{1,0:T(8,128)(2,1)} %fusion.82.q_ref.k_ref.v_ref), custom_call_target="tpu_custom_call" | custom-call | tf_op jit(solution)/shard_map/attend/pallas_call | solution.py:92
  146.7 28.4 %attend.3 = (bf16[2048,256]{1,0:T(8,128)(2,1)}, f32[2048,256]{1,0:T(8,128)}) custom-call(s32[5]{0:T(128)} %pad_add_fusion.info, bf16[2048,768]{1,0:T(8,128)(2,1)} %fusion.81.q_ref.k_ref.v_ref, bf16[2048,768]{1,0:T(8,128)(2,1)} %fusion.81.q_ref.k_ref.v_ref, bf16[2048,768]{1,0:T(8,128)(2,1)} %fusion.81.q_ref.k_ref.v_ref), custom_call_target="tpu_custom_call" | custom-call | tf_op jit(solution)/shard_map/attend/pallas_call | solution.py:92
  189.1 2.0 collective-permute-start.7
  191.9 1.9 collective-permute-start.8
  196.8 80.2 %collective-permute-done.11 = bf16[512,1024]{1,0:T(8,128)(2,1)S(1)} collective-permute-done((bf16[512,1024]{1,0:T(8,128)(2,1)}, bf16[512,1024]{1,0:T(8,128)(2,1)S(1)}, u32[]{:S(2)}, u32[]{:S(2)}) %collective-permute-start.11) | collective-permute-done | bytes 1048608 | tf_op jit(solution)/shard_map/ppermute | solution.py:236
  277.5 2.1 constant_dynamic-update-slice_fusion.3
  279.6 2.5 constant_dynamic-update-slice_fusion.5
  282.2 24.9 %collective-permute-done.8 = bf16[704,1024]{1,0:T(8,128)(2,1)S(1)} collective-permute-done((bf16[704,1024]{1,0:T(8,128)(2,1)}, bf16[704,1024]{1,0:T(8,128)(2,1)S(1)}, u32[]{:S(2)}, u32[]{:S(2)}) %collective-permute-start.8) | collective-permute-done | bytes 1441824 | tf_op jit(solution)/shard_map/ppermute | solution.py:236
  308.8 10.8 %fusion.85 = bf16[2048,1408]{1,0:T(8,128)(2,1)} fusion(bf16[1024,1408]{0,1:T(8,128)(2,1)S(1)} %constant_dynamic-update-slice_fusion.5, bf16[1024,1024]{1,0:T(8,128)(2,1)} %collective-permute-done.5, bf16[1024,1024]{1,0:T(8,128)(2,1)} %multiply_convert_fusion.2), kind=kOutput, calls=%fused_computation.191 | convolution fusion | flops 5913968640 | bytes 12845056 | tf_op jit(solution)/shard_map/dot_general | solution.py:20
  319.6 11.2 %fusion.86 = bf16[2048,1408]{1,0:T(8,128)(2,1)} fusion(bf16[1024,1408]{0,1:T(8,128)(2,1)S(1)} %constant_dynamic-update-slice_fusion.3, bf16[1024,1024]{1,0:T(8,128)(2,1)} %collective-permute-done.5, bf16[1024,1024]{1,0:T(8,128)(2,1)} %multiply_convert_fusion.2), kind=kOutput, calls=%fused_computation.192 | convolution fusion | flops 5913968640 | bytes 12845056 | tf_op jit(solution)/shard_map/dot_general | solution.py:20
  330.8 19.1 %fusion.3 = (bf16[2048,1408]{1,0:T(8,128)(2,1)}, bf16[2048,1408]{1,0:T(8,128)(2,1)}, bf16[2048,1408]{1,0:T(8,128)(2,1)}) fusion(bf16[2048,1408]{1,0:T(8,128)(2,1)} %fusion.85, bf16[2048,1408]{1,0:T(8,128)(2,1)} %fusion.86, bf16[1408,1024]{1,0:T(8,128)(2,1)} %copy-done.30, bf16[1024,1024]{1,0:T(8,128)(2,1)} %collective-permute-done.12, ...), kind=kOutput, calls=%fused_computation.11 | convolution fusion | flops 5962989568 | bytes 35913728 | tf_op jit(solution)/shard_map/dot_general | solution.py:20
  350.0 8.3 %fusion.22 = f32[1024,1024]{1,0:T(8,128)} fusion(bf16[1024,1408]{0,1:T(8,128)(2,1)} %copy-done.33, bf16[2048,1408]{1,0:T(8,128)(2,1)} %get-tuple-element.119), kind=kOutput, calls=%fused_computation.62 | convolution fusion | flops 2952790016 | bytes 9961472 | tf_op jit(solution)/shard_map/dot_general | solution.py:20
  358.3 9.3 %fusion.83 = f32[1408,1024]{1,0:T(8,128)S(1)} fusion(bf16[2048,1408]{1,0:T(8,128)(2,1)S(1)} %copy-done.56, bf16[1024,1024]{1,0:T(8,128)(2,1)} %collective-permute-done.5, bf16[1024,1024]{1,0:T(8,128)(2,1)} %multiply_convert_fusion.2), kind=kOutput, calls=%fused_computation.189 | convolution fusion | flops 5913968640 | bytes 15728640 | tf_op jit(solution)/shard_map/dot_general | solution.py:20
  367.8 2.6 copy-done.10
  370.4 9.4 %fusion.84 = f32[1408,1024]{1,0:T(8,128)S(1)} fusion(bf16[2048,1408]{1,0:T(8,128)(2,1)S(1)} %bitcast.192, bf16[1024,1024]{1,0:T(8,128)(2,1)} %collective-permute-done.5, bf16[1024,1024]{1,0:T(8,128)(2,1)} %multiply_convert_fusion.2), kind=kOutput, calls=%fused_computation.190 | convolution fusion | flops 5913968640 | bytes 15728640 | tf_op jit(solution)/shard_map/dot_general | solution.py:20
  380.0 2.6 copy-done.11
  383.7 4.8 fusion.36
  388.5 8.0 %fusion.34 = f32[1408,1024]{1,0:T(8,128)S(1)} fusion(bf16[2048,1408]{1,0:T(8,128)(2,1)S(1)} %bitcast.194, bf16[1024,1024]{1,0:T(8,128)(2,1)} %collective-permute-done.12, bf16[1024,1024]{1,0:T(8,128)(2,1)S(1)} %copy-done.23), kind=kOutput, calls=%fused_computation.77 | convolution fusion | flops 5913968640 | bytes 15728640 | tf_op jit(solution)/shard_map/dot_general | solution.py:20
  397.1 4.7 add_convert_fusion.1
  404.4 5.2 fusion.28
  409.6 5.2 fusion.26
  414.9 16.3 %collective-permute-done.30 = bf16[704,1024]{1,0:T(8,128)(2,1)S(1)} collective-permute-done((bf16[704,1024]{1,0:T(8,128)(2,1)S(1)}, bf16[704,1024]{1,0:T(8,128)(2,1)S(1)}, u32[]{:S(2)}, u32[]{:S(2)}) %collective-permute-start.30) | collective-permute-done | bytes 1441824 | tf_op jit(solution)/shard_map/ppermute | solution.py:236
  433.2 2.4 multiply_reduce_fusion
  435.7 3.8 fusion.87
  439.6 6.9 collective-permute-done.31
  447.9 5.9 multiply_convert_fusion.1
  457.3 4.1 collective-permute-done.33
  462.1 30.9 %collective-permute-done.26 = bf16[1408,1024]{1,0:T(8,128)(2,1)S(1)} collective-permute-done((bf16[1408,1024]{1,0:T(8,128)(2,1)S(1)}, bf16[1408,1024]{1,0:T(8,128)(2,1)S(1)}, u32[]{:S(2)}, u32[]{:S(2)}) %collective-permute-start.26) | collective-permute-done | bytes 2883616 | tf_op jit(solution)/shard_map/ppermute | solution.py:236
  496.6 3.9 fusion.77.do_ref
  500.6 36.1 %attend_back.2 = (bf16[2048,256]{1,0:T(8,128)(2,1)}, bf16[2048,256]{1,0:T(8,128)(2,1)}, bf16[2048,256]{1,0:T(8,128)(2,1)}) custom-call(s32[5]{0:T(128)} %pad_add_fusion.info, bf16[2048,768]{1,0:T(8,128)(2,1)} %fusion.81.q_ref.k_ref.v_ref, bf16[2048,768]{1,0:T(8,128)(2,1)} %fusion.81.q_ref.k_ref.v_ref, bf16[2048,768]{1,0:T(8,128)(2,1)} %fusion.81.q_ref.k_ref.v_ref, ...), custom_call_target="tpu_custom_call" | custom-call | tf_op jit(solution)/shard_map/attend_back/pallas_call | solution.py:185
  539.4 5.1 fusion.78.do_ref
  544.5 6.8 fusion.80
  551.3 36.2 %attend_back.3 = (bf16[2048,256]{1,0:T(8,128)(2,1)}, bf16[2048,256]{1,0:T(8,128)(2,1)}, bf16[2048,256]{1,0:T(8,128)(2,1)}) custom-call(s32[5]{0:T(128)} %pad_add_fusion.info, bf16[2048,768]{1,0:T(8,128)(2,1)} %fusion.82.q_ref.k_ref.v_ref, bf16[2048,768]{1,0:T(8,128)(2,1)} %fusion.82.q_ref.k_ref.v_ref, bf16[2048,768]{1,0:T(8,128)(2,1)} %fusion.82.q_ref.k_ref.v_ref, ...), custom_call_target="tpu_custom_call" | custom-call | tf_op jit(solution)/shard_map/attend_back/pallas_call | solution.py:185
  590.3 3.2 fusion.44
  593.6 3.3 fusion.48
  596.9 3.0 convolution_convert_fusion
  602.6 3.2 add_convert_fusion
  605.9 3.9 fusion.76
  609.8 3.4 fusion.46
  613.2 7.5 %fusion.79 = f32[768,1024]{1,0:T(8,128)} fusion(bf16[2048,768]{1,0:T(8,128)(2,1)S(1)} %constant_dynamic-update-slice_fusion.12, bf16[1024,1024]{1,0:T(8,128)(2,1)} %collective-permute-done.1, bf16[1024,1024]{1,0:T(8,128)(2,1)} %fusion.12), kind=kOutput, calls=%fused_computation.185 | convolution fusion | flops 3229614080 | bytes 10485760 | tf_op jit(solution)/shard_map/dot_general | solution.py:20
  624.1 2.6 fusion.19
  626.7 2.0 fusion.16
  630.3 4.2 all-to-all-start.3
  634.5 11.2 %collective-permute-done.22 = bf16[1024,1024]{1,0:T(8,128)(2,1)} collective-permute-done((bf16[1024,1024]{1,0:T(8,128)(2,1)}, bf16[1024,1024]{1,0:T(8,128)(2,1)}, u32[]{:S(2)}, u32[]{:S(2)}) %collective-permute-start.22) | collective-permute-done | bytes 2097184 | tf_op jit(solution)/shard_map/ppermute | solution.py:236
  645.7 3.2 copy_bitcast_fusion.1
  653.0 2.5 collective-permute-done.18
  656.4 19.2 %collective-permute-done.23 = bf16[4,1024,128]{2,1,0:T(8,128)(2,1)S(1)} collective-permute-done((bf16[4,1024,128]{2,1,0:T(8,128)(2,1)S(1)}, bf16[4,1024,128]{2,1,0:T(8,128)(2,1)S(1)}, u32[]{:S(2)}, u32[]{:S(2)}) %collective-permute-start.23) | collective-permute-done | bytes 1048608 | tf_op jit(solution)/shard_map/ppermute | solution.py:323
  677.4 4.4 all-to-all-start.2
  681.8 4.0 maximum_select_fusion
  685.8 2.0 collective-permute-start.20
  688.8 14.8 %collective-permute-done.20 = f32[2,1024]{1,0:T(2,128)S(1)} collective-permute-done((f32[2,1024]{1,0:T(2,128)S(1)}, f32[2,1024]{1,0:T(2,128)S(1)}, u32[]{:S(2)}, u32[]{:S(2)}) %collective-permute-start.20) | collective-permute-done | bytes 8224 | tf_op jit(solution)/shard_map/ppermute | solution.py:371
  706.8 3.0 collective-permute-start.25
  711.8 5.1 collective-permute-done.25
  719.9 6.9 collective-permute-done.16
  726.9 3.2 maximum_select_fusion.1
  730.1 3.7 gather_fusion.2
  (268 shorter events, 76.5 us)
Async XLA Ops:
  4.6 33.7 %all-to-all-start = ((bf16[8,64,1024]{2,1,0:T(8,128)(2,1)}), bf16[8,64,1024]{2,1,0:T(8,128)(2,1)S(1)}, u32[]{:S(2)}, u32[]{:S(2)}) async-start(bf16[8,64,1024]{2,1,0:T(8,128)(2,1)} %gather_fusion), calls=%async_computation | async-start | bytes 2097152 | tf_op jit(solution)/shard_map/all_to_all | solution.py:239
  11.9 56.9 %copy-start.46 = (f32[1024]{0:T(1024)S(1)}, f32[1024]{0:T(1024)}, u32[]{:S(2)}) copy-start(f32[1024]{0:T(1024)} %param.20) | copy-start | bytes 12292
  13.5 24.8 %collective-permute-start = (bf16[8,64,1024]{2,1,0:T(8,128)(2,1)}, bf16[8,64,1024]{2,1,0:T(8,128)(2,1)S(1)}, u32[]{:S(2)}, u32[]{:S(2)}) collective-permute-start(bf16[8,64,1024]{2,1,0:T(8,128)(2,1)} %gather_fusion.1), channel_id=1, source_target_pairs={{0,2},{2,0},{1,3},{3,1},{4,6},{6,4},{5,7},{7,5},{8,10},{10,8},{9,1... | collective-permute-start | bytes 3145736 | tf_op jit(solution)/shard_map/ppermute | solution.py:236
  38.4 144.6 %copy-start.4 = (bf16[8,64,1024]{2,1,0:T(8,128)(2,1)}, bf16[8,64,1024]{2,1,0:T(8,128)(2,1)S(1)}, u32[]{:S(2)}) copy-start(bf16[8,64,1024]{2,1,0:T(8,128)(2,1)S(1)} %all-to-all-done) | copy-start | bytes 3145732
  68.2 114.8 %copy-start.6 = (bf16[8,64,1024]{2,1,0:T(8,128)(2,1)}, bf16[8,64,1024]{2,1,0:T(8,128)(2,1)S(1)}, u32[]{:S(2)}) copy-start(bf16[8,64,1024]{2,1,0:T(8,128)(2,1)S(1)} %all_to_all.20) | copy-start | bytes 3145732
  68.8 127.4 %copy-start.42 = (f32[1024]{0:T(1024)}, f32[1024]{0:T(1024)S(1)}, u32[]{:S(2)}) copy-start(f32[1024]{0:T(1024)S(1)} %rsqrt.26) | copy-start | bytes 12292
  68.8 8.6 %copy-start.54 = (s32[16]{0:T(128)S(1)}, s32[16]{0:T(128)}, u32[]{:S(2)}) copy-start(s32[16]{0:T(128)} %param.18) | copy-start | bytes 196
  70.7 9.1 %collective-permute-start.1 = (bf16[1024,1024]{1,0:T(8,128)(2,1)}, bf16[1024,1024]{1,0:T(8,128)(2,1)}, u32[]{:S(2)}, u32[]{:S(2)}) collective-permute-start(bf16[1024,1024]{1,0:T(8,128)(2,1)} %fusion.12), channel_id=1, source_target_pairs={{0,1},{1,0},{2,3},{3,2},{4,5},{5,4},{6,7},{7,6},{8,9},{9,8},{10,11... | collective-permute-start | bytes 6291464 | tf_op jit(solution)/shard_map/ppermute | solution.py:233
  73.3 37.6 %collective-permute-start.2 = (bf16[1024,768]{1,0:T(8,128)(2,1)}, bf16[1024,768]{1,0:T(8,128)(2,1)}, u32[]{:S(2)}, u32[]{:S(2)}) collective-permute-start(bf16[1024,768]{1,0:T(8,128)(2,1)} %constant_dynamic-update-slice_fusion), channel_id=1, source_target_pairs={{0,2},{2,0},{1,3},{3,1},{4,6},{6,4},{5,7},{7,5},{8,10},{10,8},{9,1... | collective-permute-start | bytes 4718600 | tf_op jit(solution)/shard_map/ppermute | solution.py:236
  79.2 97.7 %collective-permute-start.3 = (bf16[256,1024]{1,0:T(8,128)(2,1)}, bf16[256,1024]{1,0:T(8,128)(2,1)}, u32[]{:S(2)}, u32[]{:S(2)}) collective-permute-start(bf16[256,1024]{1,0:T(8,128)(2,1)} %param.24), channel_id=1, source_target_pairs={{0,2},{2,0},{1,3},{3,1},{4,6},{6,4},{5,7},{7,5},{8,10},{10,8},{9,1... | collective-permute-start | bytes 1572872 | tf_op jit(solution)/shard_map/ppermute | solution.py:236
  146.7 28.4 %copy-start.14 = (bf16[2048,256]{1,0:T(8,128)(2,1)S(1)}, bf16[2048,256]{1,0:T(8,128)(2,1)}, u32[]{:S(2)}) copy-start(bf16[2048,256]{1,0:T(8,128)(2,1)} %get-tuple-element.33.o_ref) | copy-start | bytes 3145732
  178.8 4.2 collective-permute-start.4
  187.0 121.8 %collective-permute-start.5 = (bf16[1024,1024]{1,0:T(8,128)(2,1)}, bf16[1024,1024]{1,0:T(8,128)(2,1)}, u32[]{:S(2)}, u32[]{:S(2)}) collective-permute-start(bf16[1024,1024]{1,0:T(8,128)(2,1)} %multiply_convert_fusion.2), channel_id=1, source_target_pairs={{0,1},{1,0},{2,3},{3,2},{4,5},{5,4},{6,7},{7,6},{8,9},{9,8},{10,11... | collective-permute-start | bytes 6291464 | tf_op jit(solution)/shard_map/ppermute | solution.py:233
  189.1 87.8 %copy-start.12 = (bf16[512,1024]{1,0:T(8,128)(2,1)}, bf16[512,1024]{1,0:T(8,128)(2,1)S(1)}, u32[]{:S(2)}) copy-start(bf16[512,1024]{1,0:T(8,128)(2,1)S(1)} %get-tuple-element.123) | copy-start | bytes 3145732
  189.1 88.3 %collective-permute-start.6 = (bf16[1024,704]{0,1:T(8,128)(2,1)S(1)}, bf16[1024,704]{0,1:T(8,128)(2,1)}, u32[]{:S(2)}, u32[]{:S(2)}) collective-permute-start(bf16[1024,704]{0,1:T(8,128)(2,1)S(1)} %copy-done.26), channel_id=1, source_target_pairs={{0,2},{2,0},{1,3},{3,1},{4,6},{6,4},{5,7},{7,5},{8,10},{10,8},{9,1... | collective-permute-start | bytes 4325384 | tf_op jit(solution)/shard_map/ppermute | solution.py:236
  189.1 90.5 %collective-permute-start.7 = (bf16[1024,704]{0,1:T(8,128)(2,1)}, bf16[1024,704]{0,1:T(8,128)(2,1)}, u32[]{:S(2)}, u32[]{:S(2)}) collective-permute-start(bf16[1024,704]{0,1:T(8,128)(2,1)} %param.27), channel_id=1, source_target_pairs={{0,2},{2,0},{1,3},{3,1},{4,6},{6,4},{5,7},{7,5},{8,10},{10,8},{9,1... | collective-permute-start | bytes 4325384 | tf_op jit(solution)/shard_map/ppermute | solution.py:236
  191.2 85.8 %collective-permute-start.11 = (bf16[512,1024]{1,0:T(8,128)(2,1)}, bf16[512,1024]{1,0:T(8,128)(2,1)S(1)}, u32[]{:S(2)}, u32[]{:S(2)}) collective-permute-start(bf16[512,1024]{1,0:T(8,128)(2,1)} %get-tuple-element.40), channel_id=1, source_target_pairs={{0,2},{2,0},{1,3},{3,1},{4,6},{6,4},{5,7},{7,5},{8,10},{10,8},{9,1... | collective-permute-start | bytes 3145736 | tf_op jit(solution)/shard_map/ppermute | solution.py:236
  191.9 115.1 %collective-permute-start.8 = (bf16[704,1024]{1,0:T(8,128)(2,1)}, bf16[704,1024]{1,0:T(8,128)(2,1)S(1)}, u32[]{:S(2)}, u32[]{:S(2)}) collective-permute-start(bf16[704,1024]{1,0:T(8,128)(2,1)} %param.28), channel_id=1, source_target_pairs={{0,2},{2,0},{1,3},{3,1},{4,6},{6,4},{5,7},{7,5},{8,10},{10,8},{9,1... | collective-permute-start | bytes 4325384 | tf_op jit(solution)/shard_map/ppermute | solution.py:236
  194.5 82.5 %copy-start.48 = (f32[1024]{0:T(1024)}, f32[1024]{0:T(1024)S(1)}, u32[]{:S(2)}) copy-start(f32[1024]{0:T(1024)S(1)} %fusion.67) | copy-start | bytes 12292
  277.4 29.8 %copy-start.22 = (bf16[1024,1024]{1,0:T(8,128)(2,1)}, bf16[1024,1024]{1,0:T(8,128)(2,1)S(1)}, u32[]{:S(2)}) copy-start(bf16[1024,1024]{1,0:T(8,128)(2,1)S(1)} %fusion.20) | copy-start | bytes 6291460
  277.4 53.4 %collective-permute-start.12 = (bf16[1024,1024]{1,0:T(8,128)(2,1)S(1)}, bf16[1024,1024]{1,0:T(8,128)(2,1)}, u32[]{:S(2)}, u32[]{:S(2)}) collective-permute-start(bf16[1024,1024]{1,0:T(8,128)(2,1)S(1)} %fusion.20), channel_id=1, source_target_pairs={{0,1},{1,0},{2,3},{3,2},{4,5},{5,4},{6,7},{7,6},{8,9},{9,8},{10,11... | collective-permute-start | bytes 6291464 | tf_op jit(solution)/shard_map/ppermute | solution.py:233
  279.6 40.0 %copy-start.35 = (bf16[1024,1408]{0,1:T(8,128)(2,1)}, bf16[1024,1408]{0,1:T(8,128)(2,1)S(1)}, u32[]{:S(2)}) copy-start(bf16[1024,1408]{0,1:T(8,128)(2,1)S(1)} %constant_dynamic-update-slice_fusion.3) | copy-start | bytes 8650756
  282.2 37.4 %copy-start.33 = (bf16[1024,1408]{0,1:T(8,128)(2,1)}, bf16[1024,1408]{0,1:T(8,128)(2,1)S(1)}, u32[]{:S(2)}) copy-start(bf16[1024,1408]{0,1:T(8,128)(2,1)S(1)} %constant_dynamic-update-slice_fusion.5) | copy-start | bytes 8650756
  319.6 11.2 %copy-start.23 = (bf16[1024,1024]{1,0:T(8,128)(2,1)S(1)}, bf16[1024,1024]{1,0:T(8,128)(2,1)}, u32[]{:S(2)}) copy-start(bf16[1024,1024]{1,0:T(8,128)(2,1)} %copy-done.22) | copy-start | bytes 6291460
  350.0 8.3 %copy-start.56 = (bf16[2048,1408]{1,0:T(8,128)(2,1)S(1)}, bf16[2048,1408]{1,0:T(8,128)(2,1)}, u32[]{:S(2)}) copy-start(bf16[2048,1408]{1,0:T(8,128)(2,1)} %get-tuple-element.119) | copy-start | bytes 17301508
  350.0 20.4 %slice-start.4 = ((s8[5767168]{0:T(1024)(128)(4,1)}), s8[4194304]{0:T(1024)(128)(4,1)S(1)}, s32[]{:S(2)}) async-start(s8[5767168]{0:T(1024)(128)(4,1)} %bitcast.191), calls=%async_computation.8 | async-start | bytes 8388608
  358.3 12.1 %slice-start.5 = ((s8[5767168]{0:T(1024)(128)(4,1)}), s8[1572864]{0:T(1024)(128)(4,1)S(1)}, s32[]{:S(2)}) async-start(s8[5767168]{0:T(1024)(128)(4,1)} %bitcast.191), calls=%async_computation.9 | async-start | bytes 3145728
  367.8 14.8 %slice-start.6 = ((s8[5767168]{0:T(1024)(128)(4,1)}), s8[4194304]{0:T(1024)(128)(4,1)S(1)}, s32[]{:S(2)}) async-start(s8[5767168]{0:T(1024)(128)(4,1)} %bitcast.193), calls=%async_computation.10 | async-start | bytes 8388608
  370.4 12.2 %slice-start.7 = ((s8[5767168]{0:T(1024)(128)(4,1)}), s8[1572864]{0:T(1024)(128)(4,1)S(1)}, s32[]{:S(2)}) async-start(s8[5767168]{0:T(1024)(128)(4,1)} %bitcast.193), calls=%async_computation.11 | async-start | bytes 3145728
  388.4 8.6 %copy-start.36 = (bf16[1024,1408]{0,1:T(8,128)(2,1)S(1)}, bf16[1024,1408]{0,1:T(8,128)(2,1)}, u32[]{:S(2)}) copy-start(bf16[1024,1408]{0,1:T(8,128)(2,1)} %copy-done.35) | copy-start | bytes 8650756
  388.4 8.6 %copy-start.57 = (f32[1024,1024]{1,0:T(8,128)S(1)}, f32[1024,1024]{1,0:T(8,128)}, u32[]{:S(2)}) copy-start(f32[1024,1024]{1,0:T(8,128)} %fusion.22) | copy-start | bytes 12582916
  396.7 34.5 %collective-permute-start.30 = (bf16[704,1024]{1,0:T(8,128)(2,1)S(1)}, bf16[704,1024]{1,0:T(8,128)(2,1)S(1)}, u32[]{:S(2)}, u32[]{:S(2)}) collective-permute-start(bf16[704,1024]{1,0:T(8,128)(2,1)S(1)} %slice.253), channel_id=1, source_target_pairs={{0,2},{2,0},{1,3},{3,1},{4,6},{6,4},{5,7},{7,5},{8,10},{10,8},{9,1... | collective-permute-start | bytes 4325384 | tf_op jit(solution)/shard_map/ppermute | solution.py:236
  397.1 50.8 %collective-permute-start.9 = (bf16[1024,1024]{1,0:T(8,128)(2,1)}, bf16[1024,1024]{1,0:T(8,128)(2,1)}, u32[]{:S(2)}, u32[]{:S(2)}) collective-permute-start(bf16[1024,1024]{1,0:T(8,128)(2,1)} %fusion.36), channel_id=1, source_target_pairs={{0,1},{1,0},{2,3},{3,2},{4,5},{5,4},{6,7},{7,6},{8,9},{9,8},{10,11... | collective-permute-start | bytes 6291464 | tf_op jit(solution)/shard_map/ppermute | solution.py:233
  401.8 31.4 %collective-permute-start.13 = (bf16[1024,1024]{1,0:T(8,128)(2,1)}, bf16[1024,1024]{1,0:T(8,128)(2,1)S(1)}, u32[]{:S(2)}, u32[]{:S(2)}) collective-permute-start(bf16[1024,1024]{1,0:T(8,128)(2,1)} %add_convert_fusion.1), channel_id=1, source_target_pairs={{0,1},{1,0},{2,3},{3,2},{4,5},{5,4},{6,7},{7,6},{8,9},{9,8},{10,11... | collective-permute-start | bytes 6291464 | tf_op jit(solution)/shard_map/ppermute | solution.py:233
  402.6 90.5 %collective-permute-start.26 = (bf16[1408,1024]{1,0:T(8,128)(2,1)S(1)}, bf16[1408,1024]{1,0:T(8,128)(2,1)S(1)}, u32[]{:S(2)}, u32[]{:S(2)}) collective-permute-start(bf16[1408,1024]{1,0:T(8,128)(2,1)S(1)} %pad_maximum_fusion.4), channel_id=1, source_target_pairs={{0,2},{2,0},{1,3},{3,1},{4,6},{6,4},{5,7},{7,5},{8,10},{10,8},{9,1... | collective-permute-start | bytes 8650760 | tf_op jit(solution)/shard_map/ppermute | solution.py:236
  414.9 18.3 %copy-start.3 = (f32[1024,1024]{1,0:T(8,128)S(1)}, f32[1024,1024]{1,0:T(8,128)}, u32[]{:S(2)}) copy-start(f32[1024,1024]{1,0:T(8,128)} %copy-done.2) | copy-start | bytes 12582916
  414.9 18.3 %copy-start.45 = (f32[1024]{0:T(1024)S(1)}, f32[1024]{0:T(1024)}, u32[]{:S(2)}) copy-start(f32[1024]{0:T(1024)} %copy-done.44) | copy-start | bytes 12292
  414.9 18.3 %copy-start.51 = (f32[1024]{0:T(1024)S(1)}, f32[1024]{0:T(1024)}, u32[]{:S(2)}) copy-start(f32[1024]{0:T(1024)} %param.25) | copy-start | bytes 12292
  431.7 14.8 %collective-permute-start.31 = (bf16[4,704,128]{2,1,0:T(8,128)(2,1)S(1)}, bf16[4,704,128]{2,1,0:T(8,128)(2,1)S(1)}, u32[]{:S(2)}, u32[]{:S(2)}) collective-permute-start(bf16[4,704,128]{2,1,0:T(8,128)(2,1)S(1)} %fusion.53), channel_id=1, source_target_pairs={{0,4},{4,0},{8,12},{12,8},{16,20},{20,16},{24,28},{28,24},{1,5},{5... | collective-permute-start | bytes 2162696 | tf_op jit(solution)/shard_map/ppermute | solution.py:323
  439.6 8.3 %copy-start.32 = (bf16[1408,1024]{1,0:T(8,128)(2,1)S(1)}, bf16[1408,1024]{1,0:T(8,128)(2,1)}, u32[]{:S(2)}) copy-start(bf16[1408,1024]{1,0:T(8,128)(2,1)} %copy-done.30) | copy-start | bytes 8650756
  439.6 57.0 %collective-permute-start.14 = (bf16[1024,1024]{1,0:T(8,128)(2,1)S(1)}, bf16[1024,1024]{1,0:T(8,128)(2,1)}, u32[]{:S(2)}, u32[]{:S(2)}) collective-permute-start(bf16[1024,1024]{1,0:T(8,128)(2,1)S(1)} %get-tuple-element.113), channel_id=1, source_target_pairs={{0,1},{1,0},{2,3},{3,2},{4,5},{5,4},{6,7},{7,6},{8,9},{9,8},{10,11... | collective-permute-start | bytes 6291464 | tf_op jit(solution)/shard_map/ppermute | solution.py:233
  446.7 8.1 %collective-permute-start.32 = (bf16[2,704,128]{2,1,0:T(8,128)(2,1)S(1)}, bf16[2,704,128]{2,1,0:T(8,128)(2,1)S(1)}, u32[]{:S(2)}, u32[]{:S(2)}) collective-permute-start(bf16[2,704,128]{2,1,0:T(8,128)(2,1)S(1)} %fusion.62), channel_id=1, source_target_pairs={{0,8},{4,12},{8,0},{12,4},{16,24},{20,28},{24,16},{28,20},{1,9},{5... | collective-permute-start | bytes 1081352 | tf_op jit(solution)/shard_map/ppermute | solution.py:323
  454.8 38.3 %slice-start.3 = ((f32[1408,1024]{1,0:T(8,128)}), f32[704,1024]{1,0:T(8,128)S(1)}, s32[]{:S(2)}) async-start(f32[1408,1024]{1,0:T(8,128)} %copy-done.11), calls=%async_computation.7 | async-start | bytes 5767168 | tf_op jit(solution)/shard_map/slice | solution.py:333
  454.9 38.2 %slice-start.2 = ((f32[1408,1024]{1,0:T(8,128)}), f32[704,1024]{1,0:T(8,128)S(1)}, s32[]{:S(2)}) async-start(f32[1408,1024]{1,0:T(8,128)} %copy-done.10), calls=%async_computation.6 | async-start | bytes 5767168 | tf_op jit(solution)/shard_map/slice | solution.py:333
  454.9 6.5 collective-permute-start.33
  456.6 225.2 %collective-permute-start.10 = (bf16[512,1024]{1,0:T(8,128)(2,1)}, bf16[512,1024]{1,0:T(8,128)(2,1)}, u32[]{:S(2)}, u32[]{:S(2)}) collective-permute-start(bf16[512,1024]{1,0:T(8,128)(2,1)} %get-tuple-element.126), channel_id=1, source_target_pairs={{0,2},{2,0},{1,3},{3,1},{4,6},{6,4},{5,7},{7,5},{8,10},{10,8},{9,1... | collective-permute-start | bytes 3145736 | tf_op jit(solution)/shard_map/ppermute | solution.py:236
  495.2 125.5 %collective-permute-start.27 = (bf16[4,1408,128]{2,1,0:T(8,128)(2,1)}, bf16[4,1408,128]{2,1,0:T(8,128)(2,1)}, u32[]{:S(2)}, u32[]{:S(2)}) collective-permute-start(bf16[4,1408,128]{2,1,0:T(8,128)(2,1)} %fusion.50), channel_id=1, source_target_pairs={{0,4},{4,0},{8,12},{12,8},{16,20},{20,16},{24,28},{28,24},{1,5},{5... | collective-permute-start | bytes 4325384 | tf_op jit(solution)/shard_map/ppermute | solution.py:323
  601.4 44.3 %collective-permute-start.22 = (bf16[1024,1024]{1,0:T(8,128)(2,1)}, bf16[1024,1024]{1,0:T(8,128)(2,1)}, u32[]{:S(2)}, u32[]{:S(2)}) collective-permute-start(bf16[1024,1024]{1,0:T(8,128)(2,1)} %pad_maximum_fusion.9), channel_id=1, source_target_pairs={{0,2},{2,0},{1,3},{3,1},{4,6},{6,4},{5,7},{7,5},{8,10},{10,8},{9,1... | collective-permute-start | bytes 6291464 | tf_op jit(solution)/shard_map/ppermute | solution.py:236
  605.8 18.3 %collective-permute-start.15 = (bf16[1024,1024]{1,0:T(8,128)(2,1)S(1)}, bf16[1024,1024]{1,0:T(8,128)(2,1)S(1)}, u32[]{:S(2)}, u32[]{:S(2)}) collective-permute-start(bf16[1024,1024]{1,0:T(8,128)(2,1)S(1)} %add_convert_fusion), channel_id=1, source_target_pairs={{0,1},{1,0},{2,3},{3,2},{4,5},{5,4},{6,7},{7,6},{8,9},{9,8},{10,11... | collective-permute-start | bytes 6291464 | tf_op jit(solution)/shard_map/ppermute | solution.py:233
  609.8 10.9 %slice-start = ((s8[5767168]{0:T(1024)(128)(4,1)}), s8[4194304]{0:T(1024)(128)(4,1)S(1)}, s32[]{:S(2)}) async-start(s8[5767168]{0:T(1024)(128)(4,1)} %bitcast.164), calls=%async_computation.4 | async-start | bytes 8388608
  623.4 27.1 %collective-permute-start.28 = (bf16[2,1408,128]{2,1,0:T(8,128)(2,1)}, bf16[2,1408,128]{2,1,0:T(8,128)(2,1)}, u32[]{:S(2)}, u32[]{:S(2)}) collective-permute-start(bf16[2,1408,128]{2,1,0:T(8,128)(2,1)} %fusion.52), channel_id=1, source_target_pairs={{0,8},{4,12},{8,0},{12,4},{16,24},{20,28},{24,16},{28,20},{1,9},{5... | collective-permute-start | bytes 2162696 | tf_op jit(solution)/shard_map/ppermute | solution.py:323
  630.3 47.1 %all-to-all-start.3 = ((bf16[8,64,1024]{2,1,0:T(8,128)(2,1)}), bf16[8,64,1024]{2,1,0:T(8,128)(2,1)}, u32[]{:S(2)}, u32[]{:S(2)}) async-start(bf16[8,64,1024]{2,1,0:T(8,128)(2,1)} %bitcast.179), calls=%async_computation.3 | async-start | bytes 2097152 | tf_op jit(solution)/shard_map/all_to_all | solution.py:239
  649.1 26.4 %collective-permute-start.23 = (bf16[4,1024,128]{2,1,0:T(8,128)(2,1)S(1)}, bf16[4,1024,128]{2,1,0:T(8,128)(2,1)S(1)}, u32[]{:S(2)}, u32[]{:S(2)}) collective-permute-start(bf16[4,1024,128]{2,1,0:T(8,128)(2,1)S(1)} %fusion.51), channel_id=1, source_target_pairs={{0,4},{4,0},{8,12},{12,8},{16,20},{20,16},{24,28},{28,24},{1,5},{5... | collective-permute-start | bytes 3145736 | tf_op jit(solution)/shard_map/ppermute | solution.py:323
  650.4 1.3 collective-permute-start.17
  651.8 3.7 collective-permute-start.18
  653.0 34.8 %collective-permute-start.29 = (bf16[1,1408,128]{2,1,0:T(8,128)(2,1)}, bf16[1,1408,128]{2,1,0:T(8,128)(2,1)}, u32[]{:S(2)}, u32[]{:S(2)}) collective-permute-start(bf16[1,1408,128]{2,1,0:T(8,128)(2,1)} %dynamic-slice_convert_fusion.6), channel_id=1, source_target_pairs={{0,16},{4,20},{8,24},{12,28},{16,0},{20,4},{24,8},{28,12},{1,17},{... | collective-permute-start | bytes 1081352 | tf_op jit(solution)/shard_map/ppermute | solution.py:323
  655.5 30.3 %collective-permute-start.19 = (f32[2,1024]{1,0:T(2,128)S(1)}, f32[2,1024]{1,0:T(2,128)S(1)}, u32[]{:S(2)}, u32[]{:S(2)}) collective-permute-start(f32[2,1024]{1,0:T(2,128)S(1)} %fusion.118), channel_id=1, source_target_pairs={{0,4},{4,0},{8,12},{12,8},{16,20},{20,16},{24,28},{28,24},{1,5},{5... | collective-permute-start | bytes 24584 | tf_op jit(solution)/shard_map/ppermute | solution.py:371
  676.6 27.8 %collective-permute-start.24 = (bf16[2,1024,128]{2,1,0:T(8,128)(2,1)}, bf16[2,1024,128]{2,1,0:T(8,128)(2,1)}, u32[]{:S(2)}, u32[]{:S(2)}) collective-permute-start(bf16[2,1024,128]{2,1,0:T(8,128)(2,1)} %fusion.54), channel_id=1, source_target_pairs={{0,8},{4,12},{8,0},{12,4},{16,24},{20,28},{24,16},{28,20},{1,9},{5... | collective-permute-start | bytes 1572872 | tf_op jit(solution)/shard_map/ppermute | solution.py:323
  677.4 10.4 %copy-start.19 = (f32[2,1408,128]{2,1,0:T(8,128)S(1)}, f32[2,1408,128]{2,1,0:T(8,128)}, u32[]{:S(2)}) copy-start(f32[2,1408,128]{2,1,0:T(8,128)} %copy-done.18) | copy-start | bytes 4325380
  677.4 42.6 %all-to-all-start.2 = ((bf16[8,64,1024]{2,1,0:T(8,128)(2,1)}), bf16[8,64,1024]{2,1,0:T(8,128)(2,1)}, u32[]{:S(2)}, u32[]{:S(2)}) async-start(bf16[8,64,1024]{2,1,0:T(8,128)(2,1)} %bitcast.178), calls=%async_computation.2 | async-start | bytes 2097152 | tf_op jit(solution)/shard_map/all_to_all | solution.py:239
  685.8 17.8 %collective-permute-start.20 = (f32[2,1024]{1,0:T(2,128)S(1)}, f32[2,1024]{1,0:T(2,128)S(1)}, u32[]{:S(2)}, u32[]{:S(2)}) collective-permute-start(f32[2,1024]{1,0:T(2,128)S(1)} %add.283), channel_id=1, source_target_pairs={{0,8},{4,12},{8,0},{12,4},{16,24},{20,28},{24,16},{28,20},{1,9},{5... | collective-permute-start | bytes 24584 | tf_op jit(solution)/shard_map/ppermute | solution.py:371
  703.7 7.5 %collective-permute-start.21 = (f32[2,1024]{1,0:T(2,128)S(1)}, f32[2,1024]{1,0:T(2,128)S(1)}, u32[]{:S(2)}, u32[]{:S(2)}) collective-permute-start(f32[2,1024]{1,0:T(2,128)S(1)} %add.284), channel_id=1, source_target_pairs={{0,16},{4,20},{8,24},{12,28},{16,0},{20,4},{24,8},{28,12},{1,17},{... | collective-permute-start | bytes 24584 | tf_op jit(solution)/shard_map/ppermute | solution.py:371
  705.5 21.3 %collective-permute-start.16 = (bf16[8,64,1024]{2,1,0:T(8,128)(2,1)}, bf16[8,64,1024]{2,1,0:T(8,128)(2,1)S(1)}, u32[]{:S(2)}, u32[]{:S(2)}) collective-permute-start(bf16[8,64,1024]{2,1,0:T(8,128)(2,1)} %all-to-all-done.3), channel_id=1, source_target_pairs={{0,2},{2,0},{1,3},{3,1},{4,6},{6,4},{5,7},{7,5},{8,10},{10,8},{9,1... | collective-permute-start | bytes 3145736 | tf_op jit(solution)/shard_map/ppermute | solution.py:236
  706.8 10.1 %collective-permute-start.25 = (bf16[1,1024,128]{2,1,0:T(8,128)(2,1)S(1)}, bf16[1,1024,128]{2,1,0:T(8,128)(2,1)S(1)}, u32[]{:S(2)}, u32[]{:S(2)}) collective-permute-start(bf16[1,1024,128]{2,1,0:T(8,128)(2,1)S(1)} %dynamic-slice_convert_fusion.7), channel_id=1, source_target_pairs={{0,16},{4,20},{8,24},{12,28},{16,0},{20,4},{24,8},{28,12},{1,17},{... | collective-permute-start | bytes 786440 | tf_op jit(solution)/shard_map/ppermute | solution.py:323
  (39 other events, 141.9 us)

commit v4 on v3

--- a/solution.py
+++ b/solution.py
@@ -249,13 +249,13 @@
     inputs = jnp.stack((arrived_near, arrived_far)).reshape(2 * quarter, width).astype(F32)
 
     w_qkv = jnp.concatenate((w_query, w_key, w_value), 1)
-    w_qkv_far = swap_chip(after(w_qkv, given))
-    w_out_far = swap_chip(after(w_out, given))
-    w_gate_far = swap_chip(after(w_gate, arrived_far))
-    w_up_far = swap_chip(after(w_up, arrived_far))
-    w_down_far = swap_chip(after(w_down, arrived_far))
+    w_qkv_far = swap_chip(w_qkv)
+    w_out_far = swap_chip(w_out)
+    w_gate_far = swap_chip(w_gate)
+    w_up_far = swap_chip(w_up)
+    w_down_far = swap_chip(w_down)
     cot_near = jnp.take(cotangent[:, 0], chip, axis=0)
-    cot_far = swap_chip(after(jnp.take(cotangent[:, 0], 1 - chip, axis=0), arrived_far))
+    cot_far = swap_chip(jnp.take(cotangent[:, 0], 1 - chip, axis=0))
 
     numbers = jnp.arange(4)
     slots = 2 * (numbers % 2 != core) + (numbers // 2 != chip)
@@ -269,10 +269,12 @@
     own_rows = 2 * quarter
 
     def gather(value):
-        return jnp.concatenate((value, swap_core(value)), 0)
+        other = swap_core(value)
+        return jnp.concatenate((value, other), 0)
 
     def scatter(make):
-        far = swap_core(make(slice(own_rows, None)).astype(LOW))
+        far = make(slice(own_rows, None)).astype(LOW)
+        far = swap_core(far)
         return make(slice(0, own_rows)) + far.astype(F32)
 
     normed_attn, factor_attn = norm_rows(inputs, attn_gain)
@@ -281,7 +283,7 @@
     mixed_near, total_near = attend(info, qkv[0], quarter)
     mixed_far, total_far = attend(info, qkv[1], quarter)
     attention = scatter(
-        lambda part: dot(mixed_near[part], w_out, 1, 0) + dot(mixed_far[part], w_out_far, 1, 0)
+        lambda part: dot(mixed_near[part], w_out, 1, 0) + dot(mixed_far[part], w_out_far, 1, 0),
     )
     hidden = inputs + attention
     normed_ffn, factor_ffn = norm_rows(hidden, ffn_gain)
@@ -303,7 +305,7 @@
         jnp.stack((result_far, result[:quarter])),
     )[:, None]
 
-    grad_result = jnp.concatenate((cot_near, after(cot_far, rows_ffn)), 0).astype(F32) * live_rows
+    grad_result = jnp.concatenate((cot_near, cot_far), 0).astype(F32) * live_rows
     grad_ffn = gather(grad_result.astype(LOW))
     grad_product = dot(grad_ffn, downs, 1, 1)
     grad_gate = (grad_product * up_proj * sigmoid * (1.0 + gate_pre * (1.0 - sigmoid))).astype(LOW)
@@ -336,7 +338,7 @@
     up_halves = halves(dot(grad_up, rows_ffn, 0, 0))
     gate_up_shards = over_chips([halves(dot(grad_gate, rows_ffn, 0, 0)), up_halves])
     grad_normed_ffn = scatter(
-        lambda part: dot(grad_gate[part], gates, 1, 1) + dot(grad_up[part], ups, 1, 1)
+        lambda part: dot(grad_gate[part], gates, 1, 1) + dot(grad_up[part], ups, 1, 1),
     )
     grad_hidden, gain_ffn_part = norm_back(hidden, factor_ffn, ffn_gain, grad_normed_ffn)
     grad_hidden = grad_hidden + grad_result
@@ -350,7 +352,7 @@
     grad_near = attend_back(info, qkv[0], back_near, mixed_near, total_near, quarter)
     grad_near = jnp.concatenate(grad_near, 1)
     grad_normed_attn = scatter(
-        lambda part: dot(grad_near[part], w_qkv, 1, 1) + dot(grad_far[part], w_qkv_far, 1, 1)
+        lambda part: dot(grad_near[part], w_qkv, 1, 1) + dot(grad_far[part], w_qkv_far, 1, 1),
     )
     qkv_shards = over_chips([out_halves, (dot(grad_near, rows_attn, 0, 0), weight_far)])
     grad_inputs, gain_attn_part = norm_back(inputs, factor_attn, attn_gain, grad_normed_attn)
@@ -368,7 +370,8 @@
         value = value + swap_chip(value)
         step = 1
         while step < groups:
-            value = value + lax.ppermute(value, "dp", [(i, i ^ step) for i in range(groups)])
+            moved = lax.ppermute(value, "dp", [(i, i ^ step) for i in range(groups)])
+            value = value + moved
             step *= 2
         return value
 

time: 744 us -> 738 us (level)
    ppermute x13, waiting for transfers between devices: 220 us -> 209 us  [swap_chip(): return lax.ppermute(value, 'tensor', [(0, 2), (2, 0), (1, 3), (3, 1)])]
    unnamed x140 -> x138, local copies, waits for them, and re-layouts: 21.5 us -> 22.2 us
  transfers between devices with their start and end apart: 37 -> 37, of which waited for: 17 -> 18; matrix products, arithmetic and copies ran while one was open for 23% -> 24% of each run, Pallas kernels for 18% -> 18%
where the time goes in v4:
time: 738 us; the launch traced here: 729 us
  waiting for transfers between devices  267 us (36%)
  matrix products  168 us (23%)
  Pallas kernels  129 us (17%)
  local copies, waits for them, and re-layouts  46.9 us (6%)
  other arithmetic  42.7 us (6%)
  starting transfers between devices  40.2 us (5%)
  blocking collectives  29.9 us (4%)
    ppermute x13, waiting for transfers between devices, swap_chip(): return lax.ppermute(value, 'tensor', [(0, 2), (2, 0), (1, 3), (3, 1)])  209 us
    dot_general x28, matrix products, dot(): lax.dot_general(left, right, (((left_dim,), (right_dim,)), ((), ())), pre...  168 us
    pallas_call x2, Pallas kernels, attend_back(): pl.pallas_call(functools.partial(attend_back_kernel, block), grid_spec=pl...  72.3 us
    pallas_call x2, Pallas kernels, attend(): pl.pallas_call(attend_kernel, grid_spec=pltpu.PrefetchScalarGridSpec(num_...  56.4 us
    ppermute x9, waiting for transfers between devices, over_chips(): lax.ppermute(lax.dynamic_index_in_dim(pairs, 1 - side, 1, False).astype(L...  41.1 us
    all_to_all x1, blocking collectives, exchange(): return lax.all_to_all(value, 'dp', split_axis=0, concat_axis=0, tiled=True)  29.9 us
    unnamed x138, local copies, waits for them, and re-layouts  22.2 us
    ppermute x3, waiting for transfers between devices, total_of(): moved = lax.ppermute(value, 'dp', [(i, i ^ step) for i in range(groups)])  16.3 us
  transfers between devices with their start and end apart: 37, of which 18 were waited for; matrix products, arithmetic and copies ran while one was open for 24% of the time, Pallas kernels for 18%

profile of v4, /device:TPU:0, one launch (start us, length us, event | category | flops | bytes accessed | tf_op | source)
XLA Modules:
  0.0 728.5 jit_solution(3521306165550909178)
XLA Ops:
  0.7 2.0 sort.17
  4.6 7.3 all-to-all-start
  15.1 23.3 %collective-permute-done = bf16[8,64,1024]{2,1,0:T(8,128)(2,1)S(1)} collective-permute-done((bf16[8,64,1024]{2,1,0:T(8,128)(2,1)}, bf16[8,64,1024]{2,1,0:T(8,128)(2,1)S(1)}, u32[]{:S(2)}, u32[]{:S(2)}) %collective-permute-start) | collective-permute-done | bytes 1048608 | tf_op jit(solution)/shard_map/ppermute | solution.py:236
  38.4 29.9 %all_to_all.20 = bf16[8,64,1024]{2,1,0:T(8,128)(2,1)S(1)} all-to-all(bf16[8,64,1024]{2,1,0:T(8,128)(2,1)S(1)} %collective-permute-done), channel_id=1, replica_groups=mesh['dp'=8,'tensor'=4] {'dp'}, dimensions={0} | all-to-all | bytes 2097152 | tf_op jit(solution)/shard_map/all_to_all | solution.py:239
  68.8 1.9 fusion.12
  79.8 7.8 %fusion.86.q_ref.k_ref.v_ref = bf16[2048,768]{1,0:T(8,128)(2,1)} fusion(bf16[1024,768]{1,0:T(8,128)(2,1)} %constant_dynamic-update-slice_fusion, bf16[1024,1024]{1,0:T(8,128)(2,1)} %collective-permute-done.1, bf16[1024,1024]{1,0:T(8,128)(2,1)} %fusion.12), kind=kOutput, calls=%fused_computation.192 | convolution fusion | flops 3229614080 | bytes 8912896 | tf_op jit(solution)/shard_map/dot_general | solution.py:20
  87.5 23.4 %collective-permute-done.2 = bf16[1024,768]{1,0:T(8,128)(2,1)} collective-permute-done((bf16[1024,768]{1,0:T(8,128)(2,1)}, bf16[1024,768]{1,0:T(8,128)(2,1)}, u32[]{:S(2)}, u32[]{:S(2)}) %collective-permute-start.2) | collective-permute-done | bytes 1572896 | tf_op jit(solution)/shard_map/ppermute | solution.py:236
  110.9 7.8 %fusion.85.q_ref.k_ref.v_ref = bf16[2048,768]{1,0:T(8,128)(2,1)} fusion(bf16[1024,768]{1,0:T(8,128)(2,1)} %collective-permute-done.2, bf16[1024,1024]{1,0:T(8,128)(2,1)} %collective-permute-done.1, bf16[1024,1024]{1,0:T(8,128)(2,1)} %fusion.12), kind=kOutput, calls=%fused_computation.191 | convolution fusion | flops 3229614080 | bytes 8912896 | tf_op jit(solution)/shard_map/dot_general | solution.py:20
  118.7 28.0 %attend.2 = (bf16[2048,256]{1,0:T(8,128)(2,1)}, f32[2048,256]{1,0:T(8,128)}) custom-call(s32[5]{0:T(128)} %pad_add_fusion.info, bf16[2048,768]{1,0:T(8,128)(2,1)} %fusion.86.q_ref.k_ref.v_ref, bf16[2048,768]{1,0:T(8,128)(2,1)} %fusion.86.q_ref.k_ref.v_ref, bf16[2048,768]{1,0:T(8,128)(2,1)} %fusion.86.q_ref.k_ref.v_ref), custom_call_target="tpu_custom_call" | custom-call | tf_op jit(solution)/shard_map/attend/pallas_call | solution.py:92
  146.7 28.4 %attend.3 = (bf16[2048,256]{1,0:T(8,128)(2,1)}, f32[2048,256]{1,0:T(8,128)}) custom-call(s32[5]{0:T(128)} %pad_add_fusion.info, bf16[2048,768]{1,0:T(8,128)(2,1)} %fusion.85.q_ref.k_ref.v_ref, bf16[2048,768]{1,0:T(8,128)(2,1)} %fusion.85.q_ref.k_ref.v_ref, bf16[2048,768]{1,0:T(8,128)(2,1)} %fusion.85.q_ref.k_ref.v_ref), custom_call_target="tpu_custom_call" | custom-call | tf_op jit(solution)/shard_map/attend/pallas_call | solution.py:92
  175.1 1.8 fusion.56
  197.0 39.1 %collective-permute-done.11 = bf16[512,1024]{1,0:T(8,128)(2,1)S(1)} collective-permute-done((bf16[512,1024]{1,0:T(8,128)(2,1)}, bf16[512,1024]{1,0:T(8,128)(2,1)S(1)}, u32[]{:S(2)}, u32[]{:S(2)}) %collective-permute-start.11) | collective-permute-done | bytes 1048608 | tf_op jit(solution)/shard_map/ppermute | solution.py:236
  236.6 2.1 constant_dynamic-update-slice_fusion.3
  238.8 28.3 %collective-permute-done.7 = bf16[1024,704]{0,1:T(8,128)(2,1)} collective-permute-done((bf16[1024,704]{0,1:T(8,128)(2,1)S(1)}, bf16[1024,704]{0,1:T(8,128)(2,1)}, u32[]{:S(2)}, u32[]{:S(2)}) %collective-permute-start.7) | collective-permute-done | bytes 1441824 | tf_op jit(solution)/shard_map/ppermute | solution.py:236
  268.6 28.9 %collective-permute-done.8 = bf16[704,1024]{1,0:T(8,128)(2,1)} collective-permute-done((bf16[704,1024]{1,0:T(8,128)(2,1)}, bf16[704,1024]{1,0:T(8,128)(2,1)}, u32[]{:S(2)}, u32[]{:S(2)}) %collective-permute-start.8) | collective-permute-done | bytes 1441824 | tf_op jit(solution)/shard_map/ppermute | solution.py:236
  300.6 10.9 %fusion.81 = bf16[2048,1408]{1,0:T(8,128)(2,1)} fusion(bf16[1024,1408]{0,1:T(8,128)(2,1)S(1)} %constant_dynamic-update-slice_fusion.5, bf16[1024,1024]{1,0:T(8,128)(2,1)} %collective-permute-done.5, bf16[1024,1024]{1,0:T(8,128)(2,1)} %multiply_convert_fusion.2), kind=kOutput, calls=%fused_computation.187 | convolution fusion | flops 5913968640 | bytes 12845056 | tf_op jit(solution)/shard_map/dot_general | solution.py:20
  311.5 11.2 %fusion.82 = bf16[2048,1408]{1,0:T(8,128)(2,1)} fusion(bf16[1024,1408]{0,1:T(8,128)(2,1)S(1)} %constant_dynamic-update-slice_fusion.3, bf16[1024,1024]{1,0:T(8,128)(2,1)} %collective-permute-done.5, bf16[1024,1024]{1,0:T(8,128)(2,1)} %multiply_convert_fusion.2), kind=kOutput, calls=%fused_computation.188 | convolution fusion | flops 5913968640 | bytes 12845056 | tf_op jit(solution)/shard_map/dot_general | solution.py:20
  322.7 19.1 %fusion.3 = (bf16[2048,1408]{1,0:T(8,128)(2,1)}, bf16[2048,1408]{1,0:T(8,128)(2,1)}, bf16[2048,1408]{1,0:T(8,128)(2,1)}) fusion(bf16[2048,1408]{1,0:T(8,128)(2,1)} %fusion.81, bf16[2048,1408]{1,0:T(8,128)(2,1)} %fusion.82, bf16[1408,1024]{1,0:T(8,128)(2,1)} %copy-done.29, bf16[1024,1024]{1,0:T(8,128)(2,1)} %collective-permute-done.12, ...), kind=kOutput, calls=%fused_computation.11 | convolution fusion | flops 5962989568 | bytes 35913728 | tf_op jit(solution)/shard_map/dot_general | solution.py:20
  341.8 8.3 %fusion.22 = f32[1024,1024]{1,0:T(8,128)} fusion(bf16[1024,1408]{0,1:T(8,128)(2,1)} %copy-done.32, bf16[2048,1408]{1,0:T(8,128)(2,1)} %get-tuple-element.105), kind=kOutput, calls=%fused_computation.62 | convolution fusion | flops 2952790016 | bytes 9961472 | tf_op jit(solution)/shard_map/dot_general | solution.py:20
  350.2 9.3 %fusion.79 = f32[1408,1024]{1,0:T(8,128)S(1)} fusion(bf16[2048,1408]{1,0:T(8,128)(2,1)S(1)} %copy-done.55, bf16[1024,1024]{1,0:T(8,128)(2,1)} %collective-permute-done.5, bf16[1024,1024]{1,0:T(8,128)(2,1)} %multiply_convert_fusion.2), kind=kOutput, calls=%fused_computation.185 | convolution fusion | flops 5913968640 | bytes 15728640 | tf_op jit(solution)/shard_map/dot_general | solution.py:20
  359.7 2.6 copy-done.10
  362.3 9.4 %fusion.80 = f32[1408,1024]{1,0:T(8,128)S(1)} fusion(bf16[2048,1408]{1,0:T(8,128)(2,1)S(1)} %bitcast.192, bf16[1024,1024]{1,0:T(8,128)(2,1)} %collective-permute-done.5, bf16[1024,1024]{1,0:T(8,128)(2,1)} %multiply_convert_fusion.2), kind=kOutput, calls=%fused_computation.186 | convolution fusion | flops 5913968640 | bytes 15728640 | tf_op jit(solution)/shard_map/dot_general | solution.py:20
  371.9 2.6 copy-done.11
  375.5 4.8 fusion.36
  380.3 8.0 %fusion.34 = f32[1408,1024]{1,0:T(8,128)S(1)} fusion(bf16[2048,1408]{1,0:T(8,128)(2,1)S(1)} %bitcast.194, bf16[1024,1024]{1,0:T(8,128)(2,1)} %collective-permute-done.12, bf16[1024,1024]{1,0:T(8,128)(2,1)S(1)} %copy-done.23), kind=kOutput, calls=%fused_computation.77 | convolution fusion | flops 5913968640 | bytes 15728640 | tf_op jit(solution)/shard_map/dot_general | solution.py:20
  389.0 4.7 add_convert_fusion.1
  394.4 1.8 collective-permute-start.26
  396.2 5.2 fusion.28
  401.5 5.2 fusion.26
  406.8 16.4 %collective-permute-done.30 = bf16[704,1024]{1,0:T(8,128)(2,1)S(1)} collective-permute-done((bf16[704,1024]{1,0:T(8,128)(2,1)S(1)}, bf16[704,1024]{1,0:T(8,128)(2,1)S(1)}, u32[]{:S(2)}, u32[]{:S(2)}) %collective-permute-start.30) | collective-permute-done | bytes 1441824 | tf_op jit(solution)/shard_map/ppermute | solution.py:236
  425.1 2.4 multiply_reduce_fusion
  427.6 3.8 fusion.87
  431.4 7.6 %collective-permute-done.31 = bf16[4,704,128]{2,1,0:T(8,128)(2,1)S(1)} collective-permute-done((bf16[4,704,128]{2,1,0:T(8,128)(2,1)S(1)}, bf16[4,704,128]{2,1,0:T(8,128)(2,1)S(1)}, u32[]{:S(2)}, u32[]{:S(2)}) %collective-permute-start.31) | collective-permute-done | bytes 720928 | tf_op jit(solution)/shard_map/ppermute | solution.py:325
  440.4 5.9 multiply_convert_fusion.1
  449.5 6.2 collective-permute-done.33
  456.4 28.5 %collective-permute-done.26 = bf16[1408,1024]{1,0:T(8,128)(2,1)S(1)} collective-permute-done((bf16[1408,1024]{1,0:T(8,128)(2,1)S(1)}, bf16[1408,1024]{1,0:T(8,128)(2,1)S(1)}, u32[]{:S(2)}, u32[]{:S(2)}) %collective-permute-start.26) | collective-permute-done | bytes 2883616 | tf_op jit(solution)/shard_map/ppermute | solution.py:236
  488.5 3.9 fusion.77.do_ref
  492.4 36.1 %attend_back.2 = (bf16[2048,256]{1,0:T(8,128)(2,1)}, bf16[2048,256]{1,0:T(8,128)(2,1)}, bf16[2048,256]{1,0:T(8,128)(2,1)}) custom-call(s32[5]{0:T(128)} %pad_add_fusion.info, bf16[2048,768]{1,0:T(8,128)(2,1)} %fusion.85.q_ref.k_ref.v_ref, bf16[2048,768]{1,0:T(8,128)(2,1)} %fusion.85.q_ref.k_ref.v_ref, bf16[2048,768]{1,0:T(8,128)(2,1)} %fusion.85.q_ref.k_ref.v_ref, ...), custom_call_target="tpu_custom_call" | custom-call | tf_op jit(solution)/shard_map/attend_back/pallas_call | solution.py:185
  531.3 5.1 fusion.78.do_ref
  536.4 6.8 fusion.84
  543.2 36.2 %attend_back.3 = (bf16[2048,256]{1,0:T(8,128)(2,1)}, bf16[2048,256]{1,0:T(8,128)(2,1)}, bf16[2048,256]{1,0:T(8,128)(2,1)}) custom-call(s32[5]{0:T(128)} %pad_add_fusion.info, bf16[2048,768]{1,0:T(8,128)(2,1)} %fusion.86.q_ref.k_ref.v_ref, bf16[2048,768]{1,0:T(8,128)(2,1)} %fusion.86.q_ref.k_ref.v_ref, bf16[2048,768]{1,0:T(8,128)(2,1)} %fusion.86.q_ref.k_ref.v_ref, ...), custom_call_target="tpu_custom_call" | custom-call | tf_op jit(solution)/shard_map/attend_back/pallas_call | solution.py:185
  582.2 3.2 fusion.44
  585.5 3.3 fusion.48
  588.8 3.0 convolution_convert_fusion
  594.5 3.2 add_convert_fusion
  597.8 3.9 fusion.76
  601.7 3.4 fusion.46
  605.0 7.5 %fusion.83 = f32[768,1024]{1,0:T(8,128)} fusion(bf16[2048,768]{1,0:T(8,128)(2,1)S(1)} %constant_dynamic-update-slice_fusion.12, bf16[1024,1024]{1,0:T(8,128)(2,1)} %collective-permute-done.1, bf16[1024,1024]{1,0:T(8,128)(2,1)} %fusion.12), kind=kOutput, calls=%fused_computation.189 | convolution fusion | flops 3229614080 | bytes 10485760 | tf_op jit(solution)/shard_map/dot_general | solution.py:20
  616.0 2.6 fusion.19
  618.6 2.0 fusion.16
  622.1 4.2 all-to-all-start.3
  626.4 11.9 %collective-permute-done.22 = bf16[1024,1024]{1,0:T(8,128)(2,1)} collective-permute-done((bf16[1024,1024]{1,0:T(8,128)(2,1)}, bf16[1024,1024]{1,0:T(8,128)(2,1)}, u32[]{:S(2)}, u32[]{:S(2)}) %collective-permute-start.22) | collective-permute-done | bytes 2097184 | tf_op jit(solution)/shard_map/ppermute | solution.py:236
  638.2 3.2 copy_bitcast_fusion.1
  645.5 2.5 collective-permute-done.18
  648.9 19.6 %collective-permute-done.23 = bf16[4,1024,128]{2,1,0:T(8,128)(2,1)S(1)} collective-permute-done((bf16[4,1024,128]{2,1,0:T(8,128)(2,1)S(1)}, bf16[4,1024,128]{2,1,0:T(8,128)(2,1)S(1)}, u32[]{:S(2)}, u32[]{:S(2)}) %collective-permute-start.23) | collective-permute-done | bytes 1048608 | tf_op jit(solution)/shard_map/ppermute | solution.py:325
  670.4 4.4 all-to-all-start.2
  674.8 4.0 maximum_select_fusion
  678.8 2.0 collective-permute-start.20
  681.8 15.2 %collective-permute-done.20 = f32[2,1024]{1,0:T(2,128)S(1)} collective-permute-done((f32[2,1024]{1,0:T(2,128)S(1)}, f32[2,1024]{1,0:T(2,128)S(1)}, u32[]{:S(2)}, u32[]{:S(2)}) %collective-permute-start.20) | collective-permute-done | bytes 8224 | tf_op jit(solution)/shard_map/ppermute | solution.py:373
  699.7 1.9 collective-permute-start.25
  704.3 6.8 collective-permute-done.25
  714.1 7.2 collective-permute-done.16
  721.3 3.3 maximum_select_fusion.1
  724.6 3.7 gather_fusion.2
  (266 shorter events, 79.8 us)
Async XLA Ops:
  4.6 33.7 %all-to-all-start = ((bf16[8,64,1024]{2,1,0:T(8,128)(2,1)}), bf16[8,64,1024]{2,1,0:T(8,128)(2,1)S(1)}, u32[]{:S(2)}, u32[]{:S(2)}) async-start(bf16[8,64,1024]{2,1,0:T(8,128)(2,1)} %gather_fusion), calls=%async_computation | async-start | bytes 2097152 | tf_op jit(solution)/shard_map/all_to_all | solution.py:239
  11.9 56.9 %copy-start.45 = (f32[1024]{0:T(1024)S(1)}, f32[1024]{0:T(1024)}, u32[]{:S(2)}) copy-start(f32[1024]{0:T(1024)} %param.20) | copy-start | bytes 12292
  13.5 24.8 %collective-permute-start = (bf16[8,64,1024]{2,1,0:T(8,128)(2,1)}, bf16[8,64,1024]{2,1,0:T(8,128)(2,1)S(1)}, u32[]{:S(2)}, u32[]{:S(2)}) collective-permute-start(bf16[8,64,1024]{2,1,0:T(8,128)(2,1)} %gather_fusion.1), channel_id=1, source_target_pairs={{0,2},{2,0},{1,3},{3,1},{4,6},{6,4},{5,7},{7,5},{8,10},{10,8},{9,1... | collective-permute-start | bytes 3145736 | tf_op jit(solution)/shard_map/ppermute | solution.py:236
  38.4 144.7 %copy-start.4 = (bf16[8,64,1024]{2,1,0:T(8,128)(2,1)}, bf16[8,64,1024]{2,1,0:T(8,128)(2,1)S(1)}, u32[]{:S(2)}) copy-start(bf16[8,64,1024]{2,1,0:T(8,128)(2,1)S(1)} %all-to-all-done) | copy-start | bytes 3145732
  68.2 114.8 %copy-start.6 = (bf16[8,64,1024]{2,1,0:T(8,128)(2,1)}, bf16[8,64,1024]{2,1,0:T(8,128)(2,1)S(1)}, u32[]{:S(2)}) copy-start(bf16[8,64,1024]{2,1,0:T(8,128)(2,1)S(1)} %all_to_all.20) | copy-start | bytes 3145732
  68.8 230.1 %copy-start.41 = (f32[1024]{0:T(1024)}, f32[1024]{0:T(1024)S(1)}, u32[]{:S(2)}) copy-start(f32[1024]{0:T(1024)S(1)} %rsqrt.26) | copy-start | bytes 12292
  68.8 9.1 %copy-start.53 = (s32[16]{0:T(128)S(1)}, s32[16]{0:T(128)}, u32[]{:S(2)}) copy-start(s32[16]{0:T(128)} %param.18) | copy-start | bytes 196
  70.7 9.1 %collective-permute-start.1 = (bf16[1024,1024]{1,0:T(8,128)(2,1)}, bf16[1024,1024]{1,0:T(8,128)(2,1)}, u32[]{:S(2)}, u32[]{:S(2)}) collective-permute-start(bf16[1024,1024]{1,0:T(8,128)(2,1)} %fusion.12), channel_id=1, source_target_pairs={{0,1},{1,0},{2,3},{3,2},{4,5},{5,4},{6,7},{7,6},{8,9},{9,8},{10,11... | collective-permute-start | bytes 6291464 | tf_op jit(solution)/shard_map/ppermute | solution.py:233
  73.3 37.6 %collective-permute-start.2 = (bf16[1024,768]{1,0:T(8,128)(2,1)}, bf16[1024,768]{1,0:T(8,128)(2,1)}, u32[]{:S(2)}, u32[]{:S(2)}) collective-permute-start(bf16[1024,768]{1,0:T(8,128)(2,1)} %constant_dynamic-update-slice_fusion), channel_id=1, source_target_pairs={{0,2},{2,0},{1,3},{3,1},{4,6},{6,4},{5,7},{7,5},{8,10},{10,8},{9,1... | collective-permute-start | bytes 4718600 | tf_op jit(solution)/shard_map/ppermute | solution.py:236
  74.9 102.1 %collective-permute-start.3 = (bf16[256,1024]{1,0:T(8,128)(2,1)}, bf16[256,1024]{1,0:T(8,128)(2,1)}, u32[]{:S(2)}, u32[]{:S(2)}) collective-permute-start(bf16[256,1024]{1,0:T(8,128)(2,1)} %param.24), channel_id=1, source_target_pairs={{0,2},{2,0},{1,3},{3,1},{4,6},{6,4},{5,7},{7,5},{8,10},{10,8},{9,1... | collective-permute-start | bytes 1572872 | tf_op jit(solution)/shard_map/ppermute | solution.py:236
  146.7 28.4 %copy-start.14 = (bf16[2048,256]{1,0:T(8,128)(2,1)S(1)}, bf16[2048,256]{1,0:T(8,128)(2,1)}, u32[]{:S(2)}) copy-start(bf16[2048,256]{1,0:T(8,128)(2,1)} %get-tuple-element.26.o_ref) | copy-start | bytes 3145732
  178.8 4.2 collective-permute-start.4
  178.9 57.7 %collective-permute-start.6 = (bf16[1024,704]{0,1:T(8,128)(2,1)}, bf16[1024,704]{0,1:T(8,128)(2,1)}, u32[]{:S(2)}, u32[]{:S(2)}) collective-permute-start(bf16[1024,704]{0,1:T(8,128)(2,1)} %param.26), channel_id=1, source_target_pairs={{0,2},{2,0},{1,3},{3,1},{4,6},{6,4},{5,7},{7,5},{8,10},{10,8},{9,1... | collective-permute-start | bytes 4325384 | tf_op jit(solution)/shard_map/ppermute | solution.py:236
  187.0 113.6 %collective-permute-start.5 = (bf16[1024,1024]{1,0:T(8,128)(2,1)}, bf16[1024,1024]{1,0:T(8,128)(2,1)}, u32[]{:S(2)}, u32[]{:S(2)}) collective-permute-start(bf16[1024,1024]{1,0:T(8,128)(2,1)} %multiply_convert_fusion.2), channel_id=1, source_target_pairs={{0,1},{1,0},{2,3},{3,2},{4,5},{5,4},{6,7},{7,6},{8,9},{9,8},{10,11... | collective-permute-start | bytes 6291464 | tf_op jit(solution)/shard_map/ppermute | solution.py:233
  189.1 47.0 %copy-start.12 = (bf16[512,1024]{1,0:T(8,128)(2,1)}, bf16[512,1024]{1,0:T(8,128)(2,1)S(1)}, u32[]{:S(2)}) copy-start(bf16[512,1024]{1,0:T(8,128)(2,1)S(1)} %get-tuple-element.109) | copy-start | bytes 3145732
  189.1 47.0 %collective-permute-start.11 = (bf16[512,1024]{1,0:T(8,128)(2,1)}, bf16[512,1024]{1,0:T(8,128)(2,1)S(1)}, u32[]{:S(2)}, u32[]{:S(2)}) collective-permute-start(bf16[512,1024]{1,0:T(8,128)(2,1)} %get-tuple-element.110), channel_id=1, source_target_pairs={{0,2},{2,0},{1,3},{3,1},{4,6},{6,4},{5,7},{7,5},{8,10},{10,8},{9,1... | collective-permute-start | bytes 3145736 | tf_op jit(solution)/shard_map/ppermute | solution.py:236
  190.6 76.5 %collective-permute-start.7 = (bf16[1024,704]{0,1:T(8,128)(2,1)S(1)}, bf16[1024,704]{0,1:T(8,128)(2,1)}, u32[]{:S(2)}, u32[]{:S(2)}) collective-permute-start(bf16[1024,704]{0,1:T(8,128)(2,1)S(1)} %copy-done.26), channel_id=1, source_target_pairs={{0,2},{2,0},{1,3},{3,1},{4,6},{6,4},{5,7},{7,5},{8,10},{10,8},{9,1... | collective-permute-start | bytes 4325384 | tf_op jit(solution)/shard_map/ppermute | solution.py:236
  191.2 106.3 %collective-permute-start.8 = (bf16[704,1024]{1,0:T(8,128)(2,1)}, bf16[704,1024]{1,0:T(8,128)(2,1)}, u32[]{:S(2)}, u32[]{:S(2)}) collective-permute-start(bf16[704,1024]{1,0:T(8,128)(2,1)} %param.28), channel_id=1, source_target_pairs={{0,2},{2,0},{1,3},{3,1},{4,6},{6,4},{5,7},{7,5},{8,10},{10,8},{9,1... | collective-permute-start | bytes 4325384 | tf_op jit(solution)/shard_map/ppermute | solution.py:236
  193.9 42.2 %copy-start.47 = (f32[1024]{0:T(1024)}, f32[1024]{0:T(1024)S(1)}, u32[]{:S(2)}) copy-start(f32[1024]{0:T(1024)S(1)} %fusion.67) | copy-start | bytes 12292
  236.5 62.4 %copy-start.22 = (bf16[1024,1024]{1,0:T(8,128)(2,1)}, bf16[1024,1024]{1,0:T(8,128)(2,1)S(1)}, u32[]{:S(2)}) copy-start(bf16[1024,1024]{1,0:T(8,128)(2,1)S(1)} %fusion.20) | copy-start | bytes 6291460
  236.5 86.2 %collective-permute-start.12 = (bf16[1024,1024]{1,0:T(8,128)(2,1)S(1)}, bf16[1024,1024]{1,0:T(8,128)(2,1)}, u32[]{:S(2)}, u32[]{:S(2)}) collective-permute-start(bf16[1024,1024]{1,0:T(8,128)(2,1)S(1)} %fusion.20), channel_id=1, source_target_pairs={{0,1},{1,0},{2,3},{3,2},{4,5},{5,4},{6,7},{7,6},{8,9},{9,8},{10,11... | collective-permute-start | bytes 6291464 | tf_op jit(solution)/shard_map/ppermute | solution.py:233
  238.8 72.7 %copy-start.34 = (bf16[1024,1408]{0,1:T(8,128)(2,1)}, bf16[1024,1408]{0,1:T(8,128)(2,1)S(1)}, u32[]{:S(2)}) copy-start(bf16[1024,1408]{0,1:T(8,128)(2,1)S(1)} %constant_dynamic-update-slice_fusion.3) | copy-start | bytes 8650756
  268.6 42.9 %copy-start.32 = (bf16[1024,1408]{0,1:T(8,128)(2,1)}, bf16[1024,1408]{0,1:T(8,128)(2,1)S(1)}, u32[]{:S(2)}) copy-start(bf16[1024,1408]{0,1:T(8,128)(2,1)S(1)} %constant_dynamic-update-slice_fusion.5) | copy-start | bytes 8650756
  311.5 11.2 %copy-start.23 = (bf16[1024,1024]{1,0:T(8,128)(2,1)S(1)}, bf16[1024,1024]{1,0:T(8,128)(2,1)}, u32[]{:S(2)}) copy-start(bf16[1024,1024]{1,0:T(8,128)(2,1)} %copy-done.22) | copy-start | bytes 6291460
  341.8 8.3 %copy-start.55 = (bf16[2048,1408]{1,0:T(8,128)(2,1)S(1)}, bf16[2048,1408]{1,0:T(8,128)(2,1)}, u32[]{:S(2)}) copy-start(bf16[2048,1408]{1,0:T(8,128)(2,1)} %get-tuple-element.105) | copy-start | bytes 17301508
  341.8 20.4 %slice-start.4 = ((s8[5767168]{0:T(1024)(128)(4,1)}), s8[4194304]{0:T(1024)(128)(4,1)S(1)}, s32[]{:S(2)}) async-start(s8[5767168]{0:T(1024)(128)(4,1)} %bitcast.191), calls=%async_computation.8 | async-start | bytes 8388608
  350.2 12.1 %slice-start.5 = ((s8[5767168]{0:T(1024)(128)(4,1)}), s8[1572864]{0:T(1024)(128)(4,1)S(1)}, s32[]{:S(2)}) async-start(s8[5767168]{0:T(1024)(128)(4,1)} %bitcast.191), calls=%async_computation.9 | async-start | bytes 3145728
  359.7 14.8 %slice-start.6 = ((s8[5767168]{0:T(1024)(128)(4,1)}), s8[4194304]{0:T(1024)(128)(4,1)S(1)}, s32[]{:S(2)}) async-start(s8[5767168]{0:T(1024)(128)(4,1)} %bitcast.193), calls=%async_computation.10 | async-start | bytes 8388608
  362.3 12.2 %slice-start.7 = ((s8[5767168]{0:T(1024)(128)(4,1)}), s8[1572864]{0:T(1024)(128)(4,1)S(1)}, s32[]{:S(2)}) async-start(s8[5767168]{0:T(1024)(128)(4,1)} %bitcast.193), calls=%async_computation.11 | async-start | bytes 3145728
  380.3 8.6 %copy-start.35 = (bf16[1024,1408]{0,1:T(8,128)(2,1)S(1)}, bf16[1024,1408]{0,1:T(8,128)(2,1)}, u32[]{:S(2)}) copy-start(bf16[1024,1408]{0,1:T(8,128)(2,1)} %copy-done.34) | copy-start | bytes 8650756
  380.3 8.6 %copy-start.56 = (f32[1024,1024]{1,0:T(8,128)S(1)}, f32[1024,1024]{1,0:T(8,128)}, u32[]{:S(2)}) copy-start(f32[1024,1024]{1,0:T(8,128)} %fusion.22) | copy-start | bytes 12582916
  388.6 34.5 %collective-permute-start.30 = (bf16[704,1024]{1,0:T(8,128)(2,1)S(1)}, bf16[704,1024]{1,0:T(8,128)(2,1)S(1)}, u32[]{:S(2)}, u32[]{:S(2)}) collective-permute-start(bf16[704,1024]{1,0:T(8,128)(2,1)S(1)} %slice.253), channel_id=1, source_target_pairs={{0,2},{2,0},{1,3},{3,1},{4,6},{6,4},{5,7},{7,5},{8,10},{10,8},{9,1... | collective-permute-start | bytes 4325384 | tf_op jit(solution)/shard_map/ppermute | solution.py:236
  388.9 51.4 %collective-permute-start.9 = (bf16[1024,1024]{1,0:T(8,128)(2,1)}, bf16[1024,1024]{1,0:T(8,128)(2,1)}, u32[]{:S(2)}, u32[]{:S(2)}) collective-permute-start(bf16[1024,1024]{1,0:T(8,128)(2,1)} %fusion.36), channel_id=1, source_target_pairs={{0,1},{1,0},{2,3},{3,2},{4,5},{5,4},{6,7},{7,6},{8,9},{9,8},{10,11... | collective-permute-start | bytes 6291464 | tf_op jit(solution)/shard_map/ppermute | solution.py:233
  393.6 31.4 %collective-permute-start.13 = (bf16[1024,1024]{1,0:T(8,128)(2,1)}, bf16[1024,1024]{1,0:T(8,128)(2,1)S(1)}, u32[]{:S(2)}, u32[]{:S(2)}) collective-permute-start(bf16[1024,1024]{1,0:T(8,128)(2,1)} %add_convert_fusion.1), channel_id=1, source_target_pairs={{0,1},{1,0},{2,3},{3,2},{4,5},{5,4},{6,7},{7,6},{8,9},{9,8},{10,11... | collective-permute-start | bytes 6291464 | tf_op jit(solution)/shard_map/ppermute | solution.py:233
  394.4 90.5 %collective-permute-start.26 = (bf16[1408,1024]{1,0:T(8,128)(2,1)S(1)}, bf16[1408,1024]{1,0:T(8,128)(2,1)S(1)}, u32[]{:S(2)}, u32[]{:S(2)}) collective-permute-start(bf16[1408,1024]{1,0:T(8,128)(2,1)S(1)} %pad_maximum_fusion.4), channel_id=1, source_target_pairs={{0,2},{2,0},{1,3},{3,1},{4,6},{6,4},{5,7},{7,5},{8,10},{10,8},{9,1... | collective-permute-start | bytes 8650760 | tf_op jit(solution)/shard_map/ppermute | solution.py:236
  406.7 18.4 %copy-start.3 = (f32[1024,1024]{1,0:T(8,128)S(1)}, f32[1024,1024]{1,0:T(8,128)}, u32[]{:S(2)}) copy-start(f32[1024,1024]{1,0:T(8,128)} %copy-done.2) | copy-start | bytes 12582916
  406.7 18.4 %copy-start.44 = (f32[1024]{0:T(1024)S(1)}, f32[1024]{0:T(1024)}, u32[]{:S(2)}) copy-start(f32[1024]{0:T(1024)} %copy-done.43) | copy-start | bytes 12292
  406.7 18.3 %copy-start.50 = (f32[1024]{0:T(1024)S(1)}, f32[1024]{0:T(1024)}, u32[]{:S(2)}) copy-start(f32[1024]{0:T(1024)} %param.25) | copy-start | bytes 12292
  423.6 15.5 %collective-permute-start.31 = (bf16[4,704,128]{2,1,0:T(8,128)(2,1)S(1)}, bf16[4,704,128]{2,1,0:T(8,128)(2,1)S(1)}, u32[]{:S(2)}, u32[]{:S(2)}) collective-permute-start(bf16[4,704,128]{2,1,0:T(8,128)(2,1)S(1)} %fusion.53), channel_id=1, source_target_pairs={{0,4},{4,0},{8,12},{12,8},{16,20},{20,16},{24,28},{28,24},{1,5},{5... | collective-permute-start | bytes 2162696 | tf_op jit(solution)/shard_map/ppermute | solution.py:325
  431.4 9.0 %copy-start.31 = (bf16[1408,1024]{1,0:T(8,128)(2,1)S(1)}, bf16[1408,1024]{1,0:T(8,128)(2,1)}, u32[]{:S(2)}) copy-start(bf16[1408,1024]{1,0:T(8,128)(2,1)} %copy-done.29) | copy-start | bytes 8650756
  431.4 57.1 %collective-permute-start.14 = (bf16[1024,1024]{1,0:T(8,128)(2,1)S(1)}, bf16[1024,1024]{1,0:T(8,128)(2,1)}, u32[]{:S(2)}, u32[]{:S(2)}) collective-permute-start(bf16[1024,1024]{1,0:T(8,128)(2,1)S(1)} %get-tuple-element.99), channel_id=1, source_target_pairs={{0,1},{1,0},{2,3},{3,2},{4,5},{5,4},{6,7},{7,6},{8,9},{9,8},{10,11... | collective-permute-start | bytes 6291464 | tf_op jit(solution)/shard_map/ppermute | solution.py:233
  439.2 7.9 %collective-permute-start.32 = (bf16[2,704,128]{2,1,0:T(8,128)(2,1)S(1)}, bf16[2,704,128]{2,1,0:T(8,128)(2,1)S(1)}, u32[]{:S(2)}, u32[]{:S(2)}) collective-permute-start(bf16[2,704,128]{2,1,0:T(8,128)(2,1)S(1)} %fusion.62), channel_id=1, source_target_pairs={{0,8},{4,12},{8,0},{12,4},{16,24},{20,28},{24,16},{28,20},{1,9},{5... | collective-permute-start | bytes 1081352 | tf_op jit(solution)/shard_map/ppermute | solution.py:325
  447.2 37.8 %slice-start.3 = ((f32[1408,1024]{1,0:T(8,128)}), f32[704,1024]{1,0:T(8,128)S(1)}, s32[]{:S(2)}) async-start(f32[1408,1024]{1,0:T(8,128)} %copy-done.11), calls=%async_computation.7 | async-start | bytes 5767168 | tf_op jit(solution)/shard_map/slice | solution.py:335
  447.2 37.7 %slice-start.2 = ((f32[1408,1024]{1,0:T(8,128)}), f32[704,1024]{1,0:T(8,128)S(1)}, s32[]{:S(2)}) async-start(f32[1408,1024]{1,0:T(8,128)} %copy-done.10), calls=%async_computation.6 | async-start | bytes 5767168 | tf_op jit(solution)/shard_map/slice | solution.py:335
  447.3 8.4 %collective-permute-start.33 = (bf16[1,704,128]{2,1,0:T(8,128)(2,1)S(1)}, bf16[1,704,128]{2,1,0:T(8,128)(2,1)S(1)}, u32[]{:S(2)}, u32[]{:S(2)}) collective-permute-start(bf16[1,704,128]{2,1,0:T(8,128)(2,1)S(1)} %dynamic-slice_convert_fusion.8), channel_id=1, source_target_pairs={{0,16},{4,20},{8,24},{12,28},{16,0},{20,4},{24,8},{28,12},{1,17},{... | collective-permute-start | bytes 540680 | tf_op jit(solution)/shard_map/ppermute | solution.py:325
  448.9 225.9 %collective-permute-start.10 = (bf16[512,1024]{1,0:T(8,128)(2,1)}, bf16[512,1024]{1,0:T(8,128)(2,1)}, u32[]{:S(2)}, u32[]{:S(2)}) collective-permute-start(bf16[512,1024]{1,0:T(8,128)(2,1)} %get-tuple-element.112), channel_id=1, source_target_pairs={{0,2},{2,0},{1,3},{3,1},{4,6},{6,4},{5,7},{7,5},{8,10},{10,8},{9,1... | collective-permute-start | bytes 3145736 | tf_op jit(solution)/shard_map/ppermute | solution.py:236
  487.0 125.5 %collective-permute-start.27 = (bf16[4,1408,128]{2,1,0:T(8,128)(2,1)}, bf16[4,1408,128]{2,1,0:T(8,128)(2,1)}, u32[]{:S(2)}, u32[]{:S(2)}) collective-permute-start(bf16[4,1408,128]{2,1,0:T(8,128)(2,1)} %fusion.50), channel_id=1, source_target_pairs={{0,4},{4,0},{8,12},{12,8},{16,20},{20,16},{24,28},{28,24},{1,5},{5... | collective-permute-start | bytes 4325384 | tf_op jit(solution)/shard_map/ppermute | solution.py:325
  593.3 44.9 %collective-permute-start.22 = (bf16[1024,1024]{1,0:T(8,128)(2,1)}, bf16[1024,1024]{1,0:T(8,128)(2,1)}, u32[]{:S(2)}, u32[]{:S(2)}) collective-permute-start(bf16[1024,1024]{1,0:T(8,128)(2,1)} %pad_maximum_fusion.9), channel_id=1, source_target_pairs={{0,2},{2,0},{1,3},{3,1},{4,6},{6,4},{5,7},{7,5},{8,10},{10,8},{9,1... | collective-permute-start | bytes 6291464 | tf_op jit(solution)/shard_map/ppermute | solution.py:236
  597.7 18.2 %collective-permute-start.15 = (bf16[1024,1024]{1,0:T(8,128)(2,1)S(1)}, bf16[1024,1024]{1,0:T(8,128)(2,1)S(1)}, u32[]{:S(2)}, u32[]{:S(2)}) collective-permute-start(bf16[1024,1024]{1,0:T(8,128)(2,1)S(1)} %add_convert_fusion), channel_id=1, source_target_pairs={{0,1},{1,0},{2,3},{3,2},{4,5},{5,4},{6,7},{7,6},{8,9},{9,8},{10,11... | collective-permute-start | bytes 6291464 | tf_op jit(solution)/shard_map/ppermute | solution.py:233
  601.7 10.9 %slice-start = ((s8[5767168]{0:T(1024)(128)(4,1)}), s8[4194304]{0:T(1024)(128)(4,1)S(1)}, s32[]{:S(2)}) async-start(s8[5767168]{0:T(1024)(128)(4,1)} %bitcast.164), calls=%async_computation.4 | async-start | bytes 8388608
  615.3 27.7 %collective-permute-start.28 = (bf16[2,1408,128]{2,1,0:T(8,128)(2,1)}, bf16[2,1408,128]{2,1,0:T(8,128)(2,1)}, u32[]{:S(2)}, u32[]{:S(2)}) collective-permute-start(bf16[2,1408,128]{2,1,0:T(8,128)(2,1)} %fusion.52), channel_id=1, source_target_pairs={{0,8},{4,12},{8,0},{12,4},{16,24},{20,28},{24,16},{28,20},{1,9},{5... | collective-permute-start | bytes 2162696 | tf_op jit(solution)/shard_map/ppermute | solution.py:325
  622.1 48.2 %all-to-all-start.3 = ((bf16[8,64,1024]{2,1,0:T(8,128)(2,1)}), bf16[8,64,1024]{2,1,0:T(8,128)(2,1)}, u32[]{:S(2)}, u32[]{:S(2)}) async-start(bf16[8,64,1024]{2,1,0:T(8,128)(2,1)} %bitcast.179), calls=%async_computation.3 | async-start | bytes 2097152 | tf_op jit(solution)/shard_map/all_to_all | solution.py:239
  641.6 26.9 %collective-permute-start.23 = (bf16[4,1024,128]{2,1,0:T(8,128)(2,1)S(1)}, bf16[4,1024,128]{2,1,0:T(8,128)(2,1)S(1)}, u32[]{:S(2)}, u32[]{:S(2)}) collective-permute-start(bf16[4,1024,128]{2,1,0:T(8,128)(2,1)S(1)} %fusion.51), channel_id=1, source_target_pairs={{0,4},{4,0},{8,12},{12,8},{16,20},{20,16},{24,28},{28,24},{1,5},{5... | collective-permute-start | bytes 3145736 | tf_op jit(solution)/shard_map/ppermute | solution.py:325
  642.9 1.3 collective-permute-start.17
  644.3 3.7 collective-permute-start.18
  645.5 35.3 %collective-permute-start.29 = (bf16[1,1408,128]{2,1,0:T(8,128)(2,1)}, bf16[1,1408,128]{2,1,0:T(8,128)(2,1)}, u32[]{:S(2)}, u32[]{:S(2)}) collective-permute-start(bf16[1,1408,128]{2,1,0:T(8,128)(2,1)} %dynamic-slice_convert_fusion.6), channel_id=1, source_target_pairs={{0,16},{4,20},{8,24},{12,28},{16,0},{20,4},{24,8},{28,12},{1,17},{... | collective-permute-start | bytes 1081352 | tf_op jit(solution)/shard_map/ppermute | solution.py:325
  648.0 30.8 %collective-permute-start.19 = (f32[2,1024]{1,0:T(2,128)S(1)}, f32[2,1024]{1,0:T(2,128)S(1)}, u32[]{:S(2)}, u32[]{:S(2)}) collective-permute-start(f32[2,1024]{1,0:T(2,128)S(1)} %fusion.118), channel_id=1, source_target_pairs={{0,4},{4,0},{8,12},{12,8},{16,20},{20,16},{24,28},{28,24},{1,5},{5... | collective-permute-start | bytes 24584 | tf_op jit(solution)/shard_map/ppermute | solution.py:373
  669.6 28.7 %collective-permute-start.24 = (bf16[2,1024,128]{2,1,0:T(8,128)(2,1)}, bf16[2,1024,128]{2,1,0:T(8,128)(2,1)}, u32[]{:S(2)}, u32[]{:S(2)}) collective-permute-start(bf16[2,1024,128]{2,1,0:T(8,128)(2,1)} %fusion.54), channel_id=1, source_target_pairs={{0,8},{4,12},{8,0},{12,4},{16,24},{20,28},{24,16},{28,20},{1,9},{5... | collective-permute-start | bytes 1572872 | tf_op jit(solution)/shard_map/ppermute | solution.py:325
  670.4 10.4 %copy-start.19 = (f32[2,1408,128]{2,1,0:T(8,128)S(1)}, f32[2,1408,128]{2,1,0:T(8,128)}, u32[]{:S(2)}) copy-start(f32[2,1408,128]{2,1,0:T(8,128)} %copy-done.18) | copy-start | bytes 4325380
  670.4 43.7 %all-to-all-start.2 = ((bf16[8,64,1024]{2,1,0:T(8,128)(2,1)}), bf16[8,64,1024]{2,1,0:T(8,128)(2,1)}, u32[]{:S(2)}, u32[]{:S(2)}) async-start(bf16[8,64,1024]{2,1,0:T(8,128)(2,1)} %bitcast.178), calls=%async_computation.2 | async-start | bytes 2097152 | tf_op jit(solution)/shard_map/all_to_all | solution.py:239
  678.8 18.2 %collective-permute-start.20 = (f32[2,1024]{1,0:T(2,128)S(1)}, f32[2,1024]{1,0:T(2,128)S(1)}, u32[]{:S(2)}, u32[]{:S(2)}) collective-permute-start(f32[2,1024]{1,0:T(2,128)S(1)} %add.283), channel_id=1, source_target_pairs={{0,8},{4,12},{8,0},{12,4},{16,24},{20,28},{24,16},{28,20},{1,9},{5... | collective-permute-start | bytes 24584 | tf_op jit(solution)/shard_map/ppermute | solution.py:373
  697.1 6.6 collective-permute-start.21
  699.4 22.0 %collective-permute-start.16 = (bf16[8,64,1024]{2,1,0:T(8,128)(2,1)}, bf16[8,64,1024]{2,1,0:T(8,128)(2,1)S(1)}, u32[]{:S(2)}, u32[]{:S(2)}) collective-permute-start(bf16[8,64,1024]{2,1,0:T(8,128)(2,1)} %all-to-all-done.3), channel_id=1, source_target_pairs={{0,2},{2,0},{1,3},{3,1},{4,6},{6,4},{5,7},{7,5},{8,10},{10,8},{9,1... | collective-permute-start | bytes 3145736 | tf_op jit(solution)/shard_map/ppermute | solution.py:236
  699.7 11.3 %collective-permute-start.25 = (bf16[1,1024,128]{2,1,0:T(8,128)(2,1)S(1)}, bf16[1,1024,128]{2,1,0:T(8,128)(2,1)S(1)}, u32[]{:S(2)}, u32[]{:S(2)}) collective-permute-start(bf16[1,1024,128]{2,1,0:T(8,128)(2,1)S(1)} %dynamic-slice_convert_fusion.7), channel_id=1, source_target_pairs={{0,16},{4,20},{8,24},{12,28},{16,0},{20,4},{24,8},{28,12},{1,17},{... | collective-permute-start | bytes 786440 | tf_op jit(solution)/shard_map/ppermute | solution.py:325
  (38 other events, 139.8 us)

commit v5 on v4

--- a/solution.py
+++ b/solution.py
@@ -47,7 +47,7 @@
     def _():
         query = q_ref[...] * jnp.asarray(HEAD_DIM**-0.5, LOW)
         queries = [jnp.where(m, query, jnp.zeros_like(query)) for m in masks]
-        above = lax.broadcasted_iota(jnp.int32, (block, block), 0) >= lax.broadcasted_iota(
+        below = lax.broadcasted_iota(jnp.int32, (block, block), 0) <= lax.broadcasted_iota(
             jnp.int32, (block, block), 1
         )
 
@@ -58,26 +58,28 @@
             result = []
             for head in range(2):
                 high, acc = state[head]
-                scores = dot(queries[head], keys, 1, 1)
+                scores = dot(keys, queries[head], 1, 1)
                 if diagonal:
-                    scores = jnp.where(above, scores, NEGATIVE)
-                new_high = jnp.maximum(high, jnp.max(scores, -1, keepdims=True))
+                    scores = jnp.where(below, scores, NEGATIVE)
+                new_high = jnp.maximum(high, jnp.max(scores, 0, keepdims=True))
                 probs = jnp.exp(scores - new_high).astype(LOW)
                 extended = jnp.where(masks[head], values, jnp.ones_like(values))
-                acc = acc * jnp.exp(high - new_high) + dot(probs, extended, 1, 0)
+                acc = acc * jnp.exp(high - new_high) + dot(extended, probs, 0, 0)
                 result.append((new_high, acc))
             return tuple(result)
 
         start_state = tuple(
-            (jnp.full((block, 1), NEGATIVE, F32), jnp.zeros((block, PAIR), F32)) for _ in range(2)
+            (jnp.full((1, block), NEGATIVE, F32), jnp.zeros((PAIR, block), F32)) for _ in range(2)
         )
         state = step(number, start_state, True)
         state = lax.fori_loop(0, number, lambda n, s: step(n, s, False), state)
         (high0, acc0), (high1, acc1) = state
-        sum0 = acc0[:, HEAD_DIM : HEAD_DIM + 1]
-        sum1 = acc1[:, 0:1]
-        o_ref[...] = jnp.where(masks[0], acc0 / sum0, acc1 / sum1).astype(LOW)
-        total_ref[...] = jnp.where(masks[0], high0 + jnp.log(sum0), high1 + jnp.log(sum1))
+        sum0 = acc0[HEAD_DIM : HEAD_DIM + 1]
+        sum1 = acc1[0:1]
+        mixed = jnp.concatenate((acc0[:HEAD_DIM] / sum0, acc1[HEAD_DIM:] / sum1), 0)
+        o_ref[...] = mixed.T.astype(LOW)
+        first = lax.broadcasted_iota(jnp.int32, (PAIR, block), 0) < HEAD_DIM
+        total_ref[...] = jnp.where(first, high0 + jnp.log(sum0), high1 + jnp.log(sum1)).T
 
     @pl.when(number >= info[0])
     def _():
@@ -174,21 +176,22 @@
     dv_ref[...] = dv_acc[...].astype(LOW)
 
 
-def attend_back(info, qkv, grad_out, mixed, totals, block):
+def attend_back(info, qkv, grad_out, mixed, totals, block, first, count):
     rows, width = qkv.shape
     pairs = width // (3 * PAIR)
 
     def column(offset):
-        return pl.BlockSpec((rows, PAIR), lambda h, info: (0, offset + h))
-
-    shape = jax.ShapeDtypeStruct((rows, pairs * PAIR), LOW)
+        return pl.BlockSpec((rows, PAIR), lambda h, info: (0, offset + first + h))
+
+    given = pl.BlockSpec((rows, PAIR), lambda h, info: (0, h))
+    shape = jax.ShapeDtypeStruct((rows, count * PAIR), LOW)
     return pl.pallas_call(
         functools.partial(attend_back_kernel, block),
         grid_spec=pltpu.PrefetchScalarGridSpec(
             num_scalar_prefetch=1,
-            grid=(pairs,),
+            grid=(count,),
             in_specs=[column(0), column(pairs), column(2 * pairs), column(0), column(0), column(0)],
-            out_specs=[column(0)] * 3,
+            out_specs=[given] * 3,
             scratch_shapes=[
                 pltpu.VMEM((block, PAIR), F32),
                 pltpu.VMEM((rows, PAIR), F32),
@@ -345,12 +348,22 @@
     grad_attn = gather(grad_hidden.astype(LOW))
     out_halves = (dot(mixed_near, grad_attn, 0, 0), dot(mixed_far, grad_attn, 0, 0))
     back_far = dot(grad_attn, w_out_far, 1, 1, LOW)
-    grad_far = attend_back(info, qkv[1], back_far, mixed_far, total_far, quarter)
+    grad_far = attend_back(
+        info, qkv[1], back_far, mixed_far, total_far, quarter, 0, mixed_far.shape[1] // PAIR
+    )
     grad_far = jnp.concatenate(grad_far, 1)
     weight_far = dot(grad_far, rows_attn, 0, 0, LOW)
     back_near = after(dot(grad_attn, w_out, 1, 1, LOW), weight_far)
-    grad_near = attend_back(info, qkv[0], back_near, mixed_near, total_near, quarter)
-    grad_near = jnp.concatenate(grad_near, 1)
+    near_pairs = mixed_near.shape[1] // PAIR
+    first_near = attend_back(
+        info, qkv[0], back_near, mixed_near, total_near, quarter, 0, near_pairs // 2
+    )
+    last_near = attend_back(
+        info, qkv[0], back_near, mixed_near, total_near, quarter, near_pairs // 2, near_pairs // 2
+    )
+    grad_near = jnp.concatenate(
+        [part for both in zip(first_near, last_near) for part in both], 1
+    )
     grad_normed_attn = scatter(
         lambda part: dot(grad_near[part], w_qkv, 1, 1) + dot(grad_far[part], w_qkv_far, 1, 1),
     )

time: 738 us -> 742 us (level)
    pallas_call x2 -> x3, Pallas kernels: 72.3 us -> 76.1 us  [attend_back(): pl.pallas_call(functools.partial(attend_back_kernel, block), grid_spec=pl...]
    unnamed x138 -> x157, local copies, waits for them, and re-layouts: 22.2 us -> 24.4 us
where the time goes in v5:
time: 742 us; the launch traced here: 733 us
  waiting for transfers between devices  271 us (37%)
  matrix products  166 us (22%)
  Pallas kernels  131 us (18%)
  local copies, waits for them, and re-layouts  49.1 us (7%)
  other arithmetic  42.5 us (6%)
  starting transfers between devices  38.9 us (5%)
  blocking collectives  29.9 us (4%)
    ppermute x13, waiting for transfers between devices, swap_chip(): return lax.ppermute(value, 'tensor', [(0, 2), (2, 0), (1, 3), (3, 1)])  211 us
    dot_general x28, matrix products, dot(): lax.dot_general(left, right, (((left_dim,), (right_dim,)), ((), ())), pre...  166 us
    pallas_call x3, Pallas kernels, attend_back(): pl.pallas_call(functools.partial(attend_back_kernel, block), grid_spec=pl...  76.1 us
    pallas_call x2, Pallas kernels, attend(): pl.pallas_call(attend_kernel, grid_spec=pltpu.PrefetchScalarGridSpec(num_...  54.5 us
    ppermute x9, waiting for transfers between devices, over_chips(): lax.ppermute(lax.dynamic_index_in_dim(pairs, 1 - side, 1, False).astype(L...  41.1 us
    all_to_all x1, blocking collectives, exchange(): return lax.all_to_all(value, 'dp', split_axis=0, concat_axis=0, tiled=True)  29.9 us
    unnamed x157, local copies, waits for them, and re-layouts  24.4 us
    ppermute x3, waiting for transfers between devices, total_of(): moved = lax.ppermute(value, 'dp', [(i, i ^ step) for i in range(groups)])  16.3 us
  transfers between devices with their start and end apart: 37, of which 18 were waited for; matrix products, arithmetic and copies ran while one was open for 24% of the time, Pallas kernels for 18%

profile of v5, /device:TPU:0, one launch (start us, length us, event | category | flops | bytes accessed | tf_op | source)
XLA Modules:
  0.0 732.7 jit_solution(10678952679540552069)
XLA Ops:
  0.7 2.0 sort.17
  4.6 7.3 all-to-all-start
  15.1 23.3 %collective-permute-done = bf16[8,64,1024]{2,1,0:T(8,128)(2,1)S(1)} collective-permute-done((bf16[8,64,1024]{2,1,0:T(8,128)(2,1)}, bf16[8,64,1024]{2,1,0:T(8,128)(2,1)S(1)}, u32[]{:S(2)}, u32[]{:S(2)}) %collective-permute-start) | collective-permute-done | bytes 1048608 | tf_op jit(solution)/shard_map/ppermute | solution.py:239
  38.4 29.9 %all_to_all.20 = bf16[8,64,1024]{2,1,0:T(8,128)(2,1)S(1)} all-to-all(bf16[8,64,1024]{2,1,0:T(8,128)(2,1)S(1)} %collective-permute-done), channel_id=1, replica_groups=mesh['dp'=8,'tensor'=4] {'dp'}, dimensions={0} | all-to-all | bytes 2097152 | tf_op jit(solution)/shard_map/all_to_all | solution.py:242
  71.5 1.9 constant_dynamic-update-slice_fusion.1
  80.8 7.8 %fusion.86.q_ref.k_ref.v_ref = bf16[2048,768]{1,0:T(8,128)(2,1)} fusion(bf16[1024,768]{1,0:T(8,128)(2,1)} %constant_dynamic-update-slice_fusion, bf16[1024,1024]{1,0:T(8,128)(2,1)} %collective-permute-done.1, bf16[1024,1024]{1,0:T(8,128)(2,1)} %fusion.12), kind=kOutput, calls=%fused_computation.195 | convolution fusion | flops 3229614080 | bytes 8912896 | tf_op jit(solution)/shard_map/dot_general | solution.py:20
  88.6 23.4 %collective-permute-done.2 = bf16[1024,768]{1,0:T(8,128)(2,1)} collective-permute-done((bf16[1024,768]{1,0:T(8,128)(2,1)}, bf16[1024,768]{1,0:T(8,128)(2,1)}, u32[]{:S(2)}, u32[]{:S(2)}) %collective-permute-start.2) | collective-permute-done | bytes 1572896 | tf_op jit(solution)/shard_map/ppermute | solution.py:239
  112.0 7.7 %fusion.85.q_ref.k_ref.v_ref = bf16[2048,768]{1,0:T(8,128)(2,1)} fusion(bf16[1024,768]{1,0:T(8,128)(2,1)} %collective-permute-done.2, bf16[1024,1024]{1,0:T(8,128)(2,1)} %collective-permute-done.1, bf16[1024,1024]{1,0:T(8,128)(2,1)} %fusion.12), kind=kOutput, calls=%fused_computation.194 | convolution fusion | flops 3229614080 | bytes 8912896 | tf_op jit(solution)/shard_map/dot_general | solution.py:20
  119.7 27.2 %attend.3 = (bf16[2048,256]{1,0:T(8,128)(2,1)}, f32[2048,256]{1,0:T(8,128)}) custom-call(s32[5]{0:T(128)} %pad_add_fusion.info, bf16[2048,768]{1,0:T(8,128)(2,1)} %fusion.85.q_ref.k_ref.v_ref, bf16[2048,768]{1,0:T(8,128)(2,1)} %fusion.85.q_ref.k_ref.v_ref, bf16[2048,768]{1,0:T(8,128)(2,1)} %fusion.85.q_ref.k_ref.v_ref), custom_call_target="tpu_custom_call" | custom-call | tf_op jit(solution)/shard_map/attend/pallas_call | solution.py:94
  146.9 27.3 %attend.2 = (bf16[2048,256]{1,0:T(8,128)(2,1)}, f32[2048,256]{1,0:T(8,128)}) custom-call(s32[5]{0:T(128)} %pad_add_fusion.info, bf16[2048,768]{1,0:T(8,128)(2,1)} %fusion.86.q_ref.k_ref.v_ref, bf16[2048,768]{1,0:T(8,128)(2,1)} %fusion.86.q_ref.k_ref.v_ref, bf16[2048,768]{1,0:T(8,128)(2,1)} %fusion.86.q_ref.k_ref.v_ref), custom_call_target="tpu_custom_call" | custom-call | tf_op jit(solution)/shard_map/attend/pallas_call | solution.py:94
  176.9 1.9 add_convert_fusion.2
  180.6 2.5 collective-permute-done.4
  189.1 2.0 collective-permute-start.7
  195.6 40.5 %collective-permute-done.11 = bf16[512,1024]{1,0:T(8,128)(2,1)S(1)} collective-permute-done((bf16[512,1024]{1,0:T(8,128)(2,1)}, bf16[512,1024]{1,0:T(8,128)(2,1)S(1)}, u32[]{:S(2)}, u32[]{:S(2)}) %collective-permute-start.11) | collective-permute-done | bytes 1048608 | tf_op jit(solution)/shard_map/ppermute | solution.py:239
  236.6 2.1 constant_dynamic-update-slice_fusion.3
  238.8 28.3 %collective-permute-done.7 = bf16[1024,704]{0,1:T(8,128)(2,1)} collective-permute-done((bf16[1024,704]{0,1:T(8,128)(2,1)S(1)}, bf16[1024,704]{0,1:T(8,128)(2,1)}, u32[]{:S(2)}, u32[]{:S(2)}) %collective-permute-start.7) | collective-permute-done | bytes 1441824 | tf_op jit(solution)/shard_map/ppermute | solution.py:239
  268.6 28.9 %collective-permute-done.8 = bf16[704,1024]{1,0:T(8,128)(2,1)} collective-permute-done((bf16[704,1024]{1,0:T(8,128)(2,1)}, bf16[704,1024]{1,0:T(8,128)(2,1)}, u32[]{:S(2)}, u32[]{:S(2)}) %collective-permute-start.8) | collective-permute-done | bytes 1441824 | tf_op jit(solution)/shard_map/ppermute | solution.py:239
  300.6 10.9 %fusion.81 = bf16[2048,1408]{1,0:T(8,128)(2,1)} fusion(bf16[1024,1408]{0,1:T(8,128)(2,1)S(1)} %constant_dynamic-update-slice_fusion.5, bf16[1024,1024]{1,0:T(8,128)(2,1)} %collective-permute-done.5, bf16[1024,1024]{1,0:T(8,128)(2,1)} %multiply_convert_fusion.2), kind=kOutput, calls=%fused_computation.190 | convolution fusion | flops 5913968640 | bytes 12845056 | tf_op jit(solution)/shard_map/dot_general | solution.py:20
  311.4 11.2 %fusion.82 = bf16[2048,1408]{1,0:T(8,128)(2,1)} fusion(bf16[1024,1408]{0,1:T(8,128)(2,1)S(1)} %constant_dynamic-update-slice_fusion.3, bf16[1024,1024]{1,0:T(8,128)(2,1)} %collective-permute-done.5, bf16[1024,1024]{1,0:T(8,128)(2,1)} %multiply_convert_fusion.2), kind=kOutput, calls=%fused_computation.191 | convolution fusion | flops 5913968640 | bytes 12845056 | tf_op jit(solution)/shard_map/dot_general | solution.py:20
  322.6 19.2 %fusion.3 = (bf16[2048,1408]{1,0:T(8,128)(2,1)}, bf16[2048,1408]{1,0:T(8,128)(2,1)}, bf16[2048,1408]{1,0:T(8,128)(2,1)}) fusion(bf16[2048,1408]{1,0:T(8,128)(2,1)} %fusion.81, bf16[2048,1408]{1,0:T(8,128)(2,1)} %fusion.82, bf16[1408,1024]{1,0:T(8,128)(2,1)} %copy-done.34, bf16[1024,1024]{1,0:T(8,128)(2,1)} %collective-permute-done.12, ...), kind=kOutput, calls=%fused_computation.11 | convolution fusion | flops 5962989568 | bytes 35913728 | tf_op jit(solution)/shard_map/dot_general | solution.py:20
  341.8 8.3 %fusion.22 = f32[1024,1024]{1,0:T(8,128)} fusion(bf16[1024,1408]{0,1:T(8,128)(2,1)} %copy-done.37, bf16[2048,1408]{1,0:T(8,128)(2,1)} %get-tuple-element.111), kind=kOutput, calls=%fused_computation.62 | convolution fusion | flops 2952790016 | bytes 9961472 | tf_op jit(solution)/shard_map/dot_general | solution.py:20
  350.1 9.3 %fusion.79 = f32[1408,1024]{1,0:T(8,128)S(1)} fusion(bf16[2048,1408]{1,0:T(8,128)(2,1)S(1)} %copy-done.63, bf16[1024,1024]{1,0:T(8,128)(2,1)} %collective-permute-done.5, bf16[1024,1024]{1,0:T(8,128)(2,1)} %multiply_convert_fusion.2), kind=kOutput, calls=%fused_computation.188 | convolution fusion | flops 5913968640 | bytes 15728640 | tf_op jit(solution)/shard_map/dot_general | solution.py:20
  359.6 2.6 copy-done.12
  362.2 9.4 %fusion.80 = f32[1408,1024]{1,0:T(8,128)S(1)} fusion(bf16[2048,1408]{1,0:T(8,128)(2,1)S(1)} %bitcast.192, bf16[1024,1024]{1,0:T(8,128)(2,1)} %collective-permute-done.5, bf16[1024,1024]{1,0:T(8,128)(2,1)} %multiply_convert_fusion.2), kind=kOutput, calls=%fused_computation.189 | convolution fusion | flops 5913968640 | bytes 15728640 | tf_op jit(solution)/shard_map/dot_general | solution.py:20
  371.8 2.6 copy-done.13
  375.5 4.8 fusion.36
  380.3 8.0 %fusion.34 = f32[1408,1024]{1,0:T(8,128)S(1)} fusion(bf16[2048,1408]{1,0:T(8,128)(2,1)S(1)} %bitcast.194, bf16[1024,1024]{1,0:T(8,128)(2,1)} %collective-permute-done.12, bf16[1024,1024]{1,0:T(8,128)(2,1)S(1)} %copy-done.29), kind=kOutput, calls=%fused_computation.77 | convolution fusion | flops 5913968640 | bytes 15728640 | tf_op jit(solution)/shard_map/dot_general | solution.py:20
  388.9 4.7 add_convert_fusion.1
  396.2 5.2 fusion.28
  401.4 5.2 fusion.26
  406.7 16.3 %collective-permute-done.30 = bf16[704,1024]{1,0:T(8,128)(2,1)S(1)} collective-permute-done((bf16[704,1024]{1,0:T(8,128)(2,1)S(1)}, bf16[704,1024]{1,0:T(8,128)(2,1)S(1)}, u32[]{:S(2)}, u32[]{:S(2)}) %collective-permute-start.30) | collective-permute-done | bytes 1441824 | tf_op jit(solution)/shard_map/ppermute | solution.py:239
  425.0 2.2 multiply_reduce_fusion
  427.4 3.8 fusion.87
  431.2 7.7 %collective-permute-done.31 = bf16[4,704,128]{2,1,0:T(8,128)(2,1)S(1)} collective-permute-done((bf16[4,704,128]{2,1,0:T(8,128)(2,1)S(1)}, bf16[4,704,128]{2,1,0:T(8,128)(2,1)S(1)}, u32[]{:S(2)}, u32[]{:S(2)}) %collective-permute-start.31) | collective-permute-done | bytes 720928 | tf_op jit(solution)/shard_map/ppermute | solution.py:328
  440.3 5.9 multiply_convert_fusion.1
  449.4 6.2 collective-permute-done.33
  456.4 28.5 %collective-permute-done.26 = bf16[1408,1024]{1,0:T(8,128)(2,1)S(1)} collective-permute-done((bf16[1408,1024]{1,0:T(8,128)(2,1)S(1)}, bf16[1408,1024]{1,0:T(8,128)(2,1)S(1)}, u32[]{:S(2)}, u32[]{:S(2)}) %collective-permute-start.26) | collective-permute-done | bytes 2883616 | tf_op jit(solution)/shard_map/ppermute | solution.py:239
  488.4 3.9 fusion.77.do_ref
  492.3 36.1 %attend_back.3 = (bf16[2048,256]{1,0:T(8,128)(2,1)}, bf16[2048,256]{1,0:T(8,128)(2,1)}, bf16[2048,256]{1,0:T(8,128)(2,1)}) custom-call(s32[5]{0:T(128)} %pad_add_fusion.info, bf16[2048,768]{1,0:T(8,128)(2,1)} %fusion.85.q_ref.k_ref.v_ref, bf16[2048,768]{1,0:T(8,128)(2,1)} %fusion.85.q_ref.k_ref.v_ref, bf16[2048,768]{1,0:T(8,128)(2,1)} %fusion.85.q_ref.k_ref.v_ref, ...), custom_call_target="tpu_custom_call" | custom-call | tf_op jit(solution)/shard_map/attend_back/pallas_call | solution.py:188
  531.2 5.0 fusion.78.do_ref
  536.2 7.2 fusion.84
  543.5 19.9 %attend_back.5 = (bf16[2048,128]{1,0:T(8,128)(2,1)}, bf16[2048,128]{1,0:T(8,128)(2,1)}, bf16[2048,128]{1,0:T(8,128)(2,1)}) custom-call(s32[5]{0:T(128)} %pad_add_fusion.info, bf16[2048,768]{1,0:T(8,128)(2,1)} %fusion.86.q_ref.k_ref.v_ref, bf16[2048,768]{1,0:T(8,128)(2,1)} %fusion.86.q_ref.k_ref.v_ref, bf16[2048,768]{1,0:T(8,128)(2,1)} %fusion.86.q_ref.k_ref.v_ref, ...), custom_call_target="tpu_custom_call" | custom-call | tf_op jit(solution)/shard_map/attend_back/pallas_call | solution.py:188
  563.4 20.1 %attend_back.4 = (bf16[2048,128]{1,0:T(8,128)(2,1)}, bf16[2048,128]{1,0:T(8,128)(2,1)}, bf16[2048,128]{1,0:T(8,128)(2,1)}) custom-call(s32[5]{0:T(128)} %pad_add_fusion.info, bf16[2048,768]{1,0:T(8,128)(2,1)} %fusion.86.q_ref.k_ref.v_ref, bf16[2048,768]{1,0:T(8,128)(2,1)} %fusion.86.q_ref.k_ref.v_ref, bf16[2048,768]{1,0:T(8,128)(2,1)} %fusion.86.q_ref.k_ref.v_ref, ...), custom_call_target="tpu_custom_call" | custom-call | tf_op jit(solution)/shard_map/attend_back/pallas_call | solution.py:188
  586.5 3.2 fusion.44
  589.8 3.3 fusion.48
  593.1 3.0 convolution_convert_fusion
  598.7 3.2 add_convert_fusion
  602.1 3.9 fusion.76
  606.0 3.4 fusion.46
  609.4 7.5 %fusion.83 = f32[768,1024]{1,0:T(8,128)} fusion(bf16[2048,768]{1,0:T(8,128)(2,1)S(1)} %constant_dynamic-update-slice_fusion.12, bf16[1024,1024]{1,0:T(8,128)(2,1)} %collective-permute-done.1, bf16[1024,1024]{1,0:T(8,128)(2,1)} %fusion.12), kind=kOutput, calls=%fused_computation.192 | convolution fusion | flops 3229614080 | bytes 10485760 | tf_op jit(solution)/shard_map/dot_general | solution.py:20
  620.3 2.8 fusion.19
  626.5 4.3 all-to-all-start.3
  630.8 11.7 %collective-permute-done.22 = bf16[1024,1024]{1,0:T(8,128)(2,1)} collective-permute-done((bf16[1024,1024]{1,0:T(8,128)(2,1)}, bf16[1024,1024]{1,0:T(8,128)(2,1)}, u32[]{:S(2)}, u32[]{:S(2)}) %collective-permute-start.22) | collective-permute-done | bytes 2097184 | tf_op jit(solution)/shard_map/ppermute | solution.py:239
  642.5 3.2 copy_bitcast_fusion.1
  649.7 2.5 collective-permute-done.18
  653.1 19.6 %collective-permute-done.23 = bf16[4,1024,128]{2,1,0:T(8,128)(2,1)S(1)} collective-permute-done((bf16[4,1024,128]{2,1,0:T(8,128)(2,1)S(1)}, bf16[4,1024,128]{2,1,0:T(8,128)(2,1)S(1)}, u32[]{:S(2)}, u32[]{:S(2)}) %collective-permute-start.23) | collective-permute-done | bytes 1048608 | tf_op jit(solution)/shard_map/ppermute | solution.py:328
  674.7 4.4 all-to-all-start.2
  679.0 4.0 maximum_select_fusion
  683.1 2.0 collective-permute-start.20
  686.1 15.1 %collective-permute-done.20 = f32[2,1024]{1,0:T(2,128)S(1)} collective-permute-done((f32[2,1024]{1,0:T(2,128)S(1)}, f32[2,1024]{1,0:T(2,128)S(1)}, u32[]{:S(2)}, u32[]{:S(2)}) %collective-permute-start.20) | collective-permute-done | bytes 8224 | tf_op jit(solution)/shard_map/ppermute | solution.py:386
  708.5 6.7 collective-permute-done.25
  718.2 7.2 collective-permute-done.16
  725.5 3.3 maximum_select_fusion.1
  728.7 3.7 gather_fusion.2
  (286 shorter events, 81.7 us)
Async XLA Ops:
  4.6 33.7 %all-to-all-start = ((bf16[8,64,1024]{2,1,0:T(8,128)(2,1)}), bf16[8,64,1024]{2,1,0:T(8,128)(2,1)S(1)}, u32[]{:S(2)}, u32[]{:S(2)}) async-start(bf16[8,64,1024]{2,1,0:T(8,128)(2,1)} %gather_fusion), calls=%async_computation | async-start | bytes 2097152 | tf_op jit(solution)/shard_map/all_to_all | solution.py:242
  11.9 56.9 %copy-start.53 = (f32[1024]{0:T(1024)S(1)}, f32[1024]{0:T(1024)}, u32[]{:S(2)}) copy-start(f32[1024]{0:T(1024)} %param.20) | copy-start | bytes 12292
  13.5 24.8 %collective-permute-start = (bf16[8,64,1024]{2,1,0:T(8,128)(2,1)}, bf16[8,64,1024]{2,1,0:T(8,128)(2,1)S(1)}, u32[]{:S(2)}, u32[]{:S(2)}) collective-permute-start(bf16[8,64,1024]{2,1,0:T(8,128)(2,1)} %gather_fusion.1), channel_id=1, source_target_pairs={{0,2},{2,0},{1,3},{3,1},{4,6},{6,4},{5,7},{7,5},{8,10},{10,8},{9,1... | collective-permute-start | bytes 3145736 | tf_op jit(solution)/shard_map/ppermute | solution.py:239
  38.4 144.7 %copy-start.4 = (bf16[8,64,1024]{2,1,0:T(8,128)(2,1)}, bf16[8,64,1024]{2,1,0:T(8,128)(2,1)S(1)}, u32[]{:S(2)}) copy-start(bf16[8,64,1024]{2,1,0:T(8,128)(2,1)S(1)} %all-to-all-done) | copy-start | bytes 3145732
  68.2 114.8 %copy-start.6 = (bf16[8,64,1024]{2,1,0:T(8,128)(2,1)}, bf16[8,64,1024]{2,1,0:T(8,128)(2,1)S(1)}, u32[]{:S(2)}) copy-start(bf16[8,64,1024]{2,1,0:T(8,128)(2,1)S(1)} %all_to_all.20) | copy-start | bytes 3145732
  68.8 230.1 %copy-start.49 = (f32[1024]{0:T(1024)}, f32[1024]{0:T(1024)S(1)}, u32[]{:S(2)}) copy-start(f32[1024]{0:T(1024)S(1)} %rsqrt.26) | copy-start | bytes 12292
  68.8 10.1 %copy-start.61 = (s32[16]{0:T(128)S(1)}, s32[16]{0:T(128)}, u32[]{:S(2)}) copy-start(s32[16]{0:T(128)} %param.18) | copy-start | bytes 196
  70.7 10.1 %collective-permute-start.1 = (bf16[1024,1024]{1,0:T(8,128)(2,1)}, bf16[1024,1024]{1,0:T(8,128)(2,1)}, u32[]{:S(2)}, u32[]{:S(2)}) collective-permute-start(bf16[1024,1024]{1,0:T(8,128)(2,1)} %fusion.12), channel_id=1, source_target_pairs={{0,1},{1,0},{2,3},{3,2},{4,5},{5,4},{6,7},{7,6},{8,9},{9,8},{10,11... | collective-permute-start | bytes 6291464 | tf_op jit(solution)/shard_map/ppermute | solution.py:236
  74.4 37.6 %collective-permute-start.2 = (bf16[1024,768]{1,0:T(8,128)(2,1)}, bf16[1024,768]{1,0:T(8,128)(2,1)}, u32[]{:S(2)}, u32[]{:S(2)}) collective-permute-start(bf16[1024,768]{1,0:T(8,128)(2,1)} %constant_dynamic-update-slice_fusion), channel_id=1, source_target_pairs={{0,2},{2,0},{1,3},{3,1},{4,6},{6,4},{5,7},{7,5},{8,10},{10,8},{9,1... | collective-permute-start | bytes 4718600 | tf_op jit(solution)/shard_map/ppermute | solution.py:239
  75.9 100.1 %collective-permute-start.3 = (bf16[256,1024]{1,0:T(8,128)(2,1)S(1)}, bf16[256,1024]{1,0:T(8,128)(2,1)S(1)}, u32[]{:S(2)}, u32[]{:S(2)}) collective-permute-start(bf16[256,1024]{1,0:T(8,128)(2,1)S(1)} %copy-done.25), channel_id=1, source_target_pairs={{0,2},{2,0},{1,3},{3,1},{4,6},{6,4},{5,7},{7,5},{8,10},{10,8},{9,1... | collective-permute-start | bytes 1572872 | tf_op jit(solution)/shard_map/ppermute | solution.py:239
  178.8 4.2 collective-permute-start.4
  178.9 57.7 %collective-permute-start.6 = (bf16[1024,704]{0,1:T(8,128)(2,1)}, bf16[1024,704]{0,1:T(8,128)(2,1)}, u32[]{:S(2)}, u32[]{:S(2)}) collective-permute-start(bf16[1024,704]{0,1:T(8,128)(2,1)} %param.26), channel_id=1, source_target_pairs={{0,2},{2,0},{1,3},{3,1},{4,6},{6,4},{5,7},{7,5},{8,10},{10,8},{9,1... | collective-permute-start | bytes 4325384 | tf_op jit(solution)/shard_map/ppermute | solution.py:239
  187.0 113.6 %collective-permute-start.5 = (bf16[1024,1024]{1,0:T(8,128)(2,1)}, bf16[1024,1024]{1,0:T(8,128)(2,1)}, u32[]{:S(2)}, u32[]{:S(2)}) collective-permute-start(bf16[1024,1024]{1,0:T(8,128)(2,1)} %multiply_convert_fusion.2), channel_id=1, source_target_pairs={{0,1},{1,0},{2,3},{3,2},{4,5},{5,4},{6,7},{7,6},{8,9},{9,8},{10,11... | collective-permute-start | bytes 6291464 | tf_op jit(solution)/shard_map/ppermute | solution.py:236
  189.1 47.0 %copy-start.14 = (bf16[512,1024]{1,0:T(8,128)(2,1)}, bf16[512,1024]{1,0:T(8,128)(2,1)S(1)}, u32[]{:S(2)}) copy-start(bf16[512,1024]{1,0:T(8,128)(2,1)S(1)} %get-tuple-element.115) | copy-start | bytes 3145732
  189.1 47.0 %collective-permute-start.11 = (bf16[512,1024]{1,0:T(8,128)(2,1)}, bf16[512,1024]{1,0:T(8,128)(2,1)S(1)}, u32[]{:S(2)}, u32[]{:S(2)}) collective-permute-start(bf16[512,1024]{1,0:T(8,128)(2,1)} %get-tuple-element.116), channel_id=1, source_target_pairs={{0,2},{2,0},{1,3},{3,1},{4,6},{6,4},{5,7},{7,5},{8,10},{10,8},{9,1... | collective-permute-start | bytes 3145736 | tf_op jit(solution)/shard_map/ppermute | solution.py:239
  189.1 78.0 %collective-permute-start.7 = (bf16[1024,704]{0,1:T(8,128)(2,1)S(1)}, bf16[1024,704]{0,1:T(8,128)(2,1)}, u32[]{:S(2)}, u32[]{:S(2)}) collective-permute-start(bf16[1024,704]{0,1:T(8,128)(2,1)S(1)} %copy-done.32), channel_id=1, source_target_pairs={{0,2},{2,0},{1,3},{3,1},{4,6},{6,4},{5,7},{7,5},{8,10},{10,8},{9,1... | collective-permute-start | bytes 4325384 | tf_op jit(solution)/shard_map/ppermute | solution.py:239
  191.2 106.3 %collective-permute-start.8 = (bf16[704,1024]{1,0:T(8,128)(2,1)}, bf16[704,1024]{1,0:T(8,128)(2,1)}, u32[]{:S(2)}, u32[]{:S(2)}) collective-permute-start(bf16[704,1024]{1,0:T(8,128)(2,1)} %param.28), channel_id=1, source_target_pairs={{0,2},{2,0},{1,3},{3,1},{4,6},{6,4},{5,7},{7,5},{8,10},{10,8},{9,1... | collective-permute-start | bytes 4325384 | tf_op jit(solution)/shard_map/ppermute | solution.py:239
  192.5 43.6 %copy-start.55 = (f32[1024]{0:T(1024)}, f32[1024]{0:T(1024)S(1)}, u32[]{:S(2)}) copy-start(f32[1024]{0:T(1024)S(1)} %fusion.67) | copy-start | bytes 12292
  236.5 62.4 %copy-start.28 = (bf16[1024,1024]{1,0:T(8,128)(2,1)}, bf16[1024,1024]{1,0:T(8,128)(2,1)S(1)}, u32[]{:S(2)}) copy-start(bf16[1024,1024]{1,0:T(8,128)(2,1)S(1)} %fusion.20) | copy-start | bytes 6291460
  236.5 86.1 %collective-permute-start.12 = (bf16[1024,1024]{1,0:T(8,128)(2,1)S(1)}, bf16[1024,1024]{1,0:T(8,128)(2,1)}, u32[]{:S(2)}, u32[]{:S(2)}) collective-permute-start(bf16[1024,1024]{1,0:T(8,128)(2,1)S(1)} %fusion.20), channel_id=1, source_target_pairs={{0,1},{1,0},{2,3},{3,2},{4,5},{5,4},{6,7},{7,6},{8,9},{9,8},{10,11... | collective-permute-start | bytes 6291464 | tf_op jit(solution)/shard_map/ppermute | solution.py:236
  238.8 72.7 %copy-start.39 = (bf16[1024,1408]{0,1:T(8,128)(2,1)}, bf16[1024,1408]{0,1:T(8,128)(2,1)S(1)}, u32[]{:S(2)}) copy-start(bf16[1024,1408]{0,1:T(8,128)(2,1)S(1)} %constant_dynamic-update-slice_fusion.3) | copy-start | bytes 8650756
  268.6 42.9 %copy-start.37 = (bf16[1024,1408]{0,1:T(8,128)(2,1)}, bf16[1024,1408]{0,1:T(8,128)(2,1)S(1)}, u32[]{:S(2)}) copy-start(bf16[1024,1408]{0,1:T(8,128)(2,1)S(1)} %constant_dynamic-update-slice_fusion.5) | copy-start | bytes 8650756
  311.4 11.2 %copy-start.29 = (bf16[1024,1024]{1,0:T(8,128)(2,1)S(1)}, bf16[1024,1024]{1,0:T(8,128)(2,1)}, u32[]{:S(2)}) copy-start(bf16[1024,1024]{1,0:T(8,128)(2,1)} %copy-done.28) | copy-start | bytes 6291460
  341.8 20.4 %slice-start.4 = ((s8[5767168]{0:T(1024)(128)(4,1)}), s8[4194304]{0:T(1024)(128)(4,1)S(1)}, s32[]{:S(2)}) async-start(s8[5767168]{0:T(1024)(128)(4,1)} %bitcast.191), calls=%async_computation.8 | async-start | bytes 8388608
  350.1 12.1 %slice-start.5 = ((s8[5767168]{0:T(1024)(128)(4,1)}), s8[1572864]{0:T(1024)(128)(4,1)S(1)}, s32[]{:S(2)}) async-start(s8[5767168]{0:T(1024)(128)(4,1)} %bitcast.191), calls=%async_computation.9 | async-start | bytes 3145728
  359.6 14.8 %slice-start.6 = ((s8[5767168]{0:T(1024)(128)(4,1)}), s8[4194304]{0:T(1024)(128)(4,1)S(1)}, s32[]{:S(2)}) async-start(s8[5767168]{0:T(1024)(128)(4,1)} %bitcast.193), calls=%async_computation.10 | async-start | bytes 8388608
  362.2 12.2 %slice-start.7 = ((s8[5767168]{0:T(1024)(128)(4,1)}), s8[1572864]{0:T(1024)(128)(4,1)S(1)}, s32[]{:S(2)}) async-start(s8[5767168]{0:T(1024)(128)(4,1)} %bitcast.193), calls=%async_computation.11 | async-start | bytes 3145728
  380.3 8.7 %copy-start.40 = (bf16[1024,1408]{0,1:T(8,128)(2,1)S(1)}, bf16[1024,1408]{0,1:T(8,128)(2,1)}, u32[]{:S(2)}) copy-start(bf16[1024,1408]{0,1:T(8,128)(2,1)} %copy-done.39) | copy-start | bytes 8650756
  380.3 8.7 %copy-start.64 = (f32[1024,1024]{1,0:T(8,128)S(1)}, f32[1024,1024]{1,0:T(8,128)}, u32[]{:S(2)}) copy-start(f32[1024,1024]{1,0:T(8,128)} %fusion.22) | copy-start | bytes 12582916
  388.5 34.5 %collective-permute-start.30 = (bf16[704,1024]{1,0:T(8,128)(2,1)S(1)}, bf16[704,1024]{1,0:T(8,128)(2,1)S(1)}, u32[]{:S(2)}, u32[]{:S(2)}) collective-permute-start(bf16[704,1024]{1,0:T(8,128)(2,1)S(1)} %slice.253), channel_id=1, source_target_pairs={{0,2},{2,0},{1,3},{3,1},{4,6},{6,4},{5,7},{7,5},{8,10},{10,8},{9,1... | collective-permute-start | bytes 4325384 | tf_op jit(solution)/shard_map/ppermute | solution.py:239
  388.9 51.4 %collective-permute-start.9 = (bf16[1024,1024]{1,0:T(8,128)(2,1)}, bf16[1024,1024]{1,0:T(8,128)(2,1)}, u32[]{:S(2)}, u32[]{:S(2)}) collective-permute-start(bf16[1024,1024]{1,0:T(8,128)(2,1)} %fusion.36), channel_id=1, source_target_pairs={{0,1},{1,0},{2,3},{3,2},{4,5},{5,4},{6,7},{7,6},{8,9},{9,8},{10,11... | collective-permute-start | bytes 6291464 | tf_op jit(solution)/shard_map/ppermute | solution.py:236
  393.6 31.4 %collective-permute-start.13 = (bf16[1024,1024]{1,0:T(8,128)(2,1)}, bf16[1024,1024]{1,0:T(8,128)(2,1)S(1)}, u32[]{:S(2)}, u32[]{:S(2)}) collective-permute-start(bf16[1024,1024]{1,0:T(8,128)(2,1)} %add_convert_fusion.1), channel_id=1, source_target_pairs={{0,1},{1,0},{2,3},{3,2},{4,5},{5,4},{6,7},{7,6},{8,9},{9,8},{10,11... | collective-permute-start | bytes 6291464 | tf_op jit(solution)/shard_map/ppermute | solution.py:236
  394.4 90.5 %collective-permute-start.26 = (bf16[1408,1024]{1,0:T(8,128)(2,1)S(1)}, bf16[1408,1024]{1,0:T(8,128)(2,1)S(1)}, u32[]{:S(2)}, u32[]{:S(2)}) collective-permute-start(bf16[1408,1024]{1,0:T(8,128)(2,1)S(1)} %pad_maximum_fusion.4), channel_id=1, source_target_pairs={{0,2},{2,0},{1,3},{3,1},{4,6},{6,4},{5,7},{7,5},{8,10},{10,8},{9,1... | collective-permute-start | bytes 8650760 | tf_op jit(solution)/shard_map/ppermute | solution.py:239
  406.7 18.3 %copy-start.3 = (f32[1024,1024]{1,0:T(8,128)S(1)}, f32[1024,1024]{1,0:T(8,128)}, u32[]{:S(2)}) copy-start(f32[1024,1024]{1,0:T(8,128)} %copy-done.2) | copy-start | bytes 12582916
  406.7 18.3 %copy-start.52 = (f32[1024]{0:T(1024)S(1)}, f32[1024]{0:T(1024)}, u32[]{:S(2)}) copy-start(f32[1024]{0:T(1024)} %copy-done.51) | copy-start | bytes 12292
  406.7 18.3 %copy-start.58 = (f32[1024]{0:T(1024)S(1)}, f32[1024]{0:T(1024)}, u32[]{:S(2)}) copy-start(f32[1024]{0:T(1024)} %param.25) | copy-start | bytes 12292
  423.5 15.4 %collective-permute-start.31 = (bf16[4,704,128]{2,1,0:T(8,128)(2,1)S(1)}, bf16[4,704,128]{2,1,0:T(8,128)(2,1)S(1)}, u32[]{:S(2)}, u32[]{:S(2)}) collective-permute-start(bf16[4,704,128]{2,1,0:T(8,128)(2,1)S(1)} %fusion.53), channel_id=1, source_target_pairs={{0,4},{4,0},{8,12},{12,8},{16,20},{20,16},{24,28},{28,24},{1,5},{5... | collective-permute-start | bytes 2162696 | tf_op jit(solution)/shard_map/ppermute | solution.py:328
  431.2 9.1 %copy-start.36 = (bf16[1408,1024]{1,0:T(8,128)(2,1)S(1)}, bf16[1408,1024]{1,0:T(8,128)(2,1)}, u32[]{:S(2)}) copy-start(bf16[1408,1024]{1,0:T(8,128)(2,1)} %copy-done.34) | copy-start | bytes 8650756
  431.2 57.2 %collective-permute-start.14 = (bf16[1024,1024]{1,0:T(8,128)(2,1)S(1)}, bf16[1024,1024]{1,0:T(8,128)(2,1)}, u32[]{:S(2)}, u32[]{:S(2)}) collective-permute-start(bf16[1024,1024]{1,0:T(8,128)(2,1)S(1)} %get-tuple-element.105), channel_id=1, source_target_pairs={{0,1},{1,0},{2,3},{3,2},{4,5},{5,4},{6,7},{7,6},{8,9},{9,8},{10,11... | collective-permute-start | bytes 6291464 | tf_op jit(solution)/shard_map/ppermute | solution.py:236
  439.1 8.0 %collective-permute-start.32 = (bf16[2,704,128]{2,1,0:T(8,128)(2,1)S(1)}, bf16[2,704,128]{2,1,0:T(8,128)(2,1)S(1)}, u32[]{:S(2)}, u32[]{:S(2)}) collective-permute-start(bf16[2,704,128]{2,1,0:T(8,128)(2,1)S(1)} %fusion.62), channel_id=1, source_target_pairs={{0,8},{4,12},{8,0},{12,4},{16,24},{20,28},{24,16},{28,20},{1,9},{5... | collective-permute-start | bytes 1081352 | tf_op jit(solution)/shard_map/ppermute | solution.py:328
  447.1 37.8 %slice-start.3 = ((f32[1408,1024]{1,0:T(8,128)}), f32[704,1024]{1,0:T(8,128)S(1)}, s32[]{:S(2)}) async-start(f32[1408,1024]{1,0:T(8,128)} %copy-done.13), calls=%async_computation.7 | async-start | bytes 5767168 | tf_op jit(solution)/shard_map/slice | solution.py:338
  447.2 37.7 %slice-start.2 = ((f32[1408,1024]{1,0:T(8,128)}), f32[704,1024]{1,0:T(8,128)S(1)}, s32[]{:S(2)}) async-start(f32[1408,1024]{1,0:T(8,128)} %copy-done.12), calls=%async_computation.6 | async-start | bytes 5767168 | tf_op jit(solution)/shard_map/slice | solution.py:338
  447.2 8.4 %collective-permute-start.33 = (bf16[1,704,128]{2,1,0:T(8,128)(2,1)S(1)}, bf16[1,704,128]{2,1,0:T(8,128)(2,1)S(1)}, u32[]{:S(2)}, u32[]{:S(2)}) collective-permute-start(bf16[1,704,128]{2,1,0:T(8,128)(2,1)S(1)} %dynamic-slice_convert_fusion.8), channel_id=1, source_target_pairs={{0,16},{4,20},{8,24},{12,28},{16,0},{20,4},{24,8},{28,12},{1,17},{... | collective-permute-start | bytes 540680 | tf_op jit(solution)/shard_map/ppermute | solution.py:328
  448.8 230.2 %collective-permute-start.10 = (bf16[512,1024]{1,0:T(8,128)(2,1)}, bf16[512,1024]{1,0:T(8,128)(2,1)}, u32[]{:S(2)}, u32[]{:S(2)}) collective-permute-start(bf16[512,1024]{1,0:T(8,128)(2,1)} %get-tuple-element.118), channel_id=1, source_target_pairs={{0,2},{2,0},{1,3},{3,1},{4,6},{6,4},{5,7},{7,5},{8,10},{10,8},{9,1... | collective-permute-start | bytes 3145736 | tf_op jit(solution)/shard_map/ppermute | solution.py:239
  456.4 32.1 %copy-start.24 = (bf16[256,1024]{1,0:T(8,128)(2,1)S(1)}, bf16[256,1024]{1,0:T(8,128)(2,1)}, u32[]{:S(2)}) copy-start(bf16[256,1024]{1,0:T(8,128)(2,1)} %copy-done.22) | copy-start | bytes 1572868
  487.0 129.9 %collective-permute-start.27 = (bf16[4,1408,128]{2,1,0:T(8,128)(2,1)}, bf16[4,1408,128]{2,1,0:T(8,128)(2,1)}, u32[]{:S(2)}, u32[]{:S(2)}) collective-permute-start(bf16[4,1408,128]{2,1,0:T(8,128)(2,1)} %fusion.50), channel_id=1, source_target_pairs={{0,4},{4,0},{8,12},{12,8},{16,20},{20,16},{24,28},{28,24},{1,5},{5... | collective-permute-start | bytes 4325384 | tf_op jit(solution)/shard_map/ppermute | solution.py:328
  563.4 21.4 %copy-start.46 = (bf16[2048,128]{1,0:T(8,128)(2,1)S(1)}, bf16[2048,128]{1,0:T(8,128)(2,1)}, u32[]{:S(2)}) copy-start(bf16[2048,128]{1,0:T(8,128)(2,1)} %get-tuple-element.38) | copy-start | bytes 1572868
  597.6 44.9 %collective-permute-start.22 = (bf16[1024,1024]{1,0:T(8,128)(2,1)}, bf16[1024,1024]{1,0:T(8,128)(2,1)}, u32[]{:S(2)}, u32[]{:S(2)}) collective-permute-start(bf16[1024,1024]{1,0:T(8,128)(2,1)} %pad_maximum_fusion.9), channel_id=1, source_target_pairs={{0,2},{2,0},{1,3},{3,1},{4,6},{6,4},{5,7},{7,5},{8,10},{10,8},{9,1... | collective-permute-start | bytes 6291464 | tf_op jit(solution)/shard_map/ppermute | solution.py:239
  602.0 18.3 %collective-permute-start.15 = (bf16[1024,1024]{1,0:T(8,128)(2,1)S(1)}, bf16[1024,1024]{1,0:T(8,128)(2,1)S(1)}, u32[]{:S(2)}, u32[]{:S(2)}) collective-permute-start(bf16[1024,1024]{1,0:T(8,128)(2,1)S(1)} %add_convert_fusion), channel_id=1, source_target_pairs={{0,1},{1,0},{2,3},{3,2},{4,5},{5,4},{6,7},{7,6},{8,9},{9,8},{10,11... | collective-permute-start | bytes 6291464 | tf_op jit(solution)/shard_map/ppermute | solution.py:236
  606.0 10.9 %slice-start = ((s8[5767168]{0:T(1024)(128)(4,1)}), s8[4194304]{0:T(1024)(128)(4,1)S(1)}, s32[]{:S(2)}) async-start(s8[5767168]{0:T(1024)(128)(4,1)} %bitcast.164), calls=%async_computation.4 | async-start | bytes 8388608
  619.6 27.6 %collective-permute-start.28 = (bf16[2,1408,128]{2,1,0:T(8,128)(2,1)}, bf16[2,1408,128]{2,1,0:T(8,128)(2,1)}, u32[]{:S(2)}, u32[]{:S(2)}) collective-permute-start(bf16[2,1408,128]{2,1,0:T(8,128)(2,1)} %fusion.52), channel_id=1, source_target_pairs={{0,8},{4,12},{8,0},{12,4},{16,24},{20,28},{24,16},{28,20},{1,9},{5... | collective-permute-start | bytes 2162696 | tf_op jit(solution)/shard_map/ppermute | solution.py:328
  626.5 48.2 %all-to-all-start.3 = ((bf16[8,64,1024]{2,1,0:T(8,128)(2,1)}), bf16[8,64,1024]{2,1,0:T(8,128)(2,1)}, u32[]{:S(2)}, u32[]{:S(2)}) async-start(bf16[8,64,1024]{2,1,0:T(8,128)(2,1)} %bitcast.179), calls=%async_computation.3 | async-start | bytes 2097152 | tf_op jit(solution)/shard_map/all_to_all | solution.py:242
  645.9 26.8 %collective-permute-start.23 = (bf16[4,1024,128]{2,1,0:T(8,128)(2,1)S(1)}, bf16[4,1024,128]{2,1,0:T(8,128)(2,1)S(1)}, u32[]{:S(2)}, u32[]{:S(2)}) collective-permute-start(bf16[4,1024,128]{2,1,0:T(8,128)(2,1)S(1)} %fusion.51), channel_id=1, source_target_pairs={{0,4},{4,0},{8,12},{12,8},{16,20},{20,16},{24,28},{28,24},{1,5},{5... | collective-permute-start | bytes 3145736 | tf_op jit(solution)/shard_map/ppermute | solution.py:328
  647.2 1.3 collective-permute-start.17
  648.6 3.7 collective-permute-start.18
  649.7 35.3 %collective-permute-start.29 = (bf16[1,1408,128]{2,1,0:T(8,128)(2,1)}, bf16[1,1408,128]{2,1,0:T(8,128)(2,1)}, u32[]{:S(2)}, u32[]{:S(2)}) collective-permute-start(bf16[1,1408,128]{2,1,0:T(8,128)(2,1)} %dynamic-slice_convert_fusion.6), channel_id=1, source_target_pairs={{0,16},{4,20},{8,24},{12,28},{16,0},{20,4},{24,8},{28,12},{1,17},{... | collective-permute-start | bytes 1081352 | tf_op jit(solution)/shard_map/ppermute | solution.py:328
  652.3 30.7 %collective-permute-start.19 = (f32[2,1024]{1,0:T(2,128)S(1)}, f32[2,1024]{1,0:T(2,128)S(1)}, u32[]{:S(2)}, u32[]{:S(2)}) collective-permute-start(f32[2,1024]{1,0:T(2,128)S(1)} %fusion.118), channel_id=1, source_target_pairs={{0,4},{4,0},{8,12},{12,8},{16,20},{20,16},{24,28},{28,24},{1,5},{5... | collective-permute-start | bytes 24584 | tf_op jit(solution)/shard_map/ppermute | solution.py:386
  673.8 28.6 %collective-permute-start.24 = (bf16[2,1024,128]{2,1,0:T(8,128)(2,1)}, bf16[2,1024,128]{2,1,0:T(8,128)(2,1)}, u32[]{:S(2)}, u32[]{:S(2)}) collective-permute-start(bf16[2,1024,128]{2,1,0:T(8,128)(2,1)} %fusion.54), channel_id=1, source_target_pairs={{0,8},{4,12},{8,0},{12,4},{16,24},{20,28},{24,16},{28,20},{1,9},{5... | collective-permute-start | bytes 1572872 | tf_op jit(solution)/shard_map/ppermute | solution.py:328
  674.7 10.4 %copy-start.19 = (f32[2,1408,128]{2,1,0:T(8,128)S(1)}, f32[2,1408,128]{2,1,0:T(8,128)}, u32[]{:S(2)}) copy-start(f32[2,1408,128]{2,1,0:T(8,128)} %copy-done.18) | copy-start | bytes 4325380
  674.7 43.6 %all-to-all-start.2 = ((bf16[8,64,1024]{2,1,0:T(8,128)(2,1)}), bf16[8,64,1024]{2,1,0:T(8,128)(2,1)}, u32[]{:S(2)}, u32[]{:S(2)}) async-start(bf16[8,64,1024]{2,1,0:T(8,128)(2,1)} %bitcast.178), calls=%async_computation.2 | async-start | bytes 2097152 | tf_op jit(solution)/shard_map/all_to_all | solution.py:242
  683.1 18.1 %collective-permute-start.20 = (f32[2,1024]{1,0:T(2,128)S(1)}, f32[2,1024]{1,0:T(2,128)S(1)}, u32[]{:S(2)}, u32[]{:S(2)}) collective-permute-start(f32[2,1024]{1,0:T(2,128)S(1)} %add.283), channel_id=1, source_target_pairs={{0,8},{4,12},{8,0},{12,4},{16,24},{20,28},{24,16},{28,20},{1,9},{5... | collective-permute-start | bytes 24584 | tf_op jit(solution)/shard_map/ppermute | solution.py:386
  701.2 6.7 collective-permute-start.21
  703.5 21.9 %collective-permute-start.16 = (bf16[8,64,1024]{2,1,0:T(8,128)(2,1)}, bf16[8,64,1024]{2,1,0:T(8,128)(2,1)S(1)}, u32[]{:S(2)}, u32[]{:S(2)}) collective-permute-start(bf16[8,64,1024]{2,1,0:T(8,128)(2,1)} %all-to-all-done.3), channel_id=1, source_target_pairs={{0,2},{2,0},{1,3},{3,1},{4,6},{6,4},{5,7},{7,5},{8,10},{10,8},{9,1... | collective-permute-start | bytes 3145736 | tf_op jit(solution)/shard_map/ppermute | solution.py:239
  703.9 11.3 %collective-permute-start.25 = (bf16[1,1024,128]{2,1,0:T(8,128)(2,1)S(1)}, bf16[1,1024,128]{2,1,0:T(8,128)(2,1)S(1)}, u32[]{:S(2)}, u32[]{:S(2)}) collective-permute-start(bf16[1,1024,128]{2,1,0:T(8,128)(2,1)S(1)} %dynamic-slice_convert_fusion.7), channel_id=1, source_target_pairs={{0,16},{4,20},{8,24},{12,28},{16,0},{20,4},{24,8},{28,12},{1,17},{... | collective-permute-start | bytes 786440 | tf_op jit(solution)/shard_map/ppermute | solution.py:328
  (46 other events, 167.1 us)

commit v6 on v4

--- a/solution.py
+++ b/solution.py
@@ -47,7 +47,7 @@
     def _():
         query = q_ref[...] * jnp.asarray(HEAD_DIM**-0.5, LOW)
         queries = [jnp.where(m, query, jnp.zeros_like(query)) for m in masks]
-        above = lax.broadcasted_iota(jnp.int32, (block, block), 0) >= lax.broadcasted_iota(
+        below = lax.broadcasted_iota(jnp.int32, (block, block), 0) <= lax.broadcasted_iota(
             jnp.int32, (block, block), 1
         )
 
@@ -58,26 +58,28 @@
             result = []
             for head in range(2):
                 high, acc = state[head]
-                scores = dot(queries[head], keys, 1, 1)
+                scores = dot(keys, queries[head], 1, 1)
                 if diagonal:
-                    scores = jnp.where(above, scores, NEGATIVE)
-                new_high = jnp.maximum(high, jnp.max(scores, -1, keepdims=True))
+                    scores = jnp.where(below, scores, NEGATIVE)
+                new_high = jnp.maximum(high, jnp.max(scores, 0, keepdims=True))
                 probs = jnp.exp(scores - new_high).astype(LOW)
                 extended = jnp.where(masks[head], values, jnp.ones_like(values))
-                acc = acc * jnp.exp(high - new_high) + dot(probs, extended, 1, 0)
+                acc = acc * jnp.exp(high - new_high) + dot(extended, probs, 0, 0)
                 result.append((new_high, acc))
             return tuple(result)
 
         start_state = tuple(
-            (jnp.full((block, 1), NEGATIVE, F32), jnp.zeros((block, PAIR), F32)) for _ in range(2)
+            (jnp.full((1, block), NEGATIVE, F32), jnp.zeros((PAIR, block), F32)) for _ in range(2)
         )
         state = step(number, start_state, True)
         state = lax.fori_loop(0, number, lambda n, s: step(n, s, False), state)
         (high0, acc0), (high1, acc1) = state
-        sum0 = acc0[:, HEAD_DIM : HEAD_DIM + 1]
-        sum1 = acc1[:, 0:1]
-        o_ref[...] = jnp.where(masks[0], acc0 / sum0, acc1 / sum1).astype(LOW)
-        total_ref[...] = jnp.where(masks[0], high0 + jnp.log(sum0), high1 + jnp.log(sum1))
+        sum0 = acc0[HEAD_DIM : HEAD_DIM + 1]
+        sum1 = acc1[0:1]
+        mixed = jnp.concatenate((acc0[:HEAD_DIM] / sum0, acc1[HEAD_DIM:] / sum1), 0)
+        o_ref[...] = mixed.T.astype(LOW)
+        first = lax.broadcasted_iota(jnp.int32, (PAIR, block), 0) < HEAD_DIM
+        total_ref[...] = jnp.where(first, high0 + jnp.log(sum0), high1 + jnp.log(sum1)).T
 
     @pl.when(number >= info[0])
     def _():

time: 738 us -> 736 us (level)
  transfers between devices with their start and end apart: 37 -> 37, of which waited for: 18 -> 18; matrix products, arithmetic and copies ran while one was open for 24% -> 24% of each run, Pallas kernels for 18% -> 17%
where the time goes in v6:
time: 736 us; the launch traced here: 726 us
  waiting for transfers between devices  267 us (36%)
  matrix products  168 us (23%)
  Pallas kernels  127 us (17%)
  local copies, waits for them, and re-layouts  46.9 us (6%)
  other arithmetic  42.7 us (6%)
  starting transfers between devices  40.3 us (5%)
  blocking collectives  29.9 us (4%)
    ppermute x13, waiting for transfers between devices, swap_chip(): return lax.ppermute(value, 'tensor', [(0, 2), (2, 0), (1, 3), (3, 1)])  209 us
    dot_general x28, matrix products, dot(): lax.dot_general(left, right, (((left_dim,), (right_dim,)), ((), ())), pre...  168 us
    pallas_call x2, Pallas kernels, attend_back(): pl.pallas_call(functools.partial(attend_back_kernel, block), grid_spec=pl...  72.3 us
    pallas_call x2, Pallas kernels, attend(): pl.pallas_call(attend_kernel, grid_spec=pltpu.PrefetchScalarGridSpec(num_...  54.6 us
    ppermute x9, waiting for transfers between devices, over_chips(): lax.ppermute(lax.dynamic_index_in_dim(pairs, 1 - side, 1, False).astype(L...  40.9 us
    all_to_all x1, blocking collectives, exchange(): return lax.all_to_all(value, 'dp', split_axis=0, concat_axis=0, tiled=True)  29.9 us
    unnamed x138, local copies, waits for them, and re-layouts  22.2 us
    ppermute x3, waiting for transfers between devices, total_of(): moved = lax.ppermute(value, 'dp', [(i, i ^ step) for i in range(groups)])  16.1 us
  transfers between devices with their start and end apart: 37, of which 18 were waited for; matrix products, arithmetic and copies ran while one was open for 24% of the time, Pallas kernels for 17%

profile of v6, /device:TPU:0, one launch (start us, length us, event | category | flops | bytes accessed | tf_op | source)
XLA Modules:
  0.0 726.4 jit_solution(5844216251144077749)
XLA Ops:
  0.7 2.0 sort.17
  4.6 7.3 %all-to-all-start = ((bf16[8,64,1024]{2,1,0:T(8,128)(2,1)}), bf16[8,64,1024]{2,1,0:T(8,128)(2,1)S(1)}, u32[]{:S(2)}, u32[]{:S(2)}) async-start(bf16[8,64,1024]{2,1,0:T(8,128)(2,1)} %gather_fusion), calls=%async_computation | async-start | bytes 2097152 | tf_op jit(solution)/shard_map/all_to_all | solution.py:241
  15.1 23.3 %collective-permute-done = bf16[8,64,1024]{2,1,0:T(8,128)(2,1)S(1)} collective-permute-done((bf16[8,64,1024]{2,1,0:T(8,128)(2,1)}, bf16[8,64,1024]{2,1,0:T(8,128)(2,1)S(1)}, u32[]{:S(2)}, u32[]{:S(2)}) %collective-permute-start) | collective-permute-done | bytes 1048608 | tf_op jit(solution)/shard_map/ppermute | solution.py:238
  38.4 29.9 %all_to_all.20 = bf16[8,64,1024]{2,1,0:T(8,128)(2,1)S(1)} all-to-all(bf16[8,64,1024]{2,1,0:T(8,128)(2,1)S(1)} %collective-permute-done), channel_id=1, replica_groups=mesh['dp'=8,'tensor'=4] {'dp'}, dimensions={0} | all-to-all | bytes 2097152 | tf_op jit(solution)/shard_map/all_to_all | solution.py:241
  68.8 1.9 fusion.12
  79.8 7.8 %fusion.86.q_ref.k_ref.v_ref = bf16[2048,768]{1,0:T(8,128)(2,1)} fusion(bf16[1024,768]{1,0:T(8,128)(2,1)} %constant_dynamic-update-slice_fusion, bf16[1024,1024]{1,0:T(8,128)(2,1)} %collective-permute-done.1, bf16[1024,1024]{1,0:T(8,128)(2,1)} %fusion.12), kind=kOutput, calls=%fused_computation.192 | convolution fusion | flops 3229614080 | bytes 8912896 | tf_op jit(solution)/shard_map/dot_general | solution.py:20
  87.5 23.4 %collective-permute-done.2 = bf16[1024,768]{1,0:T(8,128)(2,1)} collective-permute-done((bf16[1024,768]{1,0:T(8,128)(2,1)}, bf16[1024,768]{1,0:T(8,128)(2,1)}, u32[]{:S(2)}, u32[]{:S(2)}) %collective-permute-start.2) | collective-permute-done | bytes 1572896 | tf_op jit(solution)/shard_map/ppermute | solution.py:238
  110.9 7.8 %fusion.85.q_ref.k_ref.v_ref = bf16[2048,768]{1,0:T(8,128)(2,1)} fusion(bf16[1024,768]{1,0:T(8,128)(2,1)} %collective-permute-done.2, bf16[1024,1024]{1,0:T(8,128)(2,1)} %collective-permute-done.1, bf16[1024,1024]{1,0:T(8,128)(2,1)} %fusion.12), kind=kOutput, calls=%fused_computation.191 | convolution fusion | flops 3229614080 | bytes 8912896 | tf_op jit(solution)/shard_map/dot_general | solution.py:20
  118.7 27.2 %attend.2 = (bf16[2048,256]{1,0:T(8,128)(2,1)}, f32[2048,256]{1,0:T(8,128)}) custom-call(s32[5]{0:T(128)} %pad_add_fusion.info, bf16[2048,768]{1,0:T(8,128)(2,1)} %fusion.86.q_ref.k_ref.v_ref, bf16[2048,768]{1,0:T(8,128)(2,1)} %fusion.86.q_ref.k_ref.v_ref, bf16[2048,768]{1,0:T(8,128)(2,1)} %fusion.86.q_ref.k_ref.v_ref), custom_call_target="tpu_custom_call" | custom-call | tf_op jit(solution)/shard_map/attend/pallas_call | solution.py:94
  145.8 27.5 %attend.3 = (bf16[2048,256]{1,0:T(8,128)(2,1)}, f32[2048,256]{1,0:T(8,128)}) custom-call(s32[5]{0:T(128)} %pad_add_fusion.info, bf16[2048,768]{1,0:T(8,128)(2,1)} %fusion.85.q_ref.k_ref.v_ref, bf16[2048,768]{1,0:T(8,128)(2,1)} %fusion.85.q_ref.k_ref.v_ref, bf16[2048,768]{1,0:T(8,128)(2,1)} %fusion.85.q_ref.k_ref.v_ref), custom_call_target="tpu_custom_call" | custom-call | tf_op jit(solution)/shard_map/attend/pallas_call | solution.py:94
  173.3 1.8 fusion.56
  195.2 39.1 %collective-permute-done.11 = bf16[512,1024]{1,0:T(8,128)(2,1)S(1)} collective-permute-done((bf16[512,1024]{1,0:T(8,128)(2,1)}, bf16[512,1024]{1,0:T(8,128)(2,1)S(1)}, u32[]{:S(2)}, u32[]{:S(2)}) %collective-permute-start.11) | collective-permute-done | bytes 1048608 | tf_op jit(solution)/shard_map/ppermute | solution.py:238
  234.8 2.1 constant_dynamic-update-slice_fusion.3
  237.0 28.3 %collective-permute-done.7 = bf16[1024,704]{0,1:T(8,128)(2,1)} collective-permute-done((bf16[1024,704]{0,1:T(8,128)(2,1)S(1)}, bf16[1024,704]{0,1:T(8,128)(2,1)}, u32[]{:S(2)}, u32[]{:S(2)}) %collective-permute-start.7) | collective-permute-done | bytes 1441824 | tf_op jit(solution)/shard_map/ppermute | solution.py:238
  266.8 28.9 %collective-permute-done.8 = bf16[704,1024]{1,0:T(8,128)(2,1)} collective-permute-done((bf16[704,1024]{1,0:T(8,128)(2,1)}, bf16[704,1024]{1,0:T(8,128)(2,1)}, u32[]{:S(2)}, u32[]{:S(2)}) %collective-permute-start.8) | collective-permute-done | bytes 1441824 | tf_op jit(solution)/shard_map/ppermute | solution.py:238
  298.8 10.9 %fusion.81 = bf16[2048,1408]{1,0:T(8,128)(2,1)} fusion(bf16[1024,1408]{0,1:T(8,128)(2,1)S(1)} %constant_dynamic-update-slice_fusion.5, bf16[1024,1024]{1,0:T(8,128)(2,1)} %collective-permute-done.5, bf16[1024,1024]{1,0:T(8,128)(2,1)} %multiply_convert_fusion.2), kind=kOutput, calls=%fused_computation.187 | convolution fusion | flops 5913968640 | bytes 12845056 | tf_op jit(solution)/shard_map/dot_general | solution.py:20
  309.7 11.2 %fusion.82 = bf16[2048,1408]{1,0:T(8,128)(2,1)} fusion(bf16[1024,1408]{0,1:T(8,128)(2,1)S(1)} %constant_dynamic-update-slice_fusion.3, bf16[1024,1024]{1,0:T(8,128)(2,1)} %collective-permute-done.5, bf16[1024,1024]{1,0:T(8,128)(2,1)} %multiply_convert_fusion.2), kind=kOutput, calls=%fused_computation.188 | convolution fusion | flops 5913968640 | bytes 12845056 | tf_op jit(solution)/shard_map/dot_general | solution.py:20
  320.9 19.1 %fusion.3 = (bf16[2048,1408]{1,0:T(8,128)(2,1)}, bf16[2048,1408]{1,0:T(8,128)(2,1)}, bf16[2048,1408]{1,0:T(8,128)(2,1)}) fusion(bf16[2048,1408]{1,0:T(8,128)(2,1)} %fusion.81, bf16[2048,1408]{1,0:T(8,128)(2,1)} %fusion.82, bf16[1408,1024]{1,0:T(8,128)(2,1)} %copy-done.29, bf16[1024,1024]{1,0:T(8,128)(2,1)} %collective-permute-done.12, ...), kind=kOutput, calls=%fused_computation.11 | convolution fusion | flops 5962989568 | bytes 35913728 | tf_op jit(solution)/shard_map/dot_general | solution.py:20
  340.1 8.3 %fusion.22 = f32[1024,1024]{1,0:T(8,128)} fusion(bf16[1024,1408]{0,1:T(8,128)(2,1)} %copy-done.32, bf16[2048,1408]{1,0:T(8,128)(2,1)} %get-tuple-element.105), kind=kOutput, calls=%fused_computation.62 | convolution fusion | flops 2952790016 | bytes 9961472 | tf_op jit(solution)/shard_map/dot_general | solution.py:20
  348.4 9.3 %fusion.79 = f32[1408,1024]{1,0:T(8,128)S(1)} fusion(bf16[2048,1408]{1,0:T(8,128)(2,1)S(1)} %copy-done.55, bf16[1024,1024]{1,0:T(8,128)(2,1)} %collective-permute-done.5, bf16[1024,1024]{1,0:T(8,128)(2,1)} %multiply_convert_fusion.2), kind=kOutput, calls=%fused_computation.185 | convolution fusion | flops 5913968640 | bytes 15728640 | tf_op jit(solution)/shard_map/dot_general | solution.py:20
  357.9 2.6 copy-done.10
  360.5 9.4 %fusion.80 = f32[1408,1024]{1,0:T(8,128)S(1)} fusion(bf16[2048,1408]{1,0:T(8,128)(2,1)S(1)} %bitcast.192, bf16[1024,1024]{1,0:T(8,128)(2,1)} %collective-permute-done.5, bf16[1024,1024]{1,0:T(8,128)(2,1)} %multiply_convert_fusion.2), kind=kOutput, calls=%fused_computation.186 | convolution fusion | flops 5913968640 | bytes 15728640 | tf_op jit(solution)/shard_map/dot_general | solution.py:20
  370.1 2.6 copy-done.11
  373.8 4.8 fusion.36
  378.6 8.0 %fusion.34 = f32[1408,1024]{1,0:T(8,128)S(1)} fusion(bf16[2048,1408]{1,0:T(8,128)(2,1)S(1)} %bitcast.194, bf16[1024,1024]{1,0:T(8,128)(2,1)} %collective-permute-done.12, bf16[1024,1024]{1,0:T(8,128)(2,1)S(1)} %copy-done.23), kind=kOutput, calls=%fused_computation.77 | convolution fusion | flops 5913968640 | bytes 15728640 | tf_op jit(solution)/shard_map/dot_general | solution.py:20
  387.1 4.7 add_convert_fusion.1
  392.6 1.8 collective-permute-start.26
  394.4 5.2 fusion.28
  399.7 5.2 fusion.26
  405.0 16.4 %collective-permute-done.30 = bf16[704,1024]{1,0:T(8,128)(2,1)S(1)} collective-permute-done((bf16[704,1024]{1,0:T(8,128)(2,1)S(1)}, bf16[704,1024]{1,0:T(8,128)(2,1)S(1)}, u32[]{:S(2)}, u32[]{:S(2)}) %collective-permute-start.30) | collective-permute-done | bytes 1441824 | tf_op jit(solution)/shard_map/ppermute | solution.py:238
  423.3 2.4 multiply_reduce_fusion
  425.8 3.8 fusion.87
  429.7 7.5 %collective-permute-done.31 = bf16[4,704,128]{2,1,0:T(8,128)(2,1)S(1)} collective-permute-done((bf16[4,704,128]{2,1,0:T(8,128)(2,1)S(1)}, bf16[4,704,128]{2,1,0:T(8,128)(2,1)S(1)}, u32[]{:S(2)}, u32[]{:S(2)}) %collective-permute-start.31) | collective-permute-done | bytes 720928 | tf_op jit(solution)/shard_map/ppermute | solution.py:327
  438.5 5.9 multiply_convert_fusion.1
  447.6 6.2 collective-permute-done.33
  454.6 28.5 %collective-permute-done.26 = bf16[1408,1024]{1,0:T(8,128)(2,1)S(1)} collective-permute-done((bf16[1408,1024]{1,0:T(8,128)(2,1)S(1)}, bf16[1408,1024]{1,0:T(8,128)(2,1)S(1)}, u32[]{:S(2)}, u32[]{:S(2)}) %collective-permute-start.26) | collective-permute-done | bytes 2883616 | tf_op jit(solution)/shard_map/ppermute | solution.py:238
  486.7 3.9 fusion.77.do_ref
  490.7 36.1 %attend_back.2 = (bf16[2048,256]{1,0:T(8,128)(2,1)}, bf16[2048,256]{1,0:T(8,128)(2,1)}, bf16[2048,256]{1,0:T(8,128)(2,1)}) custom-call(s32[5]{0:T(128)} %pad_add_fusion.info, bf16[2048,768]{1,0:T(8,128)(2,1)} %fusion.85.q_ref.k_ref.v_ref, bf16[2048,768]{1,0:T(8,128)(2,1)} %fusion.85.q_ref.k_ref.v_ref, bf16[2048,768]{1,0:T(8,128)(2,1)} %fusion.85.q_ref.k_ref.v_ref, ...), custom_call_target="tpu_custom_call" | custom-call | tf_op jit(solution)/shard_map/attend_back/pallas_call | solution.py:187
  529.5 5.1 fusion.78.do_ref
  534.6 6.8 fusion.84
  541.4 36.2 %attend_back.3 = (bf16[2048,256]{1,0:T(8,128)(2,1)}, bf16[2048,256]{1,0:T(8,128)(2,1)}, bf16[2048,256]{1,0:T(8,128)(2,1)}) custom-call(s32[5]{0:T(128)} %pad_add_fusion.info, bf16[2048,768]{1,0:T(8,128)(2,1)} %fusion.86.q_ref.k_ref.v_ref, bf16[2048,768]{1,0:T(8,128)(2,1)} %fusion.86.q_ref.k_ref.v_ref, bf16[2048,768]{1,0:T(8,128)(2,1)} %fusion.86.q_ref.k_ref.v_ref, ...), custom_call_target="tpu_custom_call" | custom-call | tf_op jit(solution)/shard_map/attend_back/pallas_call | solution.py:187
  580.5 3.2 fusion.44
  583.7 3.3 fusion.48
  587.0 3.0 convolution_convert_fusion
  592.7 3.2 add_convert_fusion
  596.0 3.9 fusion.76
  599.9 3.4 fusion.46
  603.3 7.5 %fusion.83 = f32[768,1024]{1,0:T(8,128)} fusion(bf16[2048,768]{1,0:T(8,128)(2,1)S(1)} %constant_dynamic-update-slice_fusion.12, bf16[1024,1024]{1,0:T(8,128)(2,1)} %collective-permute-done.1, bf16[1024,1024]{1,0:T(8,128)(2,1)} %fusion.12), kind=kOutput, calls=%fused_computation.189 | convolution fusion | flops 3229614080 | bytes 10485760 | tf_op jit(solution)/shard_map/dot_general | solution.py:20
  614.2 2.6 fusion.19
  616.8 2.0 fusion.16
  620.4 4.2 all-to-all-start.3
  624.6 11.8 %collective-permute-done.22 = bf16[1024,1024]{1,0:T(8,128)(2,1)} collective-permute-done((bf16[1024,1024]{1,0:T(8,128)(2,1)}, bf16[1024,1024]{1,0:T(8,128)(2,1)}, u32[]{:S(2)}, u32[]{:S(2)}) %collective-permute-start.22) | collective-permute-done | bytes 2097184 | tf_op jit(solution)/shard_map/ppermute | solution.py:238
  636.4 3.2 copy_bitcast_fusion.1
  643.6 2.5 collective-permute-done.18
  647.1 19.5 %collective-permute-done.23 = bf16[4,1024,128]{2,1,0:T(8,128)(2,1)S(1)} collective-permute-done((bf16[4,1024,128]{2,1,0:T(8,128)(2,1)S(1)}, bf16[4,1024,128]{2,1,0:T(8,128)(2,1)S(1)}, u32[]{:S(2)}, u32[]{:S(2)}) %collective-permute-start.23) | collective-permute-done | bytes 1048608 | tf_op jit(solution)/shard_map/ppermute | solution.py:327
  668.5 4.4 all-to-all-start.2
  672.9 4.0 maximum_select_fusion
  676.9 2.0 collective-permute-start.20
  679.9 15.2 %collective-permute-done.20 = f32[2,1024]{1,0:T(2,128)S(1)} collective-permute-done((f32[2,1024]{1,0:T(2,128)S(1)}, f32[2,1024]{1,0:T(2,128)S(1)}, u32[]{:S(2)}, u32[]{:S(2)}) %collective-permute-start.20) | collective-permute-done | bytes 8224 | tf_op jit(solution)/shard_map/ppermute | solution.py:375
  697.7 2.0 collective-permute-start.25
  702.2 6.8 collective-permute-done.25
  712.0 7.2 collective-permute-done.16
  719.2 3.3 maximum_select_fusion.1
  722.5 3.7 gather_fusion.2
  (266 shorter events, 79.5 us)
Async XLA Ops:
  4.6 33.7 %all-to-all-start = ((bf16[8,64,1024]{2,1,0:T(8,128)(2,1)}), bf16[8,64,1024]{2,1,0:T(8,128)(2,1)S(1)}, u32[]{:S(2)}, u32[]{:S(2)}) async-start(bf16[8,64,1024]{2,1,0:T(8,128)(2,1)} %gather_fusion), calls=%async_computation | async-start | bytes 2097152 | tf_op jit(solution)/shard_map/all_to_all | solution.py:241
  11.9 56.9 %copy-start.45 = (f32[1024]{0:T(1024)S(1)}, f32[1024]{0:T(1024)}, u32[]{:S(2)}) copy-start(f32[1024]{0:T(1024)} %param.20) | copy-start | bytes 12292
  13.5 24.8 %collective-permute-start = (bf16[8,64,1024]{2,1,0:T(8,128)(2,1)}, bf16[8,64,1024]{2,1,0:T(8,128)(2,1)S(1)}, u32[]{:S(2)}, u32[]{:S(2)}) collective-permute-start(bf16[8,64,1024]{2,1,0:T(8,128)(2,1)} %gather_fusion.1), channel_id=1, source_target_pairs={{0,2},{2,0},{1,3},{3,1},{4,6},{6,4},{5,7},{7,5},{8,10},{10,8},{9,1... | collective-permute-start | bytes 3145736 | tf_op jit(solution)/shard_map/ppermute | solution.py:238
  38.4 142.9 %copy-start.4 = (bf16[8,64,1024]{2,1,0:T(8,128)(2,1)}, bf16[8,64,1024]{2,1,0:T(8,128)(2,1)S(1)}, u32[]{:S(2)}) copy-start(bf16[8,64,1024]{2,1,0:T(8,128)(2,1)S(1)} %all-to-all-done) | copy-start | bytes 3145732
  68.2 113.0 %copy-start.6 = (bf16[8,64,1024]{2,1,0:T(8,128)(2,1)}, bf16[8,64,1024]{2,1,0:T(8,128)(2,1)S(1)}, u32[]{:S(2)}) copy-start(bf16[8,64,1024]{2,1,0:T(8,128)(2,1)S(1)} %all_to_all.20) | copy-start | bytes 3145732
  68.8 228.3 %copy-start.41 = (f32[1024]{0:T(1024)}, f32[1024]{0:T(1024)S(1)}, u32[]{:S(2)}) copy-start(f32[1024]{0:T(1024)S(1)} %rsqrt.26) | copy-start | bytes 12292
  68.8 9.1 %copy-start.53 = (s32[16]{0:T(128)S(1)}, s32[16]{0:T(128)}, u32[]{:S(2)}) copy-start(s32[16]{0:T(128)} %param.18) | copy-start | bytes 196
  70.7 9.1 %collective-permute-start.1 = (bf16[1024,1024]{1,0:T(8,128)(2,1)}, bf16[1024,1024]{1,0:T(8,128)(2,1)}, u32[]{:S(2)}, u32[]{:S(2)}) collective-permute-start(bf16[1024,1024]{1,0:T(8,128)(2,1)} %fusion.12), channel_id=1, source_target_pairs={{0,1},{1,0},{2,3},{3,2},{4,5},{5,4},{6,7},{7,6},{8,9},{9,8},{10,11... | collective-permute-start | bytes 6291464 | tf_op jit(solution)/shard_map/ppermute | solution.py:235
  73.3 37.6 %collective-permute-start.2 = (bf16[1024,768]{1,0:T(8,128)(2,1)}, bf16[1024,768]{1,0:T(8,128)(2,1)}, u32[]{:S(2)}, u32[]{:S(2)}) collective-permute-start(bf16[1024,768]{1,0:T(8,128)(2,1)} %constant_dynamic-update-slice_fusion), channel_id=1, source_target_pairs={{0,2},{2,0},{1,3},{3,1},{4,6},{6,4},{5,7},{7,5},{8,10},{10,8},{9,1... | collective-permute-start | bytes 4718600 | tf_op jit(solution)/shard_map/ppermute | solution.py:238
  74.9 100.3 %collective-permute-start.3 = (bf16[256,1024]{1,0:T(8,128)(2,1)}, bf16[256,1024]{1,0:T(8,128)(2,1)}, u32[]{:S(2)}, u32[]{:S(2)}) collective-permute-start(bf16[256,1024]{1,0:T(8,128)(2,1)} %param.24), channel_id=1, source_target_pairs={{0,2},{2,0},{1,3},{3,1},{4,6},{6,4},{5,7},{7,5},{8,10},{10,8},{9,1... | collective-permute-start | bytes 1572872 | tf_op jit(solution)/shard_map/ppermute | solution.py:238
  145.8 27.5 %copy-start.14 = (bf16[2048,256]{1,0:T(8,128)(2,1)S(1)}, bf16[2048,256]{1,0:T(8,128)(2,1)}, u32[]{:S(2)}) copy-start(bf16[2048,256]{1,0:T(8,128)(2,1)} %get-tuple-element.26.o_ref) | copy-start | bytes 3145732
  177.0 4.2 collective-permute-start.4
  177.1 57.7 %collective-permute-start.6 = (bf16[1024,704]{0,1:T(8,128)(2,1)}, bf16[1024,704]{0,1:T(8,128)(2,1)}, u32[]{:S(2)}, u32[]{:S(2)}) collective-permute-start(bf16[1024,704]{0,1:T(8,128)(2,1)} %param.26), channel_id=1, source_target_pairs={{0,2},{2,0},{1,3},{3,1},{4,6},{6,4},{5,7},{7,5},{8,10},{10,8},{9,1... | collective-permute-start | bytes 4325384 | tf_op jit(solution)/shard_map/ppermute | solution.py:238
  185.2 113.6 %collective-permute-start.5 = (bf16[1024,1024]{1,0:T(8,128)(2,1)}, bf16[1024,1024]{1,0:T(8,128)(2,1)}, u32[]{:S(2)}, u32[]{:S(2)}) collective-permute-start(bf16[1024,1024]{1,0:T(8,128)(2,1)} %multiply_convert_fusion.2), channel_id=1, source_target_pairs={{0,1},{1,0},{2,3},{3,2},{4,5},{5,4},{6,7},{7,6},{8,9},{9,8},{10,11... | collective-permute-start | bytes 6291464 | tf_op jit(solution)/shard_map/ppermute | solution.py:235
  187.3 47.0 %copy-start.12 = (bf16[512,1024]{1,0:T(8,128)(2,1)}, bf16[512,1024]{1,0:T(8,128)(2,1)S(1)}, u32[]{:S(2)}) copy-start(bf16[512,1024]{1,0:T(8,128)(2,1)S(1)} %get-tuple-element.109) | copy-start | bytes 3145732
  187.3 47.0 %collective-permute-start.11 = (bf16[512,1024]{1,0:T(8,128)(2,1)}, bf16[512,1024]{1,0:T(8,128)(2,1)S(1)}, u32[]{:S(2)}, u32[]{:S(2)}) collective-permute-start(bf16[512,1024]{1,0:T(8,128)(2,1)} %get-tuple-element.110), channel_id=1, source_target_pairs={{0,2},{2,0},{1,3},{3,1},{4,6},{6,4},{5,7},{7,5},{8,10},{10,8},{9,1... | collective-permute-start | bytes 3145736 | tf_op jit(solution)/shard_map/ppermute | solution.py:238
  188.8 76.5 %collective-permute-start.7 = (bf16[1024,704]{0,1:T(8,128)(2,1)S(1)}, bf16[1024,704]{0,1:T(8,128)(2,1)}, u32[]{:S(2)}, u32[]{:S(2)}) collective-permute-start(bf16[1024,704]{0,1:T(8,128)(2,1)S(1)} %copy-done.26), channel_id=1, source_target_pairs={{0,2},{2,0},{1,3},{3,1},{4,6},{6,4},{5,7},{7,5},{8,10},{10,8},{9,1... | collective-permute-start | bytes 4325384 | tf_op jit(solution)/shard_map/ppermute | solution.py:238
  189.4 106.3 %collective-permute-start.8 = (bf16[704,1024]{1,0:T(8,128)(2,1)}, bf16[704,1024]{1,0:T(8,128)(2,1)}, u32[]{:S(2)}, u32[]{:S(2)}) collective-permute-start(bf16[704,1024]{1,0:T(8,128)(2,1)} %param.28), channel_id=1, source_target_pairs={{0,2},{2,0},{1,3},{3,1},{4,6},{6,4},{5,7},{7,5},{8,10},{10,8},{9,1... | collective-permute-start | bytes 4325384 | tf_op jit(solution)/shard_map/ppermute | solution.py:238
  192.1 42.2 %copy-start.47 = (f32[1024]{0:T(1024)}, f32[1024]{0:T(1024)S(1)}, u32[]{:S(2)}) copy-start(f32[1024]{0:T(1024)S(1)} %fusion.67) | copy-start | bytes 12292
  234.7 62.4 %copy-start.22 = (bf16[1024,1024]{1,0:T(8,128)(2,1)}, bf16[1024,1024]{1,0:T(8,128)(2,1)S(1)}, u32[]{:S(2)}) copy-start(bf16[1024,1024]{1,0:T(8,128)(2,1)S(1)} %fusion.20) | copy-start | bytes 6291460
  234.7 86.2 %collective-permute-start.12 = (bf16[1024,1024]{1,0:T(8,128)(2,1)S(1)}, bf16[1024,1024]{1,0:T(8,128)(2,1)}, u32[]{:S(2)}, u32[]{:S(2)}) collective-permute-start(bf16[1024,1024]{1,0:T(8,128)(2,1)S(1)} %fusion.20), channel_id=1, source_target_pairs={{0,1},{1,0},{2,3},{3,2},{4,5},{5,4},{6,7},{7,6},{8,9},{9,8},{10,11... | collective-permute-start | bytes 6291464 | tf_op jit(solution)/shard_map/ppermute | solution.py:235
  236.9 72.7 %copy-start.34 = (bf16[1024,1408]{0,1:T(8,128)(2,1)}, bf16[1024,1408]{0,1:T(8,128)(2,1)S(1)}, u32[]{:S(2)}) copy-start(bf16[1024,1408]{0,1:T(8,128)(2,1)S(1)} %constant_dynamic-update-slice_fusion.3) | copy-start | bytes 8650756
  266.8 42.9 %copy-start.32 = (bf16[1024,1408]{0,1:T(8,128)(2,1)}, bf16[1024,1408]{0,1:T(8,128)(2,1)S(1)}, u32[]{:S(2)}) copy-start(bf16[1024,1408]{0,1:T(8,128)(2,1)S(1)} %constant_dynamic-update-slice_fusion.5) | copy-start | bytes 8650756
  309.7 11.2 %copy-start.23 = (bf16[1024,1024]{1,0:T(8,128)(2,1)S(1)}, bf16[1024,1024]{1,0:T(8,128)(2,1)}, u32[]{:S(2)}) copy-start(bf16[1024,1024]{1,0:T(8,128)(2,1)} %copy-done.22) | copy-start | bytes 6291460
  340.1 8.3 %copy-start.55 = (bf16[2048,1408]{1,0:T(8,128)(2,1)S(1)}, bf16[2048,1408]{1,0:T(8,128)(2,1)}, u32[]{:S(2)}) copy-start(bf16[2048,1408]{1,0:T(8,128)(2,1)} %get-tuple-element.105) | copy-start | bytes 17301508
  340.1 20.4 %slice-start.4 = ((s8[5767168]{0:T(1024)(128)(4,1)}), s8[4194304]{0:T(1024)(128)(4,1)S(1)}, s32[]{:S(2)}) async-start(s8[5767168]{0:T(1024)(128)(4,1)} %bitcast.191), calls=%async_computation.8 | async-start | bytes 8388608
  348.4 12.1 %slice-start.5 = ((s8[5767168]{0:T(1024)(128)(4,1)}), s8[1572864]{0:T(1024)(128)(4,1)S(1)}, s32[]{:S(2)}) async-start(s8[5767168]{0:T(1024)(128)(4,1)} %bitcast.191), calls=%async_computation.9 | async-start | bytes 3145728
  357.9 14.8 %slice-start.6 = ((s8[5767168]{0:T(1024)(128)(4,1)}), s8[4194304]{0:T(1024)(128)(4,1)S(1)}, s32[]{:S(2)}) async-start(s8[5767168]{0:T(1024)(128)(4,1)} %bitcast.193), calls=%async_computation.10 | async-start | bytes 8388608
  360.5 12.2 %slice-start.7 = ((s8[5767168]{0:T(1024)(128)(4,1)}), s8[1572864]{0:T(1024)(128)(4,1)S(1)}, s32[]{:S(2)}) async-start(s8[5767168]{0:T(1024)(128)(4,1)} %bitcast.193), calls=%async_computation.11 | async-start | bytes 3145728
  378.5 8.6 %copy-start.35 = (bf16[1024,1408]{0,1:T(8,128)(2,1)S(1)}, bf16[1024,1408]{0,1:T(8,128)(2,1)}, u32[]{:S(2)}) copy-start(bf16[1024,1408]{0,1:T(8,128)(2,1)} %copy-done.34) | copy-start | bytes 8650756
  378.5 8.6 %copy-start.56 = (f32[1024,1024]{1,0:T(8,128)S(1)}, f32[1024,1024]{1,0:T(8,128)}, u32[]{:S(2)}) copy-start(f32[1024,1024]{1,0:T(8,128)} %fusion.22) | copy-start | bytes 12582916
  386.8 34.5 %collective-permute-start.30 = (bf16[704,1024]{1,0:T(8,128)(2,1)S(1)}, bf16[704,1024]{1,0:T(8,128)(2,1)S(1)}, u32[]{:S(2)}, u32[]{:S(2)}) collective-permute-start(bf16[704,1024]{1,0:T(8,128)(2,1)S(1)} %slice.253), channel_id=1, source_target_pairs={{0,2},{2,0},{1,3},{3,1},{4,6},{6,4},{5,7},{7,5},{8,10},{10,8},{9,1... | collective-permute-start | bytes 4325384 | tf_op jit(solution)/shard_map/ppermute | solution.py:238
  387.1 51.4 %collective-permute-start.9 = (bf16[1024,1024]{1,0:T(8,128)(2,1)}, bf16[1024,1024]{1,0:T(8,128)(2,1)}, u32[]{:S(2)}, u32[]{:S(2)}) collective-permute-start(bf16[1024,1024]{1,0:T(8,128)(2,1)} %fusion.36), channel_id=1, source_target_pairs={{0,1},{1,0},{2,3},{3,2},{4,5},{5,4},{6,7},{7,6},{8,9},{9,8},{10,11... | collective-permute-start | bytes 6291464 | tf_op jit(solution)/shard_map/ppermute | solution.py:235
  391.8 31.5 %collective-permute-start.13 = (bf16[1024,1024]{1,0:T(8,128)(2,1)}, bf16[1024,1024]{1,0:T(8,128)(2,1)S(1)}, u32[]{:S(2)}, u32[]{:S(2)}) collective-permute-start(bf16[1024,1024]{1,0:T(8,128)(2,1)} %add_convert_fusion.1), channel_id=1, source_target_pairs={{0,1},{1,0},{2,3},{3,2},{4,5},{5,4},{6,7},{7,6},{8,9},{9,8},{10,11... | collective-permute-start | bytes 6291464 | tf_op jit(solution)/shard_map/ppermute | solution.py:235
  392.6 90.5 %collective-permute-start.26 = (bf16[1408,1024]{1,0:T(8,128)(2,1)S(1)}, bf16[1408,1024]{1,0:T(8,128)(2,1)S(1)}, u32[]{:S(2)}, u32[]{:S(2)}) collective-permute-start(bf16[1408,1024]{1,0:T(8,128)(2,1)S(1)} %pad_maximum_fusion.4), channel_id=1, source_target_pairs={{0,2},{2,0},{1,3},{3,1},{4,6},{6,4},{5,7},{7,5},{8,10},{10,8},{9,1... | collective-permute-start | bytes 8650760 | tf_op jit(solution)/shard_map/ppermute | solution.py:238
  404.9 18.4 %copy-start.3 = (f32[1024,1024]{1,0:T(8,128)S(1)}, f32[1024,1024]{1,0:T(8,128)}, u32[]{:S(2)}) copy-start(f32[1024,1024]{1,0:T(8,128)} %copy-done.2) | copy-start | bytes 12582916
  405.0 18.4 %copy-start.44 = (f32[1024]{0:T(1024)S(1)}, f32[1024]{0:T(1024)}, u32[]{:S(2)}) copy-start(f32[1024]{0:T(1024)} %copy-done.43) | copy-start | bytes 12292
  405.0 18.3 %copy-start.50 = (f32[1024]{0:T(1024)S(1)}, f32[1024]{0:T(1024)}, u32[]{:S(2)}) copy-start(f32[1024]{0:T(1024)} %param.25) | copy-start | bytes 12292
  421.8 15.4 %collective-permute-start.31 = (bf16[4,704,128]{2,1,0:T(8,128)(2,1)S(1)}, bf16[4,704,128]{2,1,0:T(8,128)(2,1)S(1)}, u32[]{:S(2)}, u32[]{:S(2)}) collective-permute-start(bf16[4,704,128]{2,1,0:T(8,128)(2,1)S(1)} %fusion.53), channel_id=1, source_target_pairs={{0,4},{4,0},{8,12},{12,8},{16,20},{20,16},{24,28},{28,24},{1,5},{5... | collective-permute-start | bytes 2162696 | tf_op jit(solution)/shard_map/ppermute | solution.py:327
  429.7 8.9 %copy-start.31 = (bf16[1408,1024]{1,0:T(8,128)(2,1)S(1)}, bf16[1408,1024]{1,0:T(8,128)(2,1)}, u32[]{:S(2)}) copy-start(bf16[1408,1024]{1,0:T(8,128)(2,1)} %copy-done.29) | copy-start | bytes 8650756
  429.7 57.1 %collective-permute-start.14 = (bf16[1024,1024]{1,0:T(8,128)(2,1)S(1)}, bf16[1024,1024]{1,0:T(8,128)(2,1)}, u32[]{:S(2)}, u32[]{:S(2)}) collective-permute-start(bf16[1024,1024]{1,0:T(8,128)(2,1)S(1)} %get-tuple-element.99), channel_id=1, source_target_pairs={{0,1},{1,0},{2,3},{3,2},{4,5},{5,4},{6,7},{7,6},{8,9},{9,8},{10,11... | collective-permute-start | bytes 6291464 | tf_op jit(solution)/shard_map/ppermute | solution.py:235
  437.4 8.0 %collective-permute-start.32 = (bf16[2,704,128]{2,1,0:T(8,128)(2,1)S(1)}, bf16[2,704,128]{2,1,0:T(8,128)(2,1)S(1)}, u32[]{:S(2)}, u32[]{:S(2)}) collective-permute-start(bf16[2,704,128]{2,1,0:T(8,128)(2,1)S(1)} %fusion.62), channel_id=1, source_target_pairs={{0,8},{4,12},{8,0},{12,4},{16,24},{20,28},{24,16},{28,20},{1,9},{5... | collective-permute-start | bytes 1081352 | tf_op jit(solution)/shard_map/ppermute | solution.py:327
  445.3 37.8 %slice-start.3 = ((f32[1408,1024]{1,0:T(8,128)}), f32[704,1024]{1,0:T(8,128)S(1)}, s32[]{:S(2)}) async-start(f32[1408,1024]{1,0:T(8,128)} %copy-done.11), calls=%async_computation.7 | async-start | bytes 5767168 | tf_op jit(solution)/shard_map/slice | solution.py:337
  445.4 37.7 %slice-start.2 = ((f32[1408,1024]{1,0:T(8,128)}), f32[704,1024]{1,0:T(8,128)S(1)}, s32[]{:S(2)}) async-start(f32[1408,1024]{1,0:T(8,128)} %copy-done.10), calls=%async_computation.6 | async-start | bytes 5767168 | tf_op jit(solution)/shard_map/slice | solution.py:337
  445.4 8.4 %collective-permute-start.33 = (bf16[1,704,128]{2,1,0:T(8,128)(2,1)S(1)}, bf16[1,704,128]{2,1,0:T(8,128)(2,1)S(1)}, u32[]{:S(2)}, u32[]{:S(2)}) collective-permute-start(bf16[1,704,128]{2,1,0:T(8,128)(2,1)S(1)} %dynamic-slice_convert_fusion.8), channel_id=1, source_target_pairs={{0,16},{4,20},{8,24},{12,28},{16,0},{20,4},{24,8},{28,12},{1,17},{... | collective-permute-start | bytes 540680 | tf_op jit(solution)/shard_map/ppermute | solution.py:327
  447.0 225.8 %collective-permute-start.10 = (bf16[512,1024]{1,0:T(8,128)(2,1)}, bf16[512,1024]{1,0:T(8,128)(2,1)}, u32[]{:S(2)}, u32[]{:S(2)}) collective-permute-start(bf16[512,1024]{1,0:T(8,128)(2,1)} %get-tuple-element.112), channel_id=1, source_target_pairs={{0,2},{2,0},{1,3},{3,1},{4,6},{6,4},{5,7},{7,5},{8,10},{10,8},{9,1... | collective-permute-start | bytes 3145736 | tf_op jit(solution)/shard_map/ppermute | solution.py:238
  485.2 125.5 %collective-permute-start.27 = (bf16[4,1408,128]{2,1,0:T(8,128)(2,1)}, bf16[4,1408,128]{2,1,0:T(8,128)(2,1)}, u32[]{:S(2)}, u32[]{:S(2)}) collective-permute-start(bf16[4,1408,128]{2,1,0:T(8,128)(2,1)} %fusion.50), channel_id=1, source_target_pairs={{0,4},{4,0},{8,12},{12,8},{16,20},{20,16},{24,28},{28,24},{1,5},{5... | collective-permute-start | bytes 4325384 | tf_op jit(solution)/shard_map/ppermute | solution.py:327
  591.5 44.9 %collective-permute-start.22 = (bf16[1024,1024]{1,0:T(8,128)(2,1)}, bf16[1024,1024]{1,0:T(8,128)(2,1)}, u32[]{:S(2)}, u32[]{:S(2)}) collective-permute-start(bf16[1024,1024]{1,0:T(8,128)(2,1)} %pad_maximum_fusion.9), channel_id=1, source_target_pairs={{0,2},{2,0},{1,3},{3,1},{4,6},{6,4},{5,7},{7,5},{8,10},{10,8},{9,1... | collective-permute-start | bytes 6291464 | tf_op jit(solution)/shard_map/ppermute | solution.py:238
  595.9 18.2 %collective-permute-start.15 = (bf16[1024,1024]{1,0:T(8,128)(2,1)S(1)}, bf16[1024,1024]{1,0:T(8,128)(2,1)S(1)}, u32[]{:S(2)}, u32[]{:S(2)}) collective-permute-start(bf16[1024,1024]{1,0:T(8,128)(2,1)S(1)} %add_convert_fusion), channel_id=1, source_target_pairs={{0,1},{1,0},{2,3},{3,2},{4,5},{5,4},{6,7},{7,6},{8,9},{9,8},{10,11... | collective-permute-start | bytes 6291464 | tf_op jit(solution)/shard_map/ppermute | solution.py:235
  599.9 10.9 %slice-start = ((s8[5767168]{0:T(1024)(128)(4,1)}), s8[4194304]{0:T(1024)(128)(4,1)S(1)}, s32[]{:S(2)}) async-start(s8[5767168]{0:T(1024)(128)(4,1)} %bitcast.164), calls=%async_computation.4 | async-start | bytes 8388608
  613.6 27.6 %collective-permute-start.28 = (bf16[2,1408,128]{2,1,0:T(8,128)(2,1)}, bf16[2,1408,128]{2,1,0:T(8,128)(2,1)}, u32[]{:S(2)}, u32[]{:S(2)}) collective-permute-start(bf16[2,1408,128]{2,1,0:T(8,128)(2,1)} %fusion.52), channel_id=1, source_target_pairs={{0,8},{4,12},{8,0},{12,4},{16,24},{20,28},{24,16},{28,20},{1,9},{5... | collective-permute-start | bytes 2162696 | tf_op jit(solution)/shard_map/ppermute | solution.py:327
  620.4 48.1 %all-to-all-start.3 = ((bf16[8,64,1024]{2,1,0:T(8,128)(2,1)}), bf16[8,64,1024]{2,1,0:T(8,128)(2,1)}, u32[]{:S(2)}, u32[]{:S(2)}) async-start(bf16[8,64,1024]{2,1,0:T(8,128)(2,1)} %bitcast.179), calls=%async_computation.3 | async-start | bytes 2097152 | tf_op jit(solution)/shard_map/all_to_all | solution.py:241
  639.8 26.8 %collective-permute-start.23 = (bf16[4,1024,128]{2,1,0:T(8,128)(2,1)S(1)}, bf16[4,1024,128]{2,1,0:T(8,128)(2,1)S(1)}, u32[]{:S(2)}, u32[]{:S(2)}) collective-permute-start(bf16[4,1024,128]{2,1,0:T(8,128)(2,1)S(1)} %fusion.51), channel_id=1, source_target_pairs={{0,4},{4,0},{8,12},{12,8},{16,20},{20,16},{24,28},{28,24},{1,5},{5... | collective-permute-start | bytes 3145736 | tf_op jit(solution)/shard_map/ppermute | solution.py:327
  641.1 1.3 collective-permute-start.17
  642.5 3.7 collective-permute-start.18
  643.6 35.3 %collective-permute-start.29 = (bf16[1,1408,128]{2,1,0:T(8,128)(2,1)}, bf16[1,1408,128]{2,1,0:T(8,128)(2,1)}, u32[]{:S(2)}, u32[]{:S(2)}) collective-permute-start(bf16[1,1408,128]{2,1,0:T(8,128)(2,1)} %dynamic-slice_convert_fusion.6), channel_id=1, source_target_pairs={{0,16},{4,20},{8,24},{12,28},{16,0},{20,4},{24,8},{28,12},{1,17},{... | collective-permute-start | bytes 1081352 | tf_op jit(solution)/shard_map/ppermute | solution.py:327
  646.2 30.7 %collective-permute-start.19 = (f32[2,1024]{1,0:T(2,128)S(1)}, f32[2,1024]{1,0:T(2,128)S(1)}, u32[]{:S(2)}, u32[]{:S(2)}) collective-permute-start(f32[2,1024]{1,0:T(2,128)S(1)} %fusion.118), channel_id=1, source_target_pairs={{0,4},{4,0},{8,12},{12,8},{16,20},{20,16},{24,28},{28,24},{1,5},{5... | collective-permute-start | bytes 24584 | tf_op jit(solution)/shard_map/ppermute | solution.py:375
  667.7 28.6 %collective-permute-start.24 = (bf16[2,1024,128]{2,1,0:T(8,128)(2,1)}, bf16[2,1024,128]{2,1,0:T(8,128)(2,1)}, u32[]{:S(2)}, u32[]{:S(2)}) collective-permute-start(bf16[2,1024,128]{2,1,0:T(8,128)(2,1)} %fusion.54), channel_id=1, source_target_pairs={{0,8},{4,12},{8,0},{12,4},{16,24},{20,28},{24,16},{28,20},{1,9},{5... | collective-permute-start | bytes 1572872 | tf_op jit(solution)/shard_map/ppermute | solution.py:327
  668.5 10.4 %copy-start.19 = (f32[2,1408,128]{2,1,0:T(8,128)S(1)}, f32[2,1408,128]{2,1,0:T(8,128)}, u32[]{:S(2)}) copy-start(f32[2,1408,128]{2,1,0:T(8,128)} %copy-done.18) | copy-start | bytes 4325380
  668.5 43.5 %all-to-all-start.2 = ((bf16[8,64,1024]{2,1,0:T(8,128)(2,1)}), bf16[8,64,1024]{2,1,0:T(8,128)(2,1)}, u32[]{:S(2)}, u32[]{:S(2)}) async-start(bf16[8,64,1024]{2,1,0:T(8,128)(2,1)} %bitcast.178), calls=%async_computation.2 | async-start | bytes 2097152 | tf_op jit(solution)/shard_map/all_to_all | solution.py:241
  676.9 18.2 %collective-permute-start.20 = (f32[2,1024]{1,0:T(2,128)S(1)}, f32[2,1024]{1,0:T(2,128)S(1)}, u32[]{:S(2)}, u32[]{:S(2)}) collective-permute-start(f32[2,1024]{1,0:T(2,128)S(1)} %add.283), channel_id=1, source_target_pairs={{0,8},{4,12},{8,0},{12,4},{16,24},{20,28},{24,16},{28,20},{1,9},{5... | collective-permute-start | bytes 24584 | tf_op jit(solution)/shard_map/ppermute | solution.py:375
  695.1 6.5 collective-permute-start.21
  697.3 21.9 %collective-permute-start.16 = (bf16[8,64,1024]{2,1,0:T(8,128)(2,1)}, bf16[8,64,1024]{2,1,0:T(8,128)(2,1)S(1)}, u32[]{:S(2)}, u32[]{:S(2)}) collective-permute-start(bf16[8,64,1024]{2,1,0:T(8,128)(2,1)} %all-to-all-done.3), channel_id=1, source_target_pairs={{0,2},{2,0},{1,3},{3,1},{4,6},{6,4},{5,7},{7,5},{8,10},{10,8},{9,1... | collective-permute-start | bytes 3145736 | tf_op jit(solution)/shard_map/ppermute | solution.py:238
  697.7 11.2 %collective-permute-start.25 = (bf16[1,1024,128]{2,1,0:T(8,128)(2,1)S(1)}, bf16[1,1024,128]{2,1,0:T(8,128)(2,1)S(1)}, u32[]{:S(2)}, u32[]{:S(2)}) collective-permute-start(bf16[1,1024,128]{2,1,0:T(8,128)(2,1)S(1)} %dynamic-slice_convert_fusion.7), channel_id=1, source_target_pairs={{0,16},{4,20},{8,24},{12,28},{16,0},{20,4},{24,8},{28,12},{1,17},{... | collective-permute-start | bytes 786440 | tf_op jit(solution)/shard_map/ppermute | solution.py:327
  (38 other events, 139.8 us)
